TPU v7x, 32 devices: a whole 2x2x4 slice. The times are simulated.
32 devices in a mesh: dp: 8 (over z, core), row: 2 (over x), col: 2 (over y).
Axes of the slice: x: 2, y: 2, z: 4, core: 2. Of those that a mesh axis runs over, the one named last changes fastest.
Arguments:
- tokens: bfloat16 [4096, 8192], P(('dp', 'row', 'col')), parts along dimension 0, may hold values from -6 to 6
- w_gate: bfloat16 [8192, 1024], P(('row', 'col')), may hold values from -0.0625 to 0.0625
- w_up: bfloat16 [8192, 1024], P(('row', 'col')), may hold values from -0.0625 to 0.0625
- w_down: bfloat16 [1024, 8192], P(None, ('row', 'col')), may hold values from -0.1875 to 0.1875
Outputs:
- mixed: bfloat16 [4096, 8192], P(('dp', 'row', 'col')), parts along dimension 0
There are 8 independent parts, one for each index of `dp`. A program takes and returns all parts, laid end to end along the dimension named above; an argument that names none is the same for every part. Nothing has to cross between parts.
All inputs are finite; a program needn't handle non-finite values.
Results may differ from a plain program's by a relative error of at most 0.029.
Values may be sent and summed in bfloat16 or wider, within the bound.
No kernel may reach another device: no remote copies, remote signals or barrier semaphores. Data moves between devices by JAX's collectives and lax.ppermute only.
A program may use at most 64 MiB of HBM per device.

v0:
```python
import jax
import jax.numpy as jnp
from jax import lax
from jax.sharding import PartitionSpec as P


def solution(mesh):
    rows, cols, dp = mesh.shape["row"], mesh.shape["col"], mesh.shape["dp"]
    cores = 2 if dp % 2 == 0 else 1
    chips = dp // cores
    shifts = [(dr, dc) for dr in range(rows) for dc in range(cols)]
    away = [s for s in shifts if s != (0, 0)]

    def send(x, shift):
        dr, dc = shift
        pairs = [
            (r * cols + c, (r + dr) % rows * cols + (c + dc) % cols) for r in range(rows) for c in range(cols)
        ]
        return lax.ppermute(x, ("row", "col"), pairs)

    def send_dp(x, chip_pairs, core_shift):
        pairs = [(z * cores + k, to * cores + (k + core_shift) % cores) for z, to in chip_pairs for k in range(cores)]
        return lax.ppermute(x, "dp", pairs)

    def swap(x, core_shift):
        return send_dp(x, [(z, z) for z in range(chips)], core_shift)

    def back(shift):
        return (-shift[0]) % rows, (-shift[1]) % cols

    def matmul(a, b):
        return jnp.dot(a, b, preferred_element_type=jnp.float32)

    def shards(tokens, w_gate, w_up, w_down):
        r, c, d = lax.axis_index("row"), lax.axis_index("col"), lax.axis_index("dp")
        chip, core = d // cores, d % cores
        slab = w_gate.shape[0]
        hidden_width, width = w_down.shape
        half = width // 2
        share = hidden_width // dp

        def place(shift):
            return (r + shift[0]) % rows * cols + (c + shift[1]) % cols

        piece = lax.dynamic_slice_in_dim(w_down, d * share, share, axis=0)
        sides = [(0, dc) for dc in range(1, cols)] + [(dr, 0) for dr in range(1, rows)]
        held = jnp.concatenate([send(piece[:, half:] if s[0] else piece[:, :half], back(s)) for s in sides], axis=0)

        feats = {s: lax.dynamic_slice_in_dim(tokens, place(s) * slab, slab, axis=1) for s in shifts}
        got = {s: send(feats[s], s) for s in away}
        got[0, 0] = feats[0, 0]

        early, late = [], []
        if chips == 4:
            two = send_dp(held, [(z, z ^ 2) for z in range(chips)], 0)
            one = send_dp(held, [(z, z ^ 1) for z in range(chips)], 0)
            middle = send_dp(held, [(1, 2), (2, 1)], 0)
            early += [(one, chip ^ 1), (two, chip ^ 2)]
        else:
            for z in range(1, chips):
                turn = send_dp(held, [(i, (i + z) % chips) for i in range(chips)], 0)
                late.append((turn, (chip - z) % chips))

        def crossed(weight, col_first):
            first, second = (cols, rows) if col_first else (rows, cols)

            def shift(a, b):
                return (b, a) if col_first else (a, b)

            parts = {s: matmul(got[s], weight) for s in away}
            parts[0, 0] = matmul(got[0, 0], weight)
            sums = {b: parts[shift(0, b)] for b in range(second)}
            for b in reversed(range(second)):
                for a in range(1, first):
                    part = send(parts[shift(a, b)].astype(jnp.bfloat16), back(shift(a, 0)))
                    sums[b] = sums[b] + part.astype(jnp.float32)
            total = sums[0]
            passed = [sums[b].astype(jnp.bfloat16) for b in range(1, second)]
            for b in range(1, second):
                total = total + send(passed[b - 1], back(shift(0, b))).astype(jnp.float32)
            return total, passed

        gate, gate_passed = crossed(w_gate, True)
        up, up_passed = crossed(w_up, False)
        hidden = (jax.nn.silu(gate) * up).astype(jnp.bfloat16)

        if chips == 4:
            relayed = send_dp(two, [(2, 3), (1, 0)], 0)
            late.append((jnp.where((chip == 0) | (chip == chips - 1), relayed, middle), chip ^ 3))

        far = {s: jnp.zeros((hidden_width, half), jnp.bfloat16) for s in sides}

        def fill(pieces):
            for k in range(cores):
                for block, from_chip in pieces:
                    moved = swap(block, k) if k else block
                    at = (from_chip * cores + (core - k) % cores) * share
                    for i, s in enumerate(sides):
                        far[s] = lax.dynamic_update_slice_in_dim(far[s], moved[i * share : (i + 1) * share], at, axis=0)

        fill([(held, chip)])
        tied, _ = lax.optimization_barrier(([p for p, _ in early], gate_passed + up_passed))
        fill([(p, at) for p, (_, at) in zip(tied, early)])

        near = {s: send(hidden, back(s)) for s in reversed(sides)}
        landed = [(matmul(hidden, w_down).astype(jnp.bfloat16), place((0, 0)) * width)]
        outs = []
        for s, other in near.items():
            weight, at = (w_down[:, :half], 0) if s[1] == 0 else (w_down[:, half:], half)
            own_out = matmul(other, weight).astype(jnp.bfloat16)
            outs.append((send(own_out, s), place(back(s)) * width + at))

        tied, _ = lax.optimization_barrier(([p for p, _ in late], hidden))
        fill([(p, at) for p, (_, at) in zip(tied, late)])
        for s in sides:
            at = half if s[0] else 0
            landed.append((matmul(hidden, far[s]).astype(jnp.bfloat16), place(s) * width + at))
        for s, other in near.items():
            at = 0 if s[1] == 0 else half
            for t in sides:
                if (t[0] == 0) == (s[1] == 0):
                    far_out = send(matmul(other, far[t]).astype(jnp.bfloat16), s)
                    outs.append((far_out, place((t[0] - s[0], t[1] - s[1])) * width + at))
        landed += outs

        mixed = jnp.zeros((tokens.shape[0], width * rows * cols), jnp.bfloat16)
        for block, at in landed:
            mixed = lax.dynamic_update_slice_in_dim(mixed, block, at, axis=1)
        return mixed

    in_specs = (
        P(("dp", "row", "col"), None),
        P(("row", "col"), None),
        P(("row", "col"), None),
        P(None, ("row", "col")),
    )
    out_specs = P(("dp", "row", "col"), None)
    return jax.shard_map(shards, mesh=mesh, in_specs=in_specs, out_specs=out_specs, check_vma=False)
```

profile of v0, /device:TPU:0, one launch (start us, length us, event | category | flops | bytes accessed | tf_op | source)
XLA Modules:
  0.0 97.1 jit_solution(7405160629160549438)
XLA Ops:
  0.0 1.9 %fusion.21 = (bf16[128,1024]{1,0:T(8,128)(2,1)S(1)}, bf16[128,1024]{1,0:T(8,128)(2,1)}) fusion(bf16[1024,2048]{1,0:T(8,128)(2,1)} %param.7, s32[]{:T(128)S(6)} %select_n.165, s32[]{:T(128)S(6)} %add.272), kind=kLoop, calls=%fused_computation.56 | loop fusion | bytes 1048584 | tf_op jit(solution)/shard_map/slice | solution.py:47
  1.9 3.0 %collective-permute-start.9 = (bf16[128,1024]{1,0:T(8,128)(2,1)}, bf16[128,1024]{1,0:T(8,128)(2,1)}, u32[]{:S(2)}, u32[]{:S(2)}) collective-permute-start(bf16[128,1024]{1,0:T(8,128)(2,1)} %get-tuple-element.12), channel_id=1, source_target_pairs={{0,1},{1,0},{2,3},{3,2},{4,5},{5,4},{6,7},{7,6},{8,9},{9,8},{10,11... | collective-permute-start | bytes 786440 | tf_op jit(solution)/shard_map/ppermute | solution.py:19
  4.9 1.5 %collective-permute-start.10 = (bf16[128,1024]{1,0:T(8,128)(2,1)S(1)}, bf16[128,1024]{1,0:T(8,128)(2,1)}, u32[]{:S(2)}, u32[]{:S(2)}) collective-permute-start(bf16[128,1024]{1,0:T(8,128)(2,1)S(1)} %get-tuple-element.11), channel_id=1, source_target_pairs={{0,2},{1,3},{2,0},{3,1},{4,6},{5,7},{6,4},{7,5},{8,10},{9,11},{10,... | collective-permute-start | bytes 786440 | tf_op jit(solution)/shard_map/ppermute | solution.py:19
  6.4 2.6 %constant_dynamic-slice_fusion.2 = (bf16[128,2048]{1,0:T(8,128)(2,1)}, bf16[128,2048]{1,0:T(8,128)(2,1)}, bf16[128,2048]{1,0:T(8,128)(2,1)}) fusion(bf16[128,8192]{1,0:T(8,128)(2,1)} %param.4, s32[]{:T(128)S(6)} %select_n.163, s32[]{:T(128)S(6)} %select_n.161, s32[]{:T(128)S(6)} %select_n.164), kind=kLoop, calls=%fused_computation.51 | loop fusion | bytes 3145740 | tf_op jit(solution)/shard_map/dynamic_slice | solution.py:49
  9.0 2.0 %collective-permute-start.2 = (bf16[128,2048]{1,0:T(8,128)(2,1)}, bf16[128,2048]{1,0:T(8,128)(2,1)S(1)}, u32[]{:S(2)}, u32[]{:S(2)}) collective-permute-start(bf16[128,2048]{1,0:T(8,128)(2,1)} %get-tuple-element.13), channel_id=1, source_target_pairs={{0,2},{1,3},{2,0},{3,1},{4,6},{5,7},{6,4},{7,5},{8,10},{9,11},{10,... | collective-permute-start | bytes 1572872 | tf_op jit(solution)/shard_map/ppermute | solution.py:19
  11.0 1.5 %collective-permute-start = (bf16[128,2048]{1,0:T(8,128)(2,1)}, bf16[128,2048]{1,0:T(8,128)(2,1)S(1)}, u32[]{:S(2)}, u32[]{:S(2)}) collective-permute-start(bf16[128,2048]{1,0:T(8,128)(2,1)} %get-tuple-element.14), channel_id=1, source_target_pairs={{0,1},{1,0},{2,3},{3,2},{4,5},{5,4},{6,7},{7,6},{8,9},{9,8},{10,11... | collective-permute-start | bytes 1572872 | tf_op jit(solution)/shard_map/ppermute | solution.py:19
  12.5 3.8 %fusion.15 = f32[128,1024]{1,0:T(8,128)} fusion(bf16[2048,1024]{1,0:T(8,128)(2,1)} %param.6, bf16[128,8192]{1,0:T(8,128)(2,1)S(1)} %copy-done.4, s32[]{:T(128)S(6)} %select_n.159), kind=kOutput, calls=%fused_computation.24 | convolution fusion | flops 536870912 | bytes 5242884 | tf_op jit(solution)/shard_map/dot_general | solution.py:32
  16.3 1.5 %fusion.17 = f32[128,1024]{1,0:T(8,128)} fusion(bf16[2048,1024]{1,0:T(8,128)(2,1)S(1)} %copy-done, bf16[128,8192]{1,0:T(8,128)(2,1)S(1)} %copy-done.4, s32[]{:T(128)S(6)} %select_n.159), kind=kOutput, calls=%fused_computation.26 | convolution fusion | flops 536870912 | bytes 5242884 | tf_op jit(solution)/shard_map/dot_general | solution.py:32
  18.1 1.2 %constant_dynamic-update-slice_fusion.7 = (bf16[256,1024]{1,0:T(8,128)(2,1)S(1)}, bf16[1024,1024]{1,0:T(8,128)(2,1)S(1)}) fusion(bf16[128,1024]{1,0:T(8,128)(2,1)} %collective-permute-done.9, bf16[1024,1024]{1,0:T(8,128)(2,1)S(1)} %broadcast.15.clone, s32[]{:T(128)S(6)} %select_n.169), kind=kLoop, calls=%fused_computation.55 | loop fusion | bytes 786436
  20.6 2.7 %collective-permute-start.13 = (bf16[256,1024]{1,0:T(8,128)(2,1)S(1)}, bf16[256,1024]{1,0:T(8,128)(2,1)S(1)}, u32[]{:S(2)}, u32[]{:S(2)}) collective-permute-start(bf16[256,1024]{1,0:T(8,128)(2,1)S(1)} %get-tuple-element.31), channel_id=1, source_target_pairs={{0,16},{4,20},{8,24},{12,28},{16,0},{20,4},{24,8},{28,12},{1,17},{... | collective-permute-start | bytes 1572872 | tf_op jit(solution)/shard_map/ppermute | solution.py:23
  25.0 1.8 %collective-permute-start.12 = (bf16[256,1024]{1,0:T(8,128)(2,1)S(1)}, bf16[256,1024]{1,0:T(8,128)(2,1)S(1)}, u32[]{:S(2)}, u32[]{:S(2)}) collective-permute-start(bf16[256,1024]{1,0:T(8,128)(2,1)S(1)} %get-tuple-element.31), channel_id=1, source_target_pairs={{0,8},{4,12},{8,0},{12,4},{16,24},{20,28},{24,16},{28,20},{1,9},{5... | collective-permute-start | bytes 1572872 | tf_op jit(solution)/shard_map/ppermute | solution.py:23
  26.8 1.8 %convolution_convert_fusion.7 = bf16[128,1024]{1,0:T(8,128)(2,1)S(1)} fusion(bf16[128,2048]{1,0:T(8,128)(2,1)} %collective-permute-done.3, bf16[2048,1024]{1,0:T(8,128)(2,1)S(1)} %copy-done.1), kind=kOutput, calls=%fused_computation.20 | convolution fusion | flops 537001984 | bytes 4980736 | tf_op jit(solution)/shard_map/dot_general | solution.py:32
  28.6 1.8 %convolution_convert_fusion.5 = bf16[128,1024]{1,0:T(8,128)(2,1)S(1)} fusion(bf16[128,2048]{1,0:T(8,128)(2,1)} %collective-permute-done.3, bf16[2048,1024]{1,0:T(8,128)(2,1)S(1)} %copy-done.2), kind=kOutput, calls=%fused_computation.18 | convolution fusion | flops 537001984 | bytes 4980736 | tf_op jit(solution)/shard_map/dot_general | solution.py:32
  30.4 4.3 %collective-permute-done = bf16[128,2048]{1,0:T(8,128)(2,1)S(1)} collective-permute-done((bf16[128,2048]{1,0:T(8,128)(2,1)}, bf16[128,2048]{1,0:T(8,128)(2,1)S(1)}, u32[]{:S(2)}, u32[]{:S(2)}) %collective-permute-start) | collective-permute-done | bytes 524320 | tf_op jit(solution)/shard_map/ppermute | solution.py:19
  35.5 1.2 %collective-permute-start.4 = (bf16[128,1024]{1,0:T(8,128)(2,1)S(1)}, bf16[128,1024]{1,0:T(8,128)(2,1)S(1)}, u32[]{:S(2)}, u32[]{:S(2)}) collective-permute-start(bf16[128,1024]{1,0:T(8,128)(2,1)S(1)} %convolution_convert_fusion.7), channel_id=1, source_target_pairs={{0,1},{1,0},{2,3},{3,2},{4,5},{5,4},{6,7},{7,6},{8,9},{9,8},{10,11... | collective-permute-start | bytes 786440 | tf_op jit(solution)/shard_map/ppermute | solution.py:19
  37.4 6.8 %collective-permute-done.4 = bf16[128,1024]{1,0:T(8,128)(2,1)S(1)} collective-permute-done((bf16[128,1024]{1,0:T(8,128)(2,1)S(1)}, bf16[128,1024]{1,0:T(8,128)(2,1)S(1)}, u32[]{:S(2)}, u32[]{:S(2)}) %collective-permute-start.4) | collective-permute-done | bytes 262176 | tf_op jit(solution)/shard_map/ppermute | solution.py:19
  45.9 6.2 %collective-permute-done.7 = bf16[128,1024]{1,0:T(8,128)(2,1)S(1)} collective-permute-done((bf16[128,1024]{1,0:T(8,128)(2,1)S(1)}, bf16[128,1024]{1,0:T(8,128)(2,1)S(1)}, u32[]{:S(2)}, u32[]{:S(2)}) %collective-permute-start.7) | collective-permute-done | bytes 262176 | tf_op jit(solution)/shard_map/ppermute | solution.py:19
  52.1 1.1 %collective-permute-start.1 = (bf16[128,1024]{1,0:T(8,128)(2,1)S(1)}, bf16[128,1024]{1,0:T(8,128)(2,1)S(1)}, u32[]{:S(2)}, u32[]{:S(2)}) collective-permute-start(bf16[128,1024]{1,0:T(8,128)(2,1)S(1)} %convolution_convert_fusion.8), channel_id=1, source_target_pairs={{0,1},{1,0},{2,3},{3,2},{4,5},{5,4},{6,7},{7,6},{8,9},{9,8},{10,11... | collective-permute-start | bytes 786440 | tf_op jit(solution)/shard_map/ppermute | solution.py:19
  54.0 1.4 %collective-permute-start.6 = (bf16[128,1024]{1,0:T(8,128)(2,1)S(1)}, bf16[128,1024]{1,0:T(8,128)(2,1)S(1)}, u32[]{:S(2)}, u32[]{:S(2)}) collective-permute-start(bf16[128,1024]{1,0:T(8,128)(2,1)S(1)} %convolution_convert_fusion.6), channel_id=1, source_target_pairs={{0,2},{1,3},{2,0},{3,1},{4,6},{5,7},{6,4},{7,5},{8,10},{9,11},{10,... | collective-permute-start | bytes 786440 | tf_op jit(solution)/shard_map/ppermute | solution.py:19
  57.2 4.1 %collective-permute-done.1 = bf16[128,1024]{1,0:T(8,128)(2,1)S(1)} collective-permute-done((bf16[128,1024]{1,0:T(8,128)(2,1)S(1)}, bf16[128,1024]{1,0:T(8,128)(2,1)S(1)}, u32[]{:S(2)}, u32[]{:S(2)}) %collective-permute-start.1) | collective-permute-done | bytes 262176 | tf_op jit(solution)/shard_map/ppermute | solution.py:19
  61.3 2.0 %collective-permute-done.6 = bf16[128,1024]{1,0:T(8,128)(2,1)S(1)} collective-permute-done((bf16[128,1024]{1,0:T(8,128)(2,1)S(1)}, bf16[128,1024]{1,0:T(8,128)(2,1)S(1)}, u32[]{:S(2)}, u32[]{:S(2)}) %collective-permute-start.6) | collective-permute-done | bytes 262176 | tf_op jit(solution)/shard_map/ppermute | solution.py:19
  63.3 3.2 %collective-permute-done.5 = bf16[128,1024]{1,0:T(8,128)(2,1)S(1)} collective-permute-done((bf16[128,1024]{1,0:T(8,128)(2,1)S(1)}, bf16[128,1024]{1,0:T(8,128)(2,1)S(1)}, u32[]{:S(2)}, u32[]{:S(2)}) %collective-permute-start.5) | collective-permute-done | bytes 262176 | tf_op jit(solution)/shard_map/ppermute | solution.py:19
  66.4 1.3 %collective-permute-start.16 = (bf16[256,1024]{1,0:T(8,128)(2,1)S(1)}, bf16[256,1024]{1,0:T(8,128)(2,1)S(1)}, u32[]{:S(2)}, u32[]{:S(2)}) collective-permute-start(bf16[256,1024]{1,0:T(8,128)(2,1)S(1)} %collective-permute-done.13), channel_id=1, source_target_pairs={{16,24},{20,28},{8,0},{12,4},{17,25},{21,29},{9,1},{13,5},{18,26},... | collective-permute-start | bytes 1572872 | tf_op jit(solution)/shard_map/ppermute | solution.py:23
  68.1 1.4 %collective-permute-start.19 = (bf16[128,1024]{1,0:T(8,128)(2,1)S(1)}, bf16[128,1024]{1,0:T(8,128)(2,1)S(1)}, u32[]{:S(2)}, u32[]{:S(2)}) collective-permute-start(bf16[128,1024]{1,0:T(8,128)(2,1)S(1)} %multiply_convert_fusion), channel_id=1, source_target_pairs={{0,2},{1,3},{2,0},{3,1},{4,6},{5,7},{6,4},{7,5},{8,10},{9,11},{10,... | collective-permute-start | bytes 786440 | tf_op jit(solution)/shard_map/ppermute | solution.py:19
  70.7 9.1 %collective-permute-done.16 = bf16[256,1024]{1,0:T(8,128)(2,1)S(1)} collective-permute-done((bf16[256,1024]{1,0:T(8,128)(2,1)S(1)}, bf16[256,1024]{1,0:T(8,128)(2,1)S(1)}, u32[]{:S(2)}, u32[]{:S(2)}) %collective-permute-start.16) | collective-permute-done | bytes 524320 | tf_op jit(solution)/shard_map/ppermute | solution.py:23
  80.4 1.4 %collective-permute-start.20 = (bf16[128,1024]{1,0:T(8,128)(2,1)S(1)}, bf16[128,1024]{1,0:T(8,128)(2,1)S(1)}, u32[]{:S(2)}, u32[]{:S(2)}) collective-permute-start(bf16[128,1024]{1,0:T(8,128)(2,1)S(1)} %fusion.5), channel_id=1, source_target_pairs={{0,2},{1,3},{2,0},{3,1},{4,6},{5,7},{6,4},{7,5},{8,10},{9,11},{10,... | collective-permute-start | bytes 786440 | tf_op jit(solution)/shard_map/ppermute | solution.py:19
  83.3 1.4 %collective-permute-start.23 = (bf16[128,1024]{1,0:T(8,128)(2,1)S(1)}, bf16[128,1024]{1,0:T(8,128)(2,1)S(1)}, u32[]{:S(2)}, u32[]{:S(2)}) collective-permute-start(bf16[128,1024]{1,0:T(8,128)(2,1)S(1)} %convolution_convert_fusion.2), channel_id=1, source_target_pairs={{0,2},{1,3},{2,0},{3,1},{4,6},{5,7},{6,4},{7,5},{8,10},{9,11},{10,... | collective-permute-start | bytes 786440 | tf_op jit(solution)/shard_map/ppermute | solution.py:19
  85.6 1.2 %collective-permute-start.24 = (bf16[128,1024]{1,0:T(8,128)(2,1)S(1)}, bf16[128,1024]{1,0:T(8,128)(2,1)S(1)}, u32[]{:S(2)}, u32[]{:S(2)}) collective-permute-start(bf16[128,1024]{1,0:T(8,128)(2,1)S(1)} %convolution_convert_fusion.1), channel_id=1, source_target_pairs={{0,1},{1,0},{2,3},{3,2},{4,5},{5,4},{6,7},{7,6},{8,9},{9,8},{10,11... | collective-permute-start | bytes 786440 | tf_op jit(solution)/shard_map/ppermute | solution.py:19
  87.2 2.4 %collective-permute-done.20 = bf16[128,1024]{1,0:T(8,128)(2,1)S(1)} collective-permute-done((bf16[128,1024]{1,0:T(8,128)(2,1)S(1)}, bf16[128,1024]{1,0:T(8,128)(2,1)S(1)}, u32[]{:S(2)}, u32[]{:S(2)}) %collective-permute-start.20) | collective-permute-done | bytes 262176 | tf_op jit(solution)/shard_map/ppermute | solution.py:19
  89.7 1.8 %collective-permute-done.22 = bf16[128,1024]{1,0:T(8,128)(2,1)S(1)} collective-permute-done((bf16[128,1024]{1,0:T(8,128)(2,1)S(1)}, bf16[128,1024]{1,0:T(8,128)(2,1)S(1)}, u32[]{:S(2)}, u32[]{:S(2)}) %collective-permute-start.22) | collective-permute-done | bytes 262176 | tf_op jit(solution)/shard_map/ppermute | solution.py:19
  91.5 3.3 %collective-permute-done.23 = bf16[128,1024]{1,0:T(8,128)(2,1)S(1)} collective-permute-done((bf16[128,1024]{1,0:T(8,128)(2,1)S(1)}, bf16[128,1024]{1,0:T(8,128)(2,1)S(1)}, u32[]{:S(2)}, u32[]{:S(2)}) %collective-permute-start.23) | collective-permute-done | bytes 262176 | tf_op jit(solution)/shard_map/ppermute | solution.py:19
  94.8 1.5 %collective-permute-done.24 = bf16[128,1024]{1,0:T(8,128)(2,1)S(1)} collective-permute-done((bf16[128,1024]{1,0:T(8,128)(2,1)S(1)}, bf16[128,1024]{1,0:T(8,128)(2,1)S(1)}, u32[]{:S(2)}, u32[]{:S(2)}) %collective-permute-start.24) | collective-permute-done | bytes 262176 | tf_op jit(solution)/shard_map/ppermute | solution.py:19
  (69 shorter events, 14.8 us)
Async XLA Ops:
  0.0 12.5 %copy-start.4 = (bf16[128,8192]{1,0:T(8,128)(2,1)S(1)}, bf16[128,8192]{1,0:T(8,128)(2,1)}, u32[]{:S(2)}) copy-start(bf16[128,8192]{1,0:T(8,128)(2,1)} %param.4) | copy-start | bytes 6291460
  1.9 15.9 %collective-permute-start.9 = (bf16[128,1024]{1,0:T(8,128)(2,1)}, bf16[128,1024]{1,0:T(8,128)(2,1)}, u32[]{:S(2)}, u32[]{:S(2)}) collective-permute-start(bf16[128,1024]{1,0:T(8,128)(2,1)} %get-tuple-element.12), channel_id=1, source_target_pairs={{0,1},{1,0},{2,3},{3,2},{4,5},{5,4},{6,7},{7,6},{8,9},{9,8},{10,11... | collective-permute-start | bytes 786440 | tf_op jit(solution)/shard_map/ppermute | solution.py:19
  4.9 14.4 %collective-permute-start.10 = (bf16[128,1024]{1,0:T(8,128)(2,1)S(1)}, bf16[128,1024]{1,0:T(8,128)(2,1)}, u32[]{:S(2)}, u32[]{:S(2)}) collective-permute-start(bf16[128,1024]{1,0:T(8,128)(2,1)S(1)} %get-tuple-element.11), channel_id=1, source_target_pairs={{0,2},{1,3},{2,0},{3,1},{4,6},{5,7},{6,4},{7,5},{8,10},{9,11},{10,... | collective-permute-start | bytes 786440 | tf_op jit(solution)/shard_map/ppermute | solution.py:19
  9.0 16.1 %collective-permute-start.3 = (bf16[128,2048]{1,0:T(8,128)(2,1)}, bf16[128,2048]{1,0:T(8,128)(2,1)}, u32[]{:S(2)}, u32[]{:S(2)}) collective-permute-start(bf16[128,2048]{1,0:T(8,128)(2,1)} %get-tuple-element.15), channel_id=1, source_target_pairs={{0,3},{1,2},{2,1},{3,0},{4,7},{5,6},{6,5},{7,4},{8,11},{9,10},{10,... | collective-permute-start | bytes 1572872 | tf_op jit(solution)/shard_map/ppermute | solution.py:19
  9.0 26.5 %collective-permute-start.2 = (bf16[128,2048]{1,0:T(8,128)(2,1)}, bf16[128,2048]{1,0:T(8,128)(2,1)S(1)}, u32[]{:S(2)}, u32[]{:S(2)}) collective-permute-start(bf16[128,2048]{1,0:T(8,128)(2,1)} %get-tuple-element.13), channel_id=1, source_target_pairs={{0,2},{1,3},{2,0},{3,1},{4,6},{5,7},{6,4},{7,5},{8,10},{9,11},{10,... | collective-permute-start | bytes 1572872 | tf_op jit(solution)/shard_map/ppermute | solution.py:19
  11.0 23.7 %collective-permute-start = (bf16[128,2048]{1,0:T(8,128)(2,1)}, bf16[128,2048]{1,0:T(8,128)(2,1)S(1)}, u32[]{:S(2)}, u32[]{:S(2)}) collective-permute-start(bf16[128,2048]{1,0:T(8,128)(2,1)} %get-tuple-element.14), channel_id=1, source_target_pairs={{0,1},{1,0},{2,3},{3,2},{4,5},{5,4},{6,7},{7,6},{8,9},{9,8},{10,11... | collective-permute-start | bytes 1572872 | tf_op jit(solution)/shard_map/ppermute | solution.py:19
  12.5 3.9 %copy-start = (bf16[2048,1024]{1,0:T(8,128)(2,1)S(1)}, bf16[2048,1024]{1,0:T(8,128)(2,1)}, u32[]{:S(2)}) copy-start(bf16[2048,1024]{1,0:T(8,128)(2,1)} %param.5) | copy-start | bytes 12582916
  17.9 8.9 %copy-start.1 = (bf16[2048,1024]{1,0:T(8,128)(2,1)S(1)}, bf16[2048,1024]{1,0:T(8,128)(2,1)}, u32[]{:S(2)}) copy-start(bf16[2048,1024]{1,0:T(8,128)(2,1)} %param.5) | copy-start | bytes 12582916
  20.6 8.0 %copy-start.2 = (bf16[2048,1024]{1,0:T(8,128)(2,1)S(1)}, bf16[2048,1024]{1,0:T(8,128)(2,1)}, u32[]{:S(2)}) copy-start(bf16[2048,1024]{1,0:T(8,128)(2,1)} %param.6) | copy-start | bytes 12582916
  20.6 33.4 %collective-permute-start.13 = (bf16[256,1024]{1,0:T(8,128)(2,1)S(1)}, bf16[256,1024]{1,0:T(8,128)(2,1)S(1)}, u32[]{:S(2)}, u32[]{:S(2)}) collective-permute-start(bf16[256,1024]{1,0:T(8,128)(2,1)S(1)} %get-tuple-element.31), channel_id=1, source_target_pairs={{0,16},{4,20},{8,24},{12,28},{16,0},{20,4},{24,8},{28,12},{1,17},{... | collective-permute-start | bytes 1572872 | tf_op jit(solution)/shard_map/ppermute | solution.py:23
  23.2 47.1 %collective-permute-start.17 = (bf16[256,1024]{1,0:T(8,128)(2,1)S(1)}, bf16[256,1024]{1,0:T(8,128)(2,1)S(1)}, u32[]{:S(2)}, u32[]{:S(2)}) collective-permute-start(bf16[256,1024]{1,0:T(8,128)(2,1)S(1)} %get-tuple-element.31), channel_id=1, source_target_pairs={{8,16},{12,20},{16,8},{20,12},{9,17},{13,21},{17,9},{21,13},{10,18... | collective-permute-start | bytes 1572872 | tf_op jit(solution)/shard_map/ppermute | solution.py:23
  25.0 30.4 %collective-permute-start.12 = (bf16[256,1024]{1,0:T(8,128)(2,1)S(1)}, bf16[256,1024]{1,0:T(8,128)(2,1)S(1)}, u32[]{:S(2)}, u32[]{:S(2)}) collective-permute-start(bf16[256,1024]{1,0:T(8,128)(2,1)S(1)} %get-tuple-element.31), channel_id=1, source_target_pairs={{0,8},{4,12},{8,0},{12,4},{16,24},{20,28},{24,16},{28,20},{1,9},{5... | collective-permute-start | bytes 1572872 | tf_op jit(solution)/shard_map/ppermute | solution.py:23
  34.7 21.4 %collective-permute-start.11 = (bf16[256,1024]{1,0:T(8,128)(2,1)S(1)}, bf16[256,1024]{1,0:T(8,128)(2,1)S(1)}, u32[]{:S(2)}, u32[]{:S(2)}) collective-permute-start(bf16[256,1024]{1,0:T(8,128)(2,1)S(1)} %get-tuple-element.31), channel_id=1, source_target_pairs={{0,4},{4,0},{8,12},{12,8},{16,20},{20,16},{24,28},{28,24},{1,5},{5... | collective-permute-start | bytes 1572872 | tf_op jit(solution)/shard_map/ppermute | solution.py:23
  35.5 8.8 %collective-permute-start.4 = (bf16[128,1024]{1,0:T(8,128)(2,1)S(1)}, bf16[128,1024]{1,0:T(8,128)(2,1)S(1)}, u32[]{:S(2)}, u32[]{:S(2)}) collective-permute-start(bf16[128,1024]{1,0:T(8,128)(2,1)S(1)} %convolution_convert_fusion.7), channel_id=1, source_target_pairs={{0,1},{1,0},{2,3},{3,2},{4,5},{5,4},{6,7},{7,6},{8,9},{9,8},{10,11... | collective-permute-start | bytes 786440 | tf_op jit(solution)/shard_map/ppermute | solution.py:19
  44.2 7.9 %collective-permute-start.7 = (bf16[128,1024]{1,0:T(8,128)(2,1)S(1)}, bf16[128,1024]{1,0:T(8,128)(2,1)S(1)}, u32[]{:S(2)}, u32[]{:S(2)}) collective-permute-start(bf16[128,1024]{1,0:T(8,128)(2,1)S(1)} %convolution_convert_fusion.5), channel_id=1, source_target_pairs={{0,2},{1,3},{2,0},{3,1},{4,6},{5,7},{6,4},{7,5},{8,10},{9,11},{10,... | collective-permute-start | bytes 786440 | tf_op jit(solution)/shard_map/ppermute | solution.py:19
  52.1 9.2 %collective-permute-start.1 = (bf16[128,1024]{1,0:T(8,128)(2,1)S(1)}, bf16[128,1024]{1,0:T(8,128)(2,1)S(1)}, u32[]{:S(2)}, u32[]{:S(2)}) collective-permute-start(bf16[128,1024]{1,0:T(8,128)(2,1)S(1)} %convolution_convert_fusion.8), channel_id=1, source_target_pairs={{0,1},{1,0},{2,3},{3,2},{4,5},{5,4},{6,7},{7,6},{8,9},{9,8},{10,11... | collective-permute-start | bytes 786440 | tf_op jit(solution)/shard_map/ppermute | solution.py:19
  54.0 13.7 %copy-start.6 = (f32[128,1024]{1,0:T(8,128)S(1)}, f32[128,1024]{1,0:T(8,128)}, u32[]{:S(2)}) copy-start(f32[128,1024]{1,0:T(8,128)} %fusion.15) | copy-start | bytes 1572868
  54.0 13.7 %copy-start.7 = (f32[128,1024]{1,0:T(8,128)S(1)}, f32[128,1024]{1,0:T(8,128)}, u32[]{:S(2)}) copy-start(f32[128,1024]{1,0:T(8,128)} %fusion.17) | copy-start | bytes 1572868
  54.0 9.2 %collective-permute-start.6 = (bf16[128,1024]{1,0:T(8,128)(2,1)S(1)}, bf16[128,1024]{1,0:T(8,128)(2,1)S(1)}, u32[]{:S(2)}, u32[]{:S(2)}) collective-permute-start(bf16[128,1024]{1,0:T(8,128)(2,1)S(1)} %convolution_convert_fusion.6), channel_id=1, source_target_pairs={{0,2},{1,3},{2,0},{3,1},{4,6},{5,7},{6,4},{7,5},{8,10},{9,11},{10,... | collective-permute-start | bytes 786440 | tf_op jit(solution)/shard_map/ppermute | solution.py:19
  55.4 11.0 %collective-permute-start.5 = (bf16[128,1024]{1,0:T(8,128)(2,1)S(1)}, bf16[128,1024]{1,0:T(8,128)(2,1)S(1)}, u32[]{:S(2)}, u32[]{:S(2)}) collective-permute-start(bf16[128,1024]{1,0:T(8,128)(2,1)S(1)} %fusion.13), channel_id=1, source_target_pairs={{0,2},{1,3},{2,0},{3,1},{4,6},{5,7},{6,4},{7,5},{8,10},{9,11},{10,... | collective-permute-start | bytes 786440 | tf_op jit(solution)/shard_map/ppermute | solution.py:19
  56.1 11.6 %collective-permute-start.8 = (bf16[128,1024]{1,0:T(8,128)(2,1)S(1)}, bf16[128,1024]{1,0:T(8,128)(2,1)S(1)}, u32[]{:S(2)}, u32[]{:S(2)}) collective-permute-start(bf16[128,1024]{1,0:T(8,128)(2,1)S(1)} %fusion.14), channel_id=1, source_target_pairs={{0,1},{1,0},{2,3},{3,2},{4,5},{5,4},{6,7},{7,6},{8,9},{9,8},{10,11... | collective-permute-start | bytes 786440 | tf_op jit(solution)/shard_map/ppermute | solution.py:19
  57.2 12.5 %copy-start.3 = (bf16[1024,2048]{1,0:T(8,128)(2,1)S(1)}, bf16[1024,2048]{1,0:T(8,128)(2,1)}, u32[]{:S(2)}) copy-start(bf16[1024,2048]{1,0:T(8,128)(2,1)} %param.7) | copy-start | bytes 12582916
  61.3 21.3 %collective-permute-start.14 = (bf16[256,1024]{1,0:T(8,128)(2,1)S(1)}, bf16[256,1024]{1,0:T(8,128)(2,1)S(1)}, u32[]{:S(2)}, u32[]{:S(2)}) collective-permute-start(bf16[256,1024]{1,0:T(8,128)(2,1)S(1)} %collective-permute-done.12), channel_id=1, source_target_pairs={{0,4},{4,0},{8,12},{12,8},{16,20},{20,16},{24,28},{28,24},{1,5},{5... | collective-permute-start | bytes 1572872 | tf_op jit(solution)/shard_map/ppermute | solution.py:23
  63.3 19.4 %collective-permute-start.15 = (bf16[256,1024]{1,0:T(8,128)(2,1)S(1)}, bf16[256,1024]{1,0:T(8,128)(2,1)S(1)}, u32[]{:S(2)}, u32[]{:S(2)}) collective-permute-start(bf16[256,1024]{1,0:T(8,128)(2,1)S(1)} %collective-permute-done.13), channel_id=1, source_target_pairs={{0,4},{4,0},{8,12},{12,8},{16,20},{20,16},{24,28},{28,24},{1,5},{5... | collective-permute-start | bytes 1572872 | tf_op jit(solution)/shard_map/ppermute | solution.py:23
  66.4 13.4 %collective-permute-start.16 = (bf16[256,1024]{1,0:T(8,128)(2,1)S(1)}, bf16[256,1024]{1,0:T(8,128)(2,1)S(1)}, u32[]{:S(2)}, u32[]{:S(2)}) collective-permute-start(bf16[256,1024]{1,0:T(8,128)(2,1)S(1)} %collective-permute-done.13), channel_id=1, source_target_pairs={{16,24},{20,28},{8,0},{12,4},{17,25},{21,29},{9,1},{13,5},{18,26},... | collective-permute-start | bytes 1572872 | tf_op jit(solution)/shard_map/ppermute | solution.py:23
  68.1 11.9 %collective-permute-start.19 = (bf16[128,1024]{1,0:T(8,128)(2,1)S(1)}, bf16[128,1024]{1,0:T(8,128)(2,1)S(1)}, u32[]{:S(2)}, u32[]{:S(2)}) collective-permute-start(bf16[128,1024]{1,0:T(8,128)(2,1)S(1)} %multiply_convert_fusion), channel_id=1, source_target_pairs={{0,2},{1,3},{2,0},{3,1},{4,6},{5,7},{6,4},{7,5},{8,10},{9,11},{10,... | collective-permute-start | bytes 786440 | tf_op jit(solution)/shard_map/ppermute | solution.py:19
  70.4 11.4 %collective-permute-start.21 = (bf16[128,1024]{1,0:T(8,128)(2,1)S(1)}, bf16[128,1024]{1,0:T(8,128)(2,1)S(1)}, u32[]{:S(2)}, u32[]{:S(2)}) collective-permute-start(bf16[128,1024]{1,0:T(8,128)(2,1)S(1)} %multiply_convert_fusion), channel_id=1, source_target_pairs={{0,1},{1,0},{2,3},{3,2},{4,5},{5,4},{6,7},{7,6},{8,9},{9,8},{10,11... | collective-permute-start | bytes 786440 | tf_op jit(solution)/shard_map/ppermute | solution.py:19
  79.9 2.9 %collective-permute-start.18 = (bf16[256,1024]{1,0:T(8,128)(2,1)S(1)}, bf16[256,1024]{1,0:T(8,128)(2,1)S(1)}, u32[]{:S(2)}, u32[]{:S(2)}) collective-permute-start(bf16[256,1024]{1,0:T(8,128)(2,1)S(1)} %broadcast_select_fusion), channel_id=1, source_target_pairs={{0,4},{4,0},{8,12},{12,8},{16,20},{20,16},{24,28},{28,24},{1,5},{5... | collective-permute-start | bytes 1572872 | tf_op jit(solution)/shard_map/ppermute | solution.py:23
  80.4 9.2 %collective-permute-start.20 = (bf16[128,1024]{1,0:T(8,128)(2,1)S(1)}, bf16[128,1024]{1,0:T(8,128)(2,1)S(1)}, u32[]{:S(2)}, u32[]{:S(2)}) collective-permute-start(bf16[128,1024]{1,0:T(8,128)(2,1)S(1)} %fusion.5), channel_id=1, source_target_pairs={{0,2},{1,3},{2,0},{3,1},{4,6},{5,7},{6,4},{7,5},{8,10},{9,11},{10,... | collective-permute-start | bytes 786440 | tf_op jit(solution)/shard_map/ppermute | solution.py:19
  82.2 9.2 %collective-permute-start.22 = (bf16[128,1024]{1,0:T(8,128)(2,1)S(1)}, bf16[128,1024]{1,0:T(8,128)(2,1)S(1)}, u32[]{:S(2)}, u32[]{:S(2)}) collective-permute-start(bf16[128,1024]{1,0:T(8,128)(2,1)S(1)} %fusion.8), channel_id=1, source_target_pairs={{0,1},{1,0},{2,3},{3,2},{4,5},{5,4},{6,7},{7,6},{8,9},{9,8},{10,11... | collective-permute-start | bytes 786440 | tf_op jit(solution)/shard_map/ppermute | solution.py:19
  83.3 11.5 %collective-permute-start.23 = (bf16[128,1024]{1,0:T(8,128)(2,1)S(1)}, bf16[128,1024]{1,0:T(8,128)(2,1)S(1)}, u32[]{:S(2)}, u32[]{:S(2)}) collective-permute-start(bf16[128,1024]{1,0:T(8,128)(2,1)S(1)} %convolution_convert_fusion.2), channel_id=1, source_target_pairs={{0,2},{1,3},{2,0},{3,1},{4,6},{5,7},{6,4},{7,5},{8,10},{9,11},{10,... | collective-permute-start | bytes 786440 | tf_op jit(solution)/shard_map/ppermute | solution.py:19
  85.6 10.8 %collective-permute-start.24 = (bf16[128,1024]{1,0:T(8,128)(2,1)S(1)}, bf16[128,1024]{1,0:T(8,128)(2,1)S(1)}, u32[]{:S(2)}, u32[]{:S(2)}) collective-permute-start(bf16[128,1024]{1,0:T(8,128)(2,1)S(1)} %convolution_convert_fusion.1), channel_id=1, source_target_pairs={{0,1},{1,0},{2,3},{3,2},{4,5},{5,4},{6,7},{7,6},{8,9},{9,8},{10,11... | collective-permute-start | bytes 786440 | tf_op jit(solution)/shard_map/ppermute | solution.py:19
  (1 other events, 1.5 us)
where the time goes:
time: 97.4 us; the launch traced here: 97.1 us
  waiting for transfers between devices  45.7 us (47%)
  starting transfers between devices  26.8 us (28%)
  matrix products  15.4 us (16%)
  local copies, waits for them, and re-layouts  8.5 us (9%)
    ppermute x17, waiting for transfers between devices, send(): return lax.ppermute(x, ('row', 'col'), pairs)  36.6 us
    ppermute x17, starting transfers between devices, send(): return lax.ppermute(x, ('row', 'col'), pairs)  20.3 us
    dot_general x15, matrix products, matmul(): return jnp.dot(a, b, preferred_element_type=jnp.float32)  15.4 us
    ppermute x8, waiting for transfers between devices, send_dp(): return lax.ppermute(x, 'dp', pairs)  9.08 us
    ppermute x8, starting transfers between devices, send_dp(): return lax.ppermute(x, 'dp', pairs)  6.48 us
    dynamic_slice x1, local copies, waits for them, and re-layouts, shards(): lax.dynamic_slice_in_dim(tokens, place(s) * slab, slab, axis=1)  2.57 us
  transfers between devices with their start and end apart: 25, of which 12 were waited for; matrix products, arithmetic and copies ran while one was open for 22% of the time, Pallas kernels for 0%

commit v1 on v0

--- a/solution.py
+++ b/solution.py
@@ -44,11 +44,15 @@
 
         piece = lax.dynamic_slice_in_dim(w_down, d * share, share, axis=0)
         sides = [(0, dc) for dc in range(1, cols)] + [(dr, 0) for dr in range(1, rows)]
-        held = jnp.concatenate([send(piece[:, half:] if s[0] else piece[:, :half], back(s)) for s in sides], axis=0)
+        hopped = [send(piece[:, half:] if s[0] else piece[:, :half], back(s)) for s in sides]
 
         feats = {s: lax.dynamic_slice_in_dim(tokens, place(s) * slab, slab, axis=1) for s in shifts}
         got = {s: send(feats[s], s) for s in away}
         got[0, 0] = feats[0, 0]
+
+        first_parts = [matmul(got[s], w).astype(jnp.bfloat16) for s in away if s[0] and s[1] for w in (w_gate, w_up)]
+        hopped, _ = lax.optimization_barrier((hopped, first_parts))
+        held = jnp.concatenate(hopped, axis=0)
 
         early, late = [], []
         if chips == 4:

time: 97.4 us -> 93.9 us (0.964)
  waiting for transfers between devices: 45.7 us -> 36.7 us
  starting transfers between devices: 26.8 us -> 34 us
  matrix products: 15.4 us -> 13.8 us
    ppermute x17, waiting for transfers between devices: 36.6 us -> 24.2 us  [send(): return lax.ppermute(x, ('row', 'col'), pairs)]
    ppermute x17, starting transfers between devices: 20.3 us -> 26.9 us  [send(): return lax.ppermute(x, ('row', 'col'), pairs)]
    ppermute x8, waiting for transfers between devices: 9.08 us -> 12.5 us  [send_dp(): return lax.ppermute(x, 'dp', pairs)]
    dot_general x15, matrix products: 15.4 us -> 13.8 us  [matmul(): return jnp.dot(a, b, preferred_element_type=jnp.float32)]
  transfers between devices with their start and end apart: 25 -> 25, of which waited for: 12 -> 13; matrix products, arithmetic and copies ran while one was open for 22% -> 20% of each run, Pallas kernels for 0% -> 0%
where the time goes in v1:
time: 93.9 us; the launch traced here: 93.6 us
  waiting for transfers between devices  36.7 us (39%)
  starting transfers between devices  34 us (36%)
  matrix products  13.8 us (15%)
  local copies, waits for them, and re-layouts  8.33 us (9%)
    ppermute x17, starting transfers between devices, send(): return lax.ppermute(x, ('row', 'col'), pairs)  26.9 us
    ppermute x17, waiting for transfers between devices, send(): return lax.ppermute(x, ('row', 'col'), pairs)  24.2 us
    dot_general x15, matrix products, matmul(): return jnp.dot(a, b, preferred_element_type=jnp.float32)  13.8 us
    ppermute x8, waiting for transfers between devices, send_dp(): return lax.ppermute(x, 'dp', pairs)  12.5 us
    ppermute x8, starting transfers between devices, send_dp(): return lax.ppermute(x, 'dp', pairs)  7.17 us
    dynamic_slice x1, local copies, waits for them, and re-layouts, shards(): lax.dynamic_slice_in_dim(tokens, place(s) * slab, slab, axis=1)  2.71 us
  transfers between devices with their start and end apart: 25, of which 13 were waited for; matrix products, arithmetic and copies ran while one was open for 20% of the time, Pallas kernels for 0%

profile of v1, /device:TPU:0, one launch (start us, length us, event | category | flops | bytes accessed | tf_op | source)
XLA Modules:
  0.0 93.6 jit_solution(10458681366382758596)
XLA Ops:
  0.0 2.7 %constant_dynamic-slice_fusion.2 = (bf16[128,2048]{1,0:T(8,128)(2,1)}, bf16[128,2048]{1,0:T(8,128)(2,1)}, bf16[128,2048]{1,0:T(8,128)(2,1)}) fusion(bf16[128,8192]{1,0:T(8,128)(2,1)} %param.4, s32[]{:T(128)S(6)} %select_n.163, s32[]{:T(128)S(6)} %select_n.161, s32[]{:T(128)S(6)} %select_n.164), kind=kLoop, calls=%fused_computation.51 | loop fusion | bytes 3145740 | tf_op jit(solution)/shard_map/dynamic_slice | solution.py:49
  2.7 3.9 %collective-permute-start.3 = (bf16[128,2048]{1,0:T(8,128)(2,1)}, bf16[128,2048]{1,0:T(8,128)(2,1)}, u32[]{:S(2)}, u32[]{:S(2)}) collective-permute-start(bf16[128,2048]{1,0:T(8,128)(2,1)} %get-tuple-element.19), channel_id=1, source_target_pairs={{0,3},{1,2},{2,1},{3,0},{4,7},{5,6},{6,5},{7,4},{8,11},{9,10},{10,... | collective-permute-start | bytes 1572872 | tf_op jit(solution)/shard_map/ppermute | solution.py:19
  6.6 1.8 %fusion.21 = (bf16[128,1024]{1,0:T(8,128)(2,1)}, bf16[128,1024]{1,0:T(8,128)(2,1)S(1)}) fusion(bf16[1024,2048]{1,0:T(8,128)(2,1)} %param.7, s32[]{:T(128)S(6)} %select_n.165, s32[]{:T(128)S(6)} %add.272), kind=kLoop, calls=%fused_computation.56 | loop fusion | bytes 1048584 | tf_op jit(solution)/shard_map/slice | solution.py:47
  9.0 2.0 %collective-permute-start.2 = (bf16[128,2048]{1,0:T(8,128)(2,1)}, bf16[128,2048]{1,0:T(8,128)(2,1)S(1)}, u32[]{:S(2)}, u32[]{:S(2)}) collective-permute-start(bf16[128,2048]{1,0:T(8,128)(2,1)} %get-tuple-element.17), channel_id=1, source_target_pairs={{0,2},{1,3},{2,0},{3,1},{4,6},{5,7},{6,4},{7,5},{8,10},{9,11},{10,... | collective-permute-start | bytes 1572872 | tf_op jit(solution)/shard_map/ppermute | solution.py:19
  10.9 1.5 %collective-permute-start = (bf16[128,2048]{1,0:T(8,128)(2,1)}, bf16[128,2048]{1,0:T(8,128)(2,1)S(1)}, u32[]{:S(2)}, u32[]{:S(2)}) collective-permute-start(bf16[128,2048]{1,0:T(8,128)(2,1)} %get-tuple-element.18), channel_id=1, source_target_pairs={{0,1},{1,0},{2,3},{3,2},{4,5},{5,4},{6,7},{7,6},{8,9},{9,8},{10,11... | collective-permute-start | bytes 1572872 | tf_op jit(solution)/shard_map/ppermute | solution.py:19
  12.5 3.0 %fusion.15 = f32[128,1024]{1,0:T(8,128)S(1)} fusion(bf16[2048,1024]{1,0:T(8,128)(2,1)} %param.6, bf16[128,8192]{1,0:T(8,128)(2,1)S(1)} %copy-done.3, s32[]{:T(128)S(6)} %select_n.159), kind=kOutput, calls=%fused_computation.24 | convolution fusion | flops 536870912 | bytes 5242884 | tf_op jit(solution)/shard_map/dot_general | solution.py:32
  15.5 4.2 %collective-permute-done.3 = bf16[128,2048]{1,0:T(8,128)(2,1)} collective-permute-done((bf16[128,2048]{1,0:T(8,128)(2,1)}, bf16[128,2048]{1,0:T(8,128)(2,1)}, u32[]{:S(2)}, u32[]{:S(2)}) %collective-permute-start.3) | collective-permute-done | bytes 524320 | tf_op jit(solution)/shard_map/ppermute | solution.py:19
  19.8 1.8 %convolution_convert_fusion.7 = bf16[128,1024]{1,0:T(8,128)(2,1)S(1)} fusion(bf16[128,2048]{1,0:T(8,128)(2,1)} %collective-permute-done.3, bf16[2048,1024]{1,0:T(8,128)(2,1)S(1)} %copy-done.1), kind=kOutput, calls=%fused_computation.20 | convolution fusion | flops 537001984 | bytes 4980736 | tf_op jit(solution)/shard_map/dot_general | solution.py:32
  21.6 2.1 %collective-permute-start.4 = (bf16[128,1024]{1,0:T(8,128)(2,1)S(1)}, bf16[128,1024]{1,0:T(8,128)(2,1)S(1)}, u32[]{:S(2)}, u32[]{:S(2)}) collective-permute-start(bf16[128,1024]{1,0:T(8,128)(2,1)S(1)} %convolution_convert_fusion.7), channel_id=1, source_target_pairs={{0,1},{1,0},{2,3},{3,2},{4,5},{5,4},{6,7},{7,6},{8,9},{9,8},{10,11... | collective-permute-start | bytes 786440 | tf_op jit(solution)/shard_map/ppermute | solution.py:19
  23.6 1.8 %convolution_convert_fusion.5 = bf16[128,1024]{1,0:T(8,128)(2,1)S(1)} fusion(bf16[128,2048]{1,0:T(8,128)(2,1)} %collective-permute-done.3, bf16[2048,1024]{1,0:T(8,128)(2,1)S(1)} %copy-done), kind=kOutput, calls=%fused_computation.18 | convolution fusion | flops 537001984 | bytes 4980736 | tf_op jit(solution)/shard_map/dot_general | solution.py:32
  25.9 1.5 %collective-permute-start.7 = (bf16[128,1024]{1,0:T(8,128)(2,1)S(1)}, bf16[128,1024]{1,0:T(8,128)(2,1)S(1)}, u32[]{:S(2)}, u32[]{:S(2)}) collective-permute-start(bf16[128,1024]{1,0:T(8,128)(2,1)S(1)} %convolution_convert_fusion.5), channel_id=1, source_target_pairs={{0,2},{1,3},{2,0},{3,1},{4,6},{5,7},{6,4},{7,5},{8,10},{9,11},{10,... | collective-permute-start | bytes 786440 | tf_op jit(solution)/shard_map/ppermute | solution.py:19
  30.0 2.7 %collective-permute-start.13 = (bf16[256,1024]{1,0:T(8,128)(2,1)S(1)}, bf16[256,1024]{1,0:T(8,128)(2,1)S(1)}, u32[]{:S(2)}, u32[]{:S(2)}) collective-permute-start(bf16[256,1024]{1,0:T(8,128)(2,1)S(1)} %get-tuple-element.35), channel_id=1, source_target_pairs={{0,16},{4,20},{8,24},{12,28},{16,0},{20,4},{24,8},{28,12},{1,17},{... | collective-permute-start | bytes 1572872 | tf_op jit(solution)/shard_map/ppermute | solution.py:23
  32.6 3.1 %collective-permute-done = bf16[128,2048]{1,0:T(8,128)(2,1)S(1)} collective-permute-done((bf16[128,2048]{1,0:T(8,128)(2,1)}, bf16[128,2048]{1,0:T(8,128)(2,1)S(1)}, u32[]{:S(2)}, u32[]{:S(2)}) %collective-permute-start) | collective-permute-done | bytes 524320 | tf_op jit(solution)/shard_map/ppermute | solution.py:19
  35.7 1.8 %collective-permute-start.12 = (bf16[256,1024]{1,0:T(8,128)(2,1)S(1)}, bf16[256,1024]{1,0:T(8,128)(2,1)S(1)}, u32[]{:S(2)}, u32[]{:S(2)}) collective-permute-start(bf16[256,1024]{1,0:T(8,128)(2,1)S(1)} %get-tuple-element.35), channel_id=1, source_target_pairs={{0,8},{4,12},{8,0},{12,4},{16,24},{20,28},{24,16},{28,20},{1,9},{5... | collective-permute-start | bytes 1572872 | tf_op jit(solution)/shard_map/ppermute | solution.py:23
  38.2 1.6 %collective-permute-start.1 = (bf16[128,1024]{1,0:T(8,128)(2,1)S(1)}, bf16[128,1024]{1,0:T(8,128)(2,1)S(1)}, u32[]{:S(2)}, u32[]{:S(2)}) collective-permute-start(bf16[128,1024]{1,0:T(8,128)(2,1)S(1)} %convolution_convert_fusion.8), channel_id=1, source_target_pairs={{0,1},{1,0},{2,3},{3,2},{4,5},{5,4},{6,7},{7,6},{8,9},{9,8},{10,11... | collective-permute-start | bytes 786440 | tf_op jit(solution)/shard_map/ppermute | solution.py:19
  41.3 1.7 %collective-permute-start.6 = (bf16[128,1024]{1,0:T(8,128)(2,1)S(1)}, bf16[128,1024]{1,0:T(8,128)(2,1)S(1)}, u32[]{:S(2)}, u32[]{:S(2)}) collective-permute-start(bf16[128,1024]{1,0:T(8,128)(2,1)S(1)} %convolution_convert_fusion.6), channel_id=1, source_target_pairs={{0,2},{1,3},{2,0},{3,1},{4,6},{5,7},{6,4},{7,5},{8,10},{9,11},{10,... | collective-permute-start | bytes 786440 | tf_op jit(solution)/shard_map/ppermute | solution.py:19
  44.9 1.9 %collective-permute-done.1 = bf16[128,1024]{1,0:T(8,128)(2,1)S(1)} collective-permute-done((bf16[128,1024]{1,0:T(8,128)(2,1)S(1)}, bf16[128,1024]{1,0:T(8,128)(2,1)S(1)}, u32[]{:S(2)}, u32[]{:S(2)}) %collective-permute-start.1) | collective-permute-done | bytes 262176 | tf_op jit(solution)/shard_map/ppermute | solution.py:19
  46.9 1.7 %collective-permute-start.8 = (bf16[128,1024]{1,0:T(8,128)(2,1)S(1)}, bf16[128,1024]{1,0:T(8,128)(2,1)S(1)}, u32[]{:S(2)}, u32[]{:S(2)}) collective-permute-start(bf16[128,1024]{1,0:T(8,128)(2,1)S(1)} %fusion.14), channel_id=1, source_target_pairs={{0,1},{1,0},{2,3},{3,2},{4,5},{5,4},{6,7},{7,6},{8,9},{9,8},{10,11... | collective-permute-start | bytes 786440 | tf_op jit(solution)/shard_map/ppermute | solution.py:19
  49.3 1.2 %collective-permute-done.6 = bf16[128,1024]{1,0:T(8,128)(2,1)S(1)} collective-permute-done((bf16[128,1024]{1,0:T(8,128)(2,1)S(1)}, bf16[128,1024]{1,0:T(8,128)(2,1)S(1)}, u32[]{:S(2)}, u32[]{:S(2)}) %collective-permute-start.6) | collective-permute-done | bytes 262176 | tf_op jit(solution)/shard_map/ppermute | solution.py:19
  51.3 3.8 %collective-permute-done.5 = bf16[128,1024]{1,0:T(8,128)(2,1)S(1)} collective-permute-done((bf16[128,1024]{1,0:T(8,128)(2,1)S(1)}, bf16[128,1024]{1,0:T(8,128)(2,1)S(1)}, u32[]{:S(2)}, u32[]{:S(2)}) %collective-permute-start.5) | collective-permute-done | bytes 262176 | tf_op jit(solution)/shard_map/ppermute | solution.py:19
  55.4 1.8 %collective-permute-start.19 = (bf16[128,1024]{1,0:T(8,128)(2,1)S(1)}, bf16[128,1024]{1,0:T(8,128)(2,1)S(1)}, u32[]{:S(2)}, u32[]{:S(2)}) collective-permute-start(bf16[128,1024]{1,0:T(8,128)(2,1)S(1)} %multiply_convert_fusion), channel_id=1, source_target_pairs={{0,2},{1,3},{2,0},{3,1},{4,6},{5,7},{6,4},{7,5},{8,10},{9,11},{10,... | collective-permute-start | bytes 786440 | tf_op jit(solution)/shard_map/ppermute | solution.py:19
  57.1 1.5 %collective-permute-start.21 = (bf16[128,1024]{1,0:T(8,128)(2,1)S(1)}, bf16[128,1024]{1,0:T(8,128)(2,1)S(1)}, u32[]{:S(2)}, u32[]{:S(2)}) collective-permute-start(bf16[128,1024]{1,0:T(8,128)(2,1)S(1)} %multiply_convert_fusion), channel_id=1, source_target_pairs={{0,1},{1,0},{2,3},{3,2},{4,5},{5,4},{6,7},{7,6},{8,9},{9,8},{10,11... | collective-permute-start | bytes 786440 | tf_op jit(solution)/shard_map/ppermute | solution.py:19
  61.3 2.8 %collective-permute-done.19 = bf16[128,1024]{1,0:T(8,128)(2,1)S(1)} collective-permute-done((bf16[128,1024]{1,0:T(8,128)(2,1)S(1)}, bf16[128,1024]{1,0:T(8,128)(2,1)S(1)}, u32[]{:S(2)}, u32[]{:S(2)}) %collective-permute-start.19) | collective-permute-done | bytes 262176 | tf_op jit(solution)/shard_map/ppermute | solution.py:19
  64.2 1.3 %collective-permute-start.16 = (bf16[256,1024]{1,0:T(8,128)(2,1)S(1)}, bf16[256,1024]{1,0:T(8,128)(2,1)S(1)}, u32[]{:S(2)}, u32[]{:S(2)}) collective-permute-start(bf16[256,1024]{1,0:T(8,128)(2,1)S(1)} %collective-permute-done.13), channel_id=1, source_target_pairs={{16,24},{20,28},{8,0},{12,4},{17,25},{21,29},{9,1},{13,5},{18,26},... | collective-permute-start | bytes 1572872 | tf_op jit(solution)/shard_map/ppermute | solution.py:23
  65.9 1.7 %collective-permute-start.20 = (bf16[128,1024]{1,0:T(8,128)(2,1)S(1)}, bf16[128,1024]{1,0:T(8,128)(2,1)S(1)}, u32[]{:S(2)}, u32[]{:S(2)}) collective-permute-start(bf16[128,1024]{1,0:T(8,128)(2,1)S(1)} %fusion.5), channel_id=1, source_target_pairs={{0,2},{1,3},{2,0},{3,1},{4,6},{5,7},{6,4},{7,5},{8,10},{9,11},{10,... | collective-permute-start | bytes 786440 | tf_op jit(solution)/shard_map/ppermute | solution.py:19
  68.1 1.6 %collective-permute-start.22 = (bf16[128,1024]{1,0:T(8,128)(2,1)S(1)}, bf16[128,1024]{1,0:T(8,128)(2,1)S(1)}, u32[]{:S(2)}, u32[]{:S(2)}) collective-permute-start(bf16[128,1024]{1,0:T(8,128)(2,1)S(1)} %fusion.8), channel_id=1, source_target_pairs={{0,1},{1,0},{2,3},{3,2},{4,5},{5,4},{6,7},{7,6},{8,9},{9,8},{10,11... | collective-permute-start | bytes 786440 | tf_op jit(solution)/shard_map/ppermute | solution.py:19
  69.7 9.8 %collective-permute-done.16 = bf16[256,1024]{1,0:T(8,128)(2,1)S(1)} collective-permute-done((bf16[256,1024]{1,0:T(8,128)(2,1)S(1)}, bf16[256,1024]{1,0:T(8,128)(2,1)S(1)}, u32[]{:S(2)}, u32[]{:S(2)}) %collective-permute-start.16) | collective-permute-done | bytes 524320 | tf_op jit(solution)/shard_map/ppermute | solution.py:23
  79.8 1.7 %collective-permute-done.18 = bf16[256,1024]{1,0:T(8,128)(2,1)S(1)} collective-permute-done((bf16[256,1024]{1,0:T(8,128)(2,1)S(1)}, bf16[256,1024]{1,0:T(8,128)(2,1)S(1)}, u32[]{:S(2)}, u32[]{:S(2)}) %collective-permute-start.18) | collective-permute-done | bytes 524320 | tf_op jit(solution)/shard_map/ppermute | solution.py:23
  82.1 1.8 %collective-permute-start.23 = (bf16[128,1024]{1,0:T(8,128)(2,1)S(1)}, bf16[128,1024]{1,0:T(8,128)(2,1)S(1)}, u32[]{:S(2)}, u32[]{:S(2)}) collective-permute-start(bf16[128,1024]{1,0:T(8,128)(2,1)S(1)} %convolution_convert_fusion.2), channel_id=1, source_target_pairs={{0,2},{1,3},{2,0},{3,1},{4,6},{5,7},{6,4},{7,5},{8,10},{9,11},{10,... | collective-permute-start | bytes 786440 | tf_op jit(solution)/shard_map/ppermute | solution.py:19
  84.7 1.6 %collective-permute-start.24 = (bf16[128,1024]{1,0:T(8,128)(2,1)S(1)}, bf16[128,1024]{1,0:T(8,128)(2,1)S(1)}, u32[]{:S(2)}, u32[]{:S(2)}) collective-permute-start(bf16[128,1024]{1,0:T(8,128)(2,1)S(1)} %convolution_convert_fusion.1), channel_id=1, source_target_pairs={{0,1},{1,0},{2,3},{3,2},{4,5},{5,4},{6,7},{7,6},{8,9},{9,8},{10,11... | collective-permute-start | bytes 786440 | tf_op jit(solution)/shard_map/ppermute | solution.py:19
  86.9 3.6 %collective-permute-done.23 = bf16[128,1024]{1,0:T(8,128)(2,1)S(1)} collective-permute-done((bf16[128,1024]{1,0:T(8,128)(2,1)S(1)}, bf16[128,1024]{1,0:T(8,128)(2,1)S(1)}, u32[]{:S(2)}, u32[]{:S(2)}) %collective-permute-start.23) | collective-permute-done | bytes 262176 | tf_op jit(solution)/shard_map/ppermute | solution.py:19
  90.5 2.3 %collective-permute-done.24 = bf16[128,1024]{1,0:T(8,128)(2,1)S(1)} collective-permute-done((bf16[128,1024]{1,0:T(8,128)(2,1)S(1)}, bf16[128,1024]{1,0:T(8,128)(2,1)S(1)}, u32[]{:S(2)}, u32[]{:S(2)}) %collective-permute-start.24) | collective-permute-done | bytes 262176 | tf_op jit(solution)/shard_map/ppermute | solution.py:19
  (63 shorter events, 16.0 us)
Async XLA Ops:
  0.0 12.5 %copy-start.3 = (bf16[128,8192]{1,0:T(8,128)(2,1)S(1)}, bf16[128,8192]{1,0:T(8,128)(2,1)}, u32[]{:S(2)}) copy-start(bf16[128,8192]{1,0:T(8,128)(2,1)} %param.4) | copy-start | bytes 6291460
  2.7 17.1 %collective-permute-start.3 = (bf16[128,2048]{1,0:T(8,128)(2,1)}, bf16[128,2048]{1,0:T(8,128)(2,1)}, u32[]{:S(2)}, u32[]{:S(2)}) collective-permute-start(bf16[128,2048]{1,0:T(8,128)(2,1)} %get-tuple-element.19), channel_id=1, source_target_pairs={{0,3},{1,2},{2,1},{3,0},{4,7},{5,6},{6,5},{7,4},{8,11},{9,10},{10,... | collective-permute-start | bytes 1572872 | tf_op jit(solution)/shard_map/ppermute | solution.py:19
  8.4 17.5 %collective-permute-start.10 = (bf16[128,1024]{1,0:T(8,128)(2,1)}, bf16[128,1024]{1,0:T(8,128)(2,1)}, u32[]{:S(2)}, u32[]{:S(2)}) collective-permute-start(bf16[128,1024]{1,0:T(8,128)(2,1)} %get-tuple-element.15), channel_id=1, source_target_pairs={{0,2},{1,3},{2,0},{3,1},{4,6},{5,7},{6,4},{7,5},{8,10},{9,11},{10,... | collective-permute-start | bytes 786440 | tf_op jit(solution)/shard_map/ppermute | solution.py:19
  8.9 18.5 %collective-permute-start.9 = (bf16[128,1024]{1,0:T(8,128)(2,1)S(1)}, bf16[128,1024]{1,0:T(8,128)(2,1)}, u32[]{:S(2)}, u32[]{:S(2)}) collective-permute-start(bf16[128,1024]{1,0:T(8,128)(2,1)S(1)} %get-tuple-element.16), channel_id=1, source_target_pairs={{0,1},{1,0},{2,3},{3,2},{4,5},{5,4},{6,7},{7,6},{8,9},{9,8},{10,11... | collective-permute-start | bytes 786440 | tf_op jit(solution)/shard_map/ppermute | solution.py:19
  9.0 29.3 %collective-permute-start.2 = (bf16[128,2048]{1,0:T(8,128)(2,1)}, bf16[128,2048]{1,0:T(8,128)(2,1)S(1)}, u32[]{:S(2)}, u32[]{:S(2)}) collective-permute-start(bf16[128,2048]{1,0:T(8,128)(2,1)} %get-tuple-element.17), channel_id=1, source_target_pairs={{0,2},{1,3},{2,0},{3,1},{4,6},{5,7},{6,4},{7,5},{8,10},{9,11},{10,... | collective-permute-start | bytes 1572872 | tf_op jit(solution)/shard_map/ppermute | solution.py:19
  10.9 24.8 %collective-permute-start = (bf16[128,2048]{1,0:T(8,128)(2,1)}, bf16[128,2048]{1,0:T(8,128)(2,1)S(1)}, u32[]{:S(2)}, u32[]{:S(2)}) collective-permute-start(bf16[128,2048]{1,0:T(8,128)(2,1)} %get-tuple-element.18), channel_id=1, source_target_pairs={{0,1},{1,0},{2,3},{3,2},{4,5},{5,4},{6,7},{7,6},{8,9},{9,8},{10,11... | collective-permute-start | bytes 1572872 | tf_op jit(solution)/shard_map/ppermute | solution.py:19
  12.5 7.3 %copy-start.1 = (bf16[2048,1024]{1,0:T(8,128)(2,1)S(1)}, bf16[2048,1024]{1,0:T(8,128)(2,1)}, u32[]{:S(2)}) copy-start(bf16[2048,1024]{1,0:T(8,128)(2,1)} %param.5) | copy-start | bytes 12582916
  15.5 8.1 %copy-start = (bf16[2048,1024]{1,0:T(8,128)(2,1)S(1)}, bf16[2048,1024]{1,0:T(8,128)(2,1)}, u32[]{:S(2)}) copy-start(bf16[2048,1024]{1,0:T(8,128)(2,1)} %param.6) | copy-start | bytes 12582916
  21.6 19.8 %collective-permute-start.4 = (bf16[128,1024]{1,0:T(8,128)(2,1)S(1)}, bf16[128,1024]{1,0:T(8,128)(2,1)S(1)}, u32[]{:S(2)}, u32[]{:S(2)}) collective-permute-start(bf16[128,1024]{1,0:T(8,128)(2,1)S(1)} %convolution_convert_fusion.7), channel_id=1, source_target_pairs={{0,1},{1,0},{2,3},{3,2},{4,5},{5,4},{6,7},{7,6},{8,9},{9,8},{10,11... | collective-permute-start | bytes 786440 | tf_op jit(solution)/shard_map/ppermute | solution.py:19
  25.9 17.9 %collective-permute-start.7 = (bf16[128,1024]{1,0:T(8,128)(2,1)S(1)}, bf16[128,1024]{1,0:T(8,128)(2,1)S(1)}, u32[]{:S(2)}, u32[]{:S(2)}) collective-permute-start(bf16[128,1024]{1,0:T(8,128)(2,1)S(1)} %convolution_convert_fusion.5), channel_id=1, source_target_pairs={{0,2},{1,3},{2,0},{3,1},{4,6},{5,7},{6,4},{7,5},{8,10},{9,11},{10,... | collective-permute-start | bytes 786440 | tf_op jit(solution)/shard_map/ppermute | solution.py:19
  30.0 27.2 %collective-permute-start.13 = (bf16[256,1024]{1,0:T(8,128)(2,1)S(1)}, bf16[256,1024]{1,0:T(8,128)(2,1)S(1)}, u32[]{:S(2)}, u32[]{:S(2)}) collective-permute-start(bf16[256,1024]{1,0:T(8,128)(2,1)S(1)} %get-tuple-element.35), channel_id=1, source_target_pairs={{0,16},{4,20},{8,24},{12,28},{16,0},{20,4},{24,8},{28,12},{1,17},{... | collective-permute-start | bytes 1572872 | tf_op jit(solution)/shard_map/ppermute | solution.py:23
  35.7 23.9 %collective-permute-start.12 = (bf16[256,1024]{1,0:T(8,128)(2,1)S(1)}, bf16[256,1024]{1,0:T(8,128)(2,1)S(1)}, u32[]{:S(2)}, u32[]{:S(2)}) collective-permute-start(bf16[256,1024]{1,0:T(8,128)(2,1)S(1)} %get-tuple-element.35), channel_id=1, source_target_pairs={{0,8},{4,12},{8,0},{12,4},{16,24},{20,28},{24,16},{28,20},{1,9},{5... | collective-permute-start | bytes 1572872 | tf_op jit(solution)/shard_map/ppermute | solution.py:23
  38.2 8.6 %collective-permute-start.1 = (bf16[128,1024]{1,0:T(8,128)(2,1)S(1)}, bf16[128,1024]{1,0:T(8,128)(2,1)S(1)}, u32[]{:S(2)}, u32[]{:S(2)}) collective-permute-start(bf16[128,1024]{1,0:T(8,128)(2,1)S(1)} %convolution_convert_fusion.8), channel_id=1, source_target_pairs={{0,1},{1,0},{2,3},{3,2},{4,5},{5,4},{6,7},{7,6},{8,9},{9,8},{10,11... | collective-permute-start | bytes 786440 | tf_op jit(solution)/shard_map/ppermute | solution.py:19
  41.3 9.2 %collective-permute-start.6 = (bf16[128,1024]{1,0:T(8,128)(2,1)S(1)}, bf16[128,1024]{1,0:T(8,128)(2,1)S(1)}, u32[]{:S(2)}, u32[]{:S(2)}) collective-permute-start(bf16[128,1024]{1,0:T(8,128)(2,1)S(1)} %convolution_convert_fusion.6), channel_id=1, source_target_pairs={{0,2},{1,3},{2,0},{3,1},{4,6},{5,7},{6,4},{7,5},{8,10},{9,11},{10,... | collective-permute-start | bytes 786440 | tf_op jit(solution)/shard_map/ppermute | solution.py:19
  43.8 11.3 %collective-permute-start.5 = (bf16[128,1024]{1,0:T(8,128)(2,1)S(1)}, bf16[128,1024]{1,0:T(8,128)(2,1)S(1)}, u32[]{:S(2)}, u32[]{:S(2)}) collective-permute-start(bf16[128,1024]{1,0:T(8,128)(2,1)S(1)} %fusion.13), channel_id=1, source_target_pairs={{0,2},{1,3},{2,0},{3,1},{4,6},{5,7},{6,4},{7,5},{8,10},{9,11},{10,... | collective-permute-start | bytes 786440 | tf_op jit(solution)/shard_map/ppermute | solution.py:19
  46.9 8.2 %collective-permute-start.8 = (bf16[128,1024]{1,0:T(8,128)(2,1)S(1)}, bf16[128,1024]{1,0:T(8,128)(2,1)S(1)}, u32[]{:S(2)}, u32[]{:S(2)}) collective-permute-start(bf16[128,1024]{1,0:T(8,128)(2,1)S(1)} %fusion.14), channel_id=1, source_target_pairs={{0,1},{1,0},{2,3},{3,2},{4,5},{5,4},{6,7},{7,6},{8,9},{9,8},{10,11... | collective-permute-start | bytes 786440 | tf_op jit(solution)/shard_map/ppermute | solution.py:19
  49.3 10.5 %copy-start.2 = (bf16[1024,2048]{1,0:T(8,128)(2,1)S(1)}, bf16[1024,2048]{1,0:T(8,128)(2,1)}, u32[]{:S(2)}) copy-start(bf16[1024,2048]{1,0:T(8,128)(2,1)} %param.7) | copy-start | bytes 12582916
  50.5 17.6 %collective-permute-start.17 = (bf16[256,1024]{1,0:T(8,128)(2,1)S(1)}, bf16[256,1024]{1,0:T(8,128)(2,1)S(1)}, u32[]{:S(2)}, u32[]{:S(2)}) collective-permute-start(bf16[256,1024]{1,0:T(8,128)(2,1)S(1)} %get-tuple-element.35), channel_id=1, source_target_pairs={{8,16},{12,20},{16,8},{20,12},{9,17},{13,21},{17,9},{21,13},{10,18... | collective-permute-start | bytes 1572872 | tf_op jit(solution)/shard_map/ppermute | solution.py:23
  55.1 5.5 %collective-permute-start.11 = (bf16[256,1024]{1,0:T(8,128)(2,1)S(1)}, bf16[256,1024]{1,0:T(8,128)(2,1)S(1)}, u32[]{:S(2)}, u32[]{:S(2)}) collective-permute-start(bf16[256,1024]{1,0:T(8,128)(2,1)S(1)} %get-tuple-element.35), channel_id=1, source_target_pairs={{0,4},{4,0},{8,12},{12,8},{16,20},{20,16},{24,28},{28,24},{1,5},{5... | collective-permute-start | bytes 1572872 | tf_op jit(solution)/shard_map/ppermute | solution.py:23
  55.4 8.8 %collective-permute-start.19 = (bf16[128,1024]{1,0:T(8,128)(2,1)S(1)}, bf16[128,1024]{1,0:T(8,128)(2,1)S(1)}, u32[]{:S(2)}, u32[]{:S(2)}) collective-permute-start(bf16[128,1024]{1,0:T(8,128)(2,1)S(1)} %multiply_convert_fusion), channel_id=1, source_target_pairs={{0,2},{1,3},{2,0},{3,1},{4,6},{5,7},{6,4},{7,5},{8,10},{9,11},{10,... | collective-permute-start | bytes 786440 | tf_op jit(solution)/shard_map/ppermute | solution.py:19
  57.1 8.8 %collective-permute-start.21 = (bf16[128,1024]{1,0:T(8,128)(2,1)S(1)}, bf16[128,1024]{1,0:T(8,128)(2,1)S(1)}, u32[]{:S(2)}, u32[]{:S(2)}) collective-permute-start(bf16[128,1024]{1,0:T(8,128)(2,1)S(1)} %multiply_convert_fusion), channel_id=1, source_target_pairs={{0,1},{1,0},{2,3},{3,2},{4,5},{5,4},{6,7},{7,6},{8,9},{9,8},{10,11... | collective-permute-start | bytes 786440 | tf_op jit(solution)/shard_map/ppermute | solution.py:19
  59.6 20.1 %collective-permute-start.14 = (bf16[256,1024]{1,0:T(8,128)(2,1)S(1)}, bf16[256,1024]{1,0:T(8,128)(2,1)S(1)}, u32[]{:S(2)}, u32[]{:S(2)}) collective-permute-start(bf16[256,1024]{1,0:T(8,128)(2,1)S(1)} %collective-permute-done.12), channel_id=1, source_target_pairs={{0,4},{4,0},{8,12},{12,8},{16,20},{20,16},{24,28},{28,24},{1,5},{5... | collective-permute-start | bytes 1572872 | tf_op jit(solution)/shard_map/ppermute | solution.py:23
  60.6 19.2 %collective-permute-start.15 = (bf16[256,1024]{1,0:T(8,128)(2,1)S(1)}, bf16[256,1024]{1,0:T(8,128)(2,1)S(1)}, u32[]{:S(2)}, u32[]{:S(2)}) collective-permute-start(bf16[256,1024]{1,0:T(8,128)(2,1)S(1)} %collective-permute-done.13), channel_id=1, source_target_pairs={{0,4},{4,0},{8,12},{12,8},{16,20},{20,16},{24,28},{28,24},{1,5},{5... | collective-permute-start | bytes 1572872 | tf_op jit(solution)/shard_map/ppermute | solution.py:23
  64.2 15.4 %collective-permute-start.16 = (bf16[256,1024]{1,0:T(8,128)(2,1)S(1)}, bf16[256,1024]{1,0:T(8,128)(2,1)S(1)}, u32[]{:S(2)}, u32[]{:S(2)}) collective-permute-start(bf16[256,1024]{1,0:T(8,128)(2,1)S(1)} %collective-permute-done.13), channel_id=1, source_target_pairs={{16,24},{20,28},{8,0},{12,4},{17,25},{21,29},{9,1},{13,5},{18,26},... | collective-permute-start | bytes 1572872 | tf_op jit(solution)/shard_map/ppermute | solution.py:23
  65.9 20.8 %collective-permute-start.20 = (bf16[128,1024]{1,0:T(8,128)(2,1)S(1)}, bf16[128,1024]{1,0:T(8,128)(2,1)S(1)}, u32[]{:S(2)}, u32[]{:S(2)}) collective-permute-start(bf16[128,1024]{1,0:T(8,128)(2,1)S(1)} %fusion.5), channel_id=1, source_target_pairs={{0,2},{1,3},{2,0},{3,1},{4,6},{5,7},{6,4},{7,5},{8,10},{9,11},{10,... | collective-permute-start | bytes 786440 | tf_op jit(solution)/shard_map/ppermute | solution.py:19
  68.1 18.7 %collective-permute-start.22 = (bf16[128,1024]{1,0:T(8,128)(2,1)S(1)}, bf16[128,1024]{1,0:T(8,128)(2,1)S(1)}, u32[]{:S(2)}, u32[]{:S(2)}) collective-permute-start(bf16[128,1024]{1,0:T(8,128)(2,1)S(1)} %fusion.8), channel_id=1, source_target_pairs={{0,1},{1,0},{2,3},{3,2},{4,5},{5,4},{6,7},{7,6},{8,9},{9,8},{10,11... | collective-permute-start | bytes 786440 | tf_op jit(solution)/shard_map/ppermute | solution.py:19
  79.6 2.0 %collective-permute-start.18 = (bf16[256,1024]{1,0:T(8,128)(2,1)S(1)}, bf16[256,1024]{1,0:T(8,128)(2,1)S(1)}, u32[]{:S(2)}, u32[]{:S(2)}) collective-permute-start(bf16[256,1024]{1,0:T(8,128)(2,1)S(1)} %broadcast_select_fusion), channel_id=1, source_target_pairs={{0,4},{4,0},{8,12},{12,8},{16,20},{20,16},{24,28},{28,24},{1,5},{5... | collective-permute-start | bytes 1572872 | tf_op jit(solution)/shard_map/ppermute | solution.py:23
  82.1 8.4 %collective-permute-start.23 = (bf16[128,1024]{1,0:T(8,128)(2,1)S(1)}, bf16[128,1024]{1,0:T(8,128)(2,1)S(1)}, u32[]{:S(2)}, u32[]{:S(2)}) collective-permute-start(bf16[128,1024]{1,0:T(8,128)(2,1)S(1)} %convolution_convert_fusion.2), channel_id=1, source_target_pairs={{0,2},{1,3},{2,0},{3,1},{4,6},{5,7},{6,4},{7,5},{8,10},{9,11},{10,... | collective-permute-start | bytes 786440 | tf_op jit(solution)/shard_map/ppermute | solution.py:19
  84.7 8.1 %collective-permute-start.24 = (bf16[128,1024]{1,0:T(8,128)(2,1)S(1)}, bf16[128,1024]{1,0:T(8,128)(2,1)S(1)}, u32[]{:S(2)}, u32[]{:S(2)}) collective-permute-start(bf16[128,1024]{1,0:T(8,128)(2,1)S(1)} %convolution_convert_fusion.1), channel_id=1, source_target_pairs={{0,1},{1,0},{2,3},{3,2},{4,5},{5,4},{6,7},{7,6},{8,9},{9,8},{10,11... | collective-permute-start | bytes 786440 | tf_op jit(solution)/shard_map/ppermute | solution.py:19
  90.5 2.4 %copy-start.4 = (bf16[128,8192]{1,0:T(8,128)(2,1)}, bf16[128,8192]{1,0:T(8,128)(2,1)S(1)}, u32[]{:S(2)}) copy-start(bf16[128,8192]{1,0:T(8,128)(2,1)S(1)} %constant_dynamic-update-slice_fusion.1) | copy-start | bytes 6291460

commit v2 on v0

--- a/solution.py
+++ b/solution.py
@@ -52,9 +52,13 @@
 
         early, late = [], []
         if chips == 4:
-            two = send_dp(held, [(z, z ^ 2) for z in range(chips)], 0)
+            two_a = send_dp(held, [(0, 2), (3, 1)], 0)
+            two_b = send_dp(held, [(1, 3), (2, 0)], 0)
             one = send_dp(held, [(z, z ^ 1) for z in range(chips)], 0)
             middle = send_dp(held, [(1, 2), (2, 1)], 0)
+            relayed = send_dp(two_a, [(2, 3), (1, 0)], 0)
+            outer = (chip == 0) | (chip == chips - 1)
+            two = jnp.where(outer, two_b, two_a)
             early += [(one, chip ^ 1), (two, chip ^ 2)]
         else:
             for z in range(1, chips):
@@ -85,8 +89,7 @@
         hidden = (jax.nn.silu(gate) * up).astype(jnp.bfloat16)
 
         if chips == 4:
-            relayed = send_dp(two, [(2, 3), (1, 0)], 0)
-            late.append((jnp.where((chip == 0) | (chip == chips - 1), relayed, middle), chip ^ 3))
+            late.append((jnp.where(outer, relayed, middle), chip ^ 3))
 
         far = {s: jnp.zeros((hidden_width, half), jnp.bfloat16) for s in sides}
 
@@ -102,6 +105,8 @@
         tied, _ = lax.optimization_barrier(([p for p, _ in early], gate_passed + up_passed))
         fill([(p, at) for p, (_, at) in zip(tied, early)])
 
+        tied, _ = lax.optimization_barrier(([p for p, _ in late], hidden))
+        fill([(p, at) for p, (_, at) in zip(tied, late)])
         near = {s: send(hidden, back(s)) for s in reversed(sides)}
         landed = [(matmul(hidden, w_down).astype(jnp.bfloat16), place((0, 0)) * width)]
         outs = []
@@ -110,8 +115,6 @@
             own_out = matmul(other, weight).astype(jnp.bfloat16)
             outs.append((send(own_out, s), place(back(s)) * width + at))
 
-        tied, _ = lax.optimization_barrier(([p for p, _ in late], hidden))
-        fill([(p, at) for p, (_, at) in zip(tied, late)])
         for s in sides:
             at = half if s[0] else 0
             landed.append((matmul(hidden, far[s]).astype(jnp.bfloat16), place(s) * width + at))

time: 97.4 us -> 106 us (1.088)
  waiting for transfers between devices: 45.7 us -> 49.7 us
  starting transfers between devices: 26.8 us -> 30.3 us
    ppermute x8 -> x9, waiting for transfers between devices: 9.08 us -> 23.2 us  [send_dp(): return lax.ppermute(x, 'dp', pairs)]
    ppermute x17, waiting for transfers between devices: 36.6 us -> 26.4 us  [send(): return lax.ppermute(x, ('row', 'col'), pairs)]
    ppermute x8 -> x9, starting transfers between devices: 6.48 us -> 9.7 us  [send_dp(): return lax.ppermute(x, 'dp', pairs)]
  transfers between devices with their start and end apart: 25 -> 26, of which waited for: 12 -> 11; matrix products, arithmetic and copies ran while one was open for 22% -> 21% of each run, Pallas kernels for 0% -> 0%
where the time goes in v2:
time: 106 us; the launch traced here: 105 us
  waiting for transfers between devices  49.7 us (47%)
  starting transfers between devices  30.3 us (29%)
  matrix products  15.4 us (15%)
  local copies, waits for them, and re-layouts  9.06 us (9%)
    ppermute x17, waiting for transfers between devices, send(): return lax.ppermute(x, ('row', 'col'), pairs)  26.4 us
    ppermute x9, waiting for transfers between devices, send_dp(): return lax.ppermute(x, 'dp', pairs)  23.2 us
    ppermute x17, starting transfers between devices, send(): return lax.ppermute(x, ('row', 'col'), pairs)  20.6 us
    dot_general x15, matrix products, matmul(): return jnp.dot(a, b, preferred_element_type=jnp.float32)  15.4 us
    ppermute x9, starting transfers between devices, send_dp(): return lax.ppermute(x, 'dp', pairs)  9.7 us
    dynamic_slice x1, local copies, waits for them, and re-layouts, shards(): lax.dynamic_slice_in_dim(tokens, place(s) * slab, slab, axis=1)  2.56 us
  transfers between devices with their start and end apart: 26, of which 11 were waited for; matrix products, arithmetic and copies ran while one was open for 21% of the time, Pallas kernels for 0%

profile of v2, /device:TPU:0, one launch (start us, length us, event | category | flops | bytes accessed | tf_op | source)
XLA Modules:
  0.0 105.3 jit_solution(4005894023501308673)
XLA Ops:
  0.0 1.9 %fusion.21 = (bf16[128,1024]{1,0:T(8,128)(2,1)S(1)}, bf16[128,1024]{1,0:T(8,128)(2,1)}) fusion(bf16[1024,2048]{1,0:T(8,128)(2,1)} %param.7, s32[]{:T(128)S(6)} %select_n.169, s32[]{:T(128)S(6)} %add.272), kind=kLoop, calls=%fused_computation.57 | loop fusion | bytes 1048584 | tf_op jit(solution)/shard_map/slice | solution.py:47
  1.9 3.0 %collective-permute-start.9 = (bf16[128,1024]{1,0:T(8,128)(2,1)}, bf16[128,1024]{1,0:T(8,128)(2,1)}, u32[]{:S(2)}, u32[]{:S(2)}) collective-permute-start(bf16[128,1024]{1,0:T(8,128)(2,1)} %get-tuple-element.12), channel_id=1, source_target_pairs={{0,1},{1,0},{2,3},{3,2},{4,5},{5,4},{6,7},{7,6},{8,9},{9,8},{10,11... | collective-permute-start | bytes 786440 | tf_op jit(solution)/shard_map/ppermute | solution.py:19
  4.9 1.5 %collective-permute-start.10 = (bf16[128,1024]{1,0:T(8,128)(2,1)S(1)}, bf16[128,1024]{1,0:T(8,128)(2,1)}, u32[]{:S(2)}, u32[]{:S(2)}) collective-permute-start(bf16[128,1024]{1,0:T(8,128)(2,1)S(1)} %get-tuple-element.11), channel_id=1, source_target_pairs={{0,2},{1,3},{2,0},{3,1},{4,6},{5,7},{6,4},{7,5},{8,10},{9,11},{10,... | collective-permute-start | bytes 786440 | tf_op jit(solution)/shard_map/ppermute | solution.py:19
  6.4 2.6 %constant_dynamic-slice_fusion.2 = (bf16[128,2048]{1,0:T(8,128)(2,1)}, bf16[128,2048]{1,0:T(8,128)(2,1)}, bf16[128,2048]{1,0:T(8,128)(2,1)}) fusion(bf16[128,8192]{1,0:T(8,128)(2,1)} %param.4, s32[]{:T(128)S(6)} %select_n.167, s32[]{:T(128)S(6)} %select_n.165, s32[]{:T(128)S(6)} %select_n.168), kind=kLoop, calls=%fused_computation.52 | loop fusion | bytes 3145740 | tf_op jit(solution)/shard_map/dynamic_slice | solution.py:49
  9.0 2.0 %collective-permute-start.2 = (bf16[128,2048]{1,0:T(8,128)(2,1)}, bf16[128,2048]{1,0:T(8,128)(2,1)S(1)}, u32[]{:S(2)}, u32[]{:S(2)}) collective-permute-start(bf16[128,2048]{1,0:T(8,128)(2,1)} %get-tuple-element.13), channel_id=1, source_target_pairs={{0,2},{1,3},{2,0},{3,1},{4,6},{5,7},{6,4},{7,5},{8,10},{9,11},{10,... | collective-permute-start | bytes 1572872 | tf_op jit(solution)/shard_map/ppermute | solution.py:19
  10.9 1.5 %collective-permute-start = (bf16[128,2048]{1,0:T(8,128)(2,1)}, bf16[128,2048]{1,0:T(8,128)(2,1)S(1)}, u32[]{:S(2)}, u32[]{:S(2)}) collective-permute-start(bf16[128,2048]{1,0:T(8,128)(2,1)} %get-tuple-element.14), channel_id=1, source_target_pairs={{0,1},{1,0},{2,3},{3,2},{4,5},{5,4},{6,7},{7,6},{8,9},{9,8},{10,11... | collective-permute-start | bytes 1572872 | tf_op jit(solution)/shard_map/ppermute | solution.py:19
  12.5 3.9 %fusion.15 = f32[128,1024]{1,0:T(8,128)} fusion(bf16[2048,1024]{1,0:T(8,128)(2,1)} %param.6, bf16[128,8192]{1,0:T(8,128)(2,1)S(1)} %copy-done.4, s32[]{:T(128)S(6)} %select_n.163), kind=kOutput, calls=%fused_computation.25 | convolution fusion | flops 536870912 | bytes 5242884 | tf_op jit(solution)/shard_map/dot_general | solution.py:32
  16.3 1.6 %fusion.17 = f32[128,1024]{1,0:T(8,128)} fusion(bf16[2048,1024]{1,0:T(8,128)(2,1)S(1)} %copy-done, bf16[128,8192]{1,0:T(8,128)(2,1)S(1)} %copy-done.4, s32[]{:T(128)S(6)} %select_n.163), kind=kOutput, calls=%fused_computation.27 | convolution fusion | flops 536870912 | bytes 5242884 | tf_op jit(solution)/shard_map/dot_general | solution.py:32
  18.2 1.2 %constant_dynamic-update-slice_fusion.7 = (bf16[256,1024]{1,0:T(8,128)(2,1)S(1)}, bf16[1024,1024]{1,0:T(8,128)(2,1)S(1)}) fusion(bf16[128,1024]{1,0:T(8,128)(2,1)} %collective-permute-done.9, bf16[1024,1024]{1,0:T(8,128)(2,1)S(1)} %broadcast.15.clone, s32[]{:T(128)S(6)} %select_n.173), kind=kLoop, calls=%fused_computation.56 | loop fusion | bytes 786436
  19.6 1.0 constant_dynamic-update-slice_fusion.4
  20.6 4.8 %collective-permute-start.14 = (bf16[256,1024]{1,0:T(8,128)(2,1)S(1)}, bf16[256,1024]{1,0:T(8,128)(2,1)S(1)}, u32[]{:S(2)}, u32[]{:S(2)}) collective-permute-start(bf16[256,1024]{1,0:T(8,128)(2,1)S(1)} %get-tuple-element.31), channel_id=1, source_target_pairs={{0,16},{4,20},{24,8},{28,12},{1,17},{5,21},{25,9},{29,13},{2,18},{... | collective-permute-start | bytes 1572872 | tf_op jit(solution)/shard_map/ppermute | solution.py:23
  26.1 1.3 %collective-permute-start.13 = (bf16[256,1024]{1,0:T(8,128)(2,1)S(1)}, bf16[256,1024]{1,0:T(8,128)(2,1)S(1)}, u32[]{:S(2)}, u32[]{:S(2)}) collective-permute-start(bf16[256,1024]{1,0:T(8,128)(2,1)S(1)} %get-tuple-element.31), channel_id=1, source_target_pairs={{8,24},{12,28},{16,0},{20,4},{9,25},{13,29},{17,1},{21,5},{10,26},... | collective-permute-start | bytes 1572872 | tf_op jit(solution)/shard_map/ppermute | solution.py:23
  27.4 1.8 %convolution_convert_fusion.7 = bf16[128,1024]{1,0:T(8,128)(2,1)S(1)} fusion(bf16[128,2048]{1,0:T(8,128)(2,1)} %collective-permute-done.3, bf16[2048,1024]{1,0:T(8,128)(2,1)S(1)} %copy-done.1), kind=kOutput, calls=%fused_computation.20 | convolution fusion | flops 537001984 | bytes 4980736 | tf_op jit(solution)/shard_map/dot_general | solution.py:32
  29.2 1.8 %convolution_convert_fusion.5 = bf16[128,1024]{1,0:T(8,128)(2,1)S(1)} fusion(bf16[128,2048]{1,0:T(8,128)(2,1)} %collective-permute-done.3, bf16[2048,1024]{1,0:T(8,128)(2,1)S(1)} %copy-done.2), kind=kOutput, calls=%fused_computation.18 | convolution fusion | flops 537001984 | bytes 4980736 | tf_op jit(solution)/shard_map/dot_general | solution.py:32
  31.0 3.6 %collective-permute-done = bf16[128,2048]{1,0:T(8,128)(2,1)S(1)} collective-permute-done((bf16[128,2048]{1,0:T(8,128)(2,1)}, bf16[128,2048]{1,0:T(8,128)(2,1)S(1)}, u32[]{:S(2)}, u32[]{:S(2)}) %collective-permute-start) | collective-permute-done | bytes 524320 | tf_op jit(solution)/shard_map/ppermute | solution.py:19
  34.7 1.6 %collective-permute-start.12 = (bf16[256,1024]{1,0:T(8,128)(2,1)S(1)}, bf16[256,1024]{1,0:T(8,128)(2,1)S(1)}, u32[]{:S(2)}, u32[]{:S(2)}) collective-permute-start(bf16[256,1024]{1,0:T(8,128)(2,1)S(1)} %get-tuple-element.31), channel_id=1, source_target_pairs={{0,8},{4,12},{8,0},{12,4},{16,24},{20,28},{24,16},{28,20},{1,9},{5... | collective-permute-start | bytes 1572872 | tf_op jit(solution)/shard_map/ppermute | solution.py:23
  37.0 1.2 %collective-permute-start.4 = (bf16[128,1024]{1,0:T(8,128)(2,1)S(1)}, bf16[128,1024]{1,0:T(8,128)(2,1)S(1)}, u32[]{:S(2)}, u32[]{:S(2)}) collective-permute-start(bf16[128,1024]{1,0:T(8,128)(2,1)S(1)} %convolution_convert_fusion.7), channel_id=1, source_target_pairs={{0,1},{1,0},{2,3},{3,2},{4,5},{5,4},{6,7},{7,6},{8,9},{9,8},{10,11... | collective-permute-start | bytes 786440 | tf_op jit(solution)/shard_map/ppermute | solution.py:19
  39.0 5.6 %collective-permute-done.4 = bf16[128,1024]{1,0:T(8,128)(2,1)S(1)} collective-permute-done((bf16[128,1024]{1,0:T(8,128)(2,1)S(1)}, bf16[128,1024]{1,0:T(8,128)(2,1)S(1)}, u32[]{:S(2)}, u32[]{:S(2)}) %collective-permute-start.4) | collective-permute-done | bytes 262176 | tf_op jit(solution)/shard_map/ppermute | solution.py:19
  44.6 0.7 fusion.13
  46.1 13.4 %collective-permute-done.13 = bf16[256,1024]{1,0:T(8,128)(2,1)S(1)} collective-permute-done((bf16[256,1024]{1,0:T(8,128)(2,1)S(1)}, bf16[256,1024]{1,0:T(8,128)(2,1)S(1)}, u32[]{:S(2)}, u32[]{:S(2)}) %collective-permute-start.13) | collective-permute-done | bytes 524320 | tf_op jit(solution)/shard_map/ppermute | solution.py:23
  61.5 1.6 %collective-permute-start.5 = (bf16[128,1024]{1,0:T(8,128)(2,1)S(1)}, bf16[128,1024]{1,0:T(8,128)(2,1)S(1)}, u32[]{:S(2)}, u32[]{:S(2)}) collective-permute-start(bf16[128,1024]{1,0:T(8,128)(2,1)S(1)} %fusion.13), channel_id=1, source_target_pairs={{0,2},{1,3},{2,0},{3,1},{4,6},{5,7},{6,4},{7,5},{8,10},{9,11},{10,... | collective-permute-start | bytes 786440 | tf_op jit(solution)/shard_map/ppermute | solution.py:19
  63.0 1.5 %collective-permute-start.8 = (bf16[128,1024]{1,0:T(8,128)(2,1)S(1)}, bf16[128,1024]{1,0:T(8,128)(2,1)S(1)}, u32[]{:S(2)}, u32[]{:S(2)}) collective-permute-start(bf16[128,1024]{1,0:T(8,128)(2,1)S(1)} %fusion.14), channel_id=1, source_target_pairs={{0,1},{1,0},{2,3},{3,2},{4,5},{5,4},{6,7},{7,6},{8,9},{9,8},{10,11... | collective-permute-start | bytes 786440 | tf_op jit(solution)/shard_map/ppermute | solution.py:19
  64.7 4.0 %collective-permute-done.1 = bf16[128,1024]{1,0:T(8,128)(2,1)S(1)} collective-permute-done((bf16[128,1024]{1,0:T(8,128)(2,1)S(1)}, bf16[128,1024]{1,0:T(8,128)(2,1)S(1)}, u32[]{:S(2)}, u32[]{:S(2)}) %collective-permute-start.1) | collective-permute-done | bytes 262176 | tf_op jit(solution)/shard_map/ppermute | solution.py:19
  69.3 4.3 %collective-permute-done.5 = bf16[128,1024]{1,0:T(8,128)(2,1)S(1)} collective-permute-done((bf16[128,1024]{1,0:T(8,128)(2,1)S(1)}, bf16[128,1024]{1,0:T(8,128)(2,1)S(1)}, u32[]{:S(2)}, u32[]{:S(2)}) %collective-permute-start.5) | collective-permute-done | bytes 262176 | tf_op jit(solution)/shard_map/ppermute | solution.py:19
  73.7 1.3 %collective-permute-start.17 = (bf16[256,1024]{1,0:T(8,128)(2,1)S(1)}, bf16[256,1024]{1,0:T(8,128)(2,1)S(1)}, u32[]{:S(2)}, u32[]{:S(2)}) collective-permute-start(bf16[256,1024]{1,0:T(8,128)(2,1)S(1)} %collective-permute-done.14), channel_id=1, source_target_pairs={{16,24},{20,28},{8,0},{12,4},{17,25},{21,29},{9,1},{13,5},{18,26},... | collective-permute-start | bytes 1572872 | tf_op jit(solution)/shard_map/ppermute | solution.py:23
  76.8 1.6 %collective-permute-start.22 = (bf16[128,1024]{1,0:T(8,128)(2,1)S(1)}, bf16[128,1024]{1,0:T(8,128)(2,1)S(1)}, u32[]{:S(2)}, u32[]{:S(2)}) collective-permute-start(bf16[128,1024]{1,0:T(8,128)(2,1)S(1)} %multiply_convert_fusion), channel_id=1, source_target_pairs={{0,1},{1,0},{2,3},{3,2},{4,5},{5,4},{6,7},{7,6},{8,9},{9,8},{10,11... | collective-permute-start | bytes 786440 | tf_op jit(solution)/shard_map/ppermute | solution.py:19
  78.4 9.8 %collective-permute-done.17 = bf16[256,1024]{1,0:T(8,128)(2,1)S(1)} collective-permute-done((bf16[256,1024]{1,0:T(8,128)(2,1)S(1)}, bf16[256,1024]{1,0:T(8,128)(2,1)S(1)}, u32[]{:S(2)}, u32[]{:S(2)}) %collective-permute-start.17) | collective-permute-done | bytes 524320 | tf_op jit(solution)/shard_map/ppermute | solution.py:23
  89.9 1.6 %collective-permute-start.23 = (bf16[128,1024]{1,0:T(8,128)(2,1)S(1)}, bf16[128,1024]{1,0:T(8,128)(2,1)S(1)}, u32[]{:S(2)}, u32[]{:S(2)}) collective-permute-start(bf16[128,1024]{1,0:T(8,128)(2,1)S(1)} %fusion.8), channel_id=1, source_target_pairs={{0,1},{1,0},{2,3},{3,2},{4,5},{5,4},{6,7},{7,6},{8,9},{9,8},{10,11... | collective-permute-start | bytes 786440 | tf_op jit(solution)/shard_map/ppermute | solution.py:19
  92.2 1.5 %collective-permute-start.24 = (bf16[128,1024]{1,0:T(8,128)(2,1)S(1)}, bf16[128,1024]{1,0:T(8,128)(2,1)S(1)}, u32[]{:S(2)}, u32[]{:S(2)}) collective-permute-start(bf16[128,1024]{1,0:T(8,128)(2,1)S(1)} %convolution_convert_fusion.2), channel_id=1, source_target_pairs={{0,2},{1,3},{2,0},{3,1},{4,6},{5,7},{6,4},{7,5},{8,10},{9,11},{10,... | collective-permute-start | bytes 786440 | tf_op jit(solution)/shard_map/ppermute | solution.py:19
  95.7 2.4 %collective-permute-done.21 = bf16[128,1024]{1,0:T(8,128)(2,1)S(1)} collective-permute-done((bf16[128,1024]{1,0:T(8,128)(2,1)S(1)}, bf16[128,1024]{1,0:T(8,128)(2,1)S(1)}, u32[]{:S(2)}, u32[]{:S(2)}) %collective-permute-start.21) | collective-permute-done | bytes 262176 | tf_op jit(solution)/shard_map/ppermute | solution.py:19
  98.1 1.0 collective-permute-done.23
  99.1 4.1 %collective-permute-done.24 = bf16[128,1024]{1,0:T(8,128)(2,1)S(1)} collective-permute-done((bf16[128,1024]{1,0:T(8,128)(2,1)S(1)}, bf16[128,1024]{1,0:T(8,128)(2,1)S(1)}, u32[]{:S(2)}, u32[]{:S(2)}) %collective-permute-start.24) | collective-permute-done | bytes 262176 | tf_op jit(solution)/shard_map/ppermute | solution.py:19
  (72 shorter events, 14.2 us)
Async XLA Ops:
  0.0 12.5 %copy-start.4 = (bf16[128,8192]{1,0:T(8,128)(2,1)S(1)}, bf16[128,8192]{1,0:T(8,128)(2,1)}, u32[]{:S(2)}) copy-start(bf16[128,8192]{1,0:T(8,128)(2,1)} %param.4) | copy-start | bytes 6291460
  1.9 16.0 %collective-permute-start.9 = (bf16[128,1024]{1,0:T(8,128)(2,1)}, bf16[128,1024]{1,0:T(8,128)(2,1)}, u32[]{:S(2)}, u32[]{:S(2)}) collective-permute-start(bf16[128,1024]{1,0:T(8,128)(2,1)} %get-tuple-element.12), channel_id=1, source_target_pairs={{0,1},{1,0},{2,3},{3,2},{4,5},{5,4},{6,7},{7,6},{8,9},{9,8},{10,11... | collective-permute-start | bytes 786440 | tf_op jit(solution)/shard_map/ppermute | solution.py:19
  4.9 14.4 %collective-permute-start.10 = (bf16[128,1024]{1,0:T(8,128)(2,1)S(1)}, bf16[128,1024]{1,0:T(8,128)(2,1)}, u32[]{:S(2)}, u32[]{:S(2)}) collective-permute-start(bf16[128,1024]{1,0:T(8,128)(2,1)S(1)} %get-tuple-element.11), channel_id=1, source_target_pairs={{0,2},{1,3},{2,0},{3,1},{4,6},{5,7},{6,4},{7,5},{8,10},{9,11},{10,... | collective-permute-start | bytes 786440 | tf_op jit(solution)/shard_map/ppermute | solution.py:19
  9.0 17.1 %collective-permute-start.3 = (bf16[128,2048]{1,0:T(8,128)(2,1)}, bf16[128,2048]{1,0:T(8,128)(2,1)}, u32[]{:S(2)}, u32[]{:S(2)}) collective-permute-start(bf16[128,2048]{1,0:T(8,128)(2,1)} %get-tuple-element.15), channel_id=1, source_target_pairs={{0,3},{1,2},{2,1},{3,0},{4,7},{5,6},{6,5},{7,4},{8,11},{9,10},{10,... | collective-permute-start | bytes 1572872 | tf_op jit(solution)/shard_map/ppermute | solution.py:19
  9.0 28.0 %collective-permute-start.2 = (bf16[128,2048]{1,0:T(8,128)(2,1)}, bf16[128,2048]{1,0:T(8,128)(2,1)S(1)}, u32[]{:S(2)}, u32[]{:S(2)}) collective-permute-start(bf16[128,2048]{1,0:T(8,128)(2,1)} %get-tuple-element.13), channel_id=1, source_target_pairs={{0,2},{1,3},{2,0},{3,1},{4,6},{5,7},{6,4},{7,5},{8,10},{9,11},{10,... | collective-permute-start | bytes 1572872 | tf_op jit(solution)/shard_map/ppermute | solution.py:19
  10.9 23.7 %collective-permute-start = (bf16[128,2048]{1,0:T(8,128)(2,1)}, bf16[128,2048]{1,0:T(8,128)(2,1)S(1)}, u32[]{:S(2)}, u32[]{:S(2)}) collective-permute-start(bf16[128,2048]{1,0:T(8,128)(2,1)} %get-tuple-element.14), channel_id=1, source_target_pairs={{0,1},{1,0},{2,3},{3,2},{4,5},{5,4},{6,7},{7,6},{8,9},{9,8},{10,11... | collective-permute-start | bytes 1572872 | tf_op jit(solution)/shard_map/ppermute | solution.py:19
  17.9 9.5 %copy-start.1 = (bf16[2048,1024]{1,0:T(8,128)(2,1)S(1)}, bf16[2048,1024]{1,0:T(8,128)(2,1)}, u32[]{:S(2)}) copy-start(bf16[2048,1024]{1,0:T(8,128)(2,1)} %param.5) | copy-start | bytes 12582916
  20.6 8.6 %copy-start.2 = (bf16[2048,1024]{1,0:T(8,128)(2,1)S(1)}, bf16[2048,1024]{1,0:T(8,128)(2,1)}, u32[]{:S(2)}) copy-start(bf16[2048,1024]{1,0:T(8,128)(2,1)} %param.6) | copy-start | bytes 12582916
  20.6 24.8 %collective-permute-start.14 = (bf16[256,1024]{1,0:T(8,128)(2,1)S(1)}, bf16[256,1024]{1,0:T(8,128)(2,1)S(1)}, u32[]{:S(2)}, u32[]{:S(2)}) collective-permute-start(bf16[256,1024]{1,0:T(8,128)(2,1)S(1)} %get-tuple-element.31), channel_id=1, source_target_pairs={{0,16},{4,20},{24,8},{28,12},{1,17},{5,21},{25,9},{29,13},{2,18},{... | collective-permute-start | bytes 1572872 | tf_op jit(solution)/shard_map/ppermute | solution.py:23
  25.4 51.4 %collective-permute-start.18 = (bf16[256,1024]{1,0:T(8,128)(2,1)S(1)}, bf16[256,1024]{1,0:T(8,128)(2,1)S(1)}, u32[]{:S(2)}, u32[]{:S(2)}) collective-permute-start(bf16[256,1024]{1,0:T(8,128)(2,1)S(1)} %get-tuple-element.31), channel_id=1, source_target_pairs={{8,16},{12,20},{16,8},{20,12},{9,17},{13,21},{17,9},{21,13},{10,18... | collective-permute-start | bytes 1572872 | tf_op jit(solution)/shard_map/ppermute | solution.py:23
  26.1 33.4 %collective-permute-start.13 = (bf16[256,1024]{1,0:T(8,128)(2,1)S(1)}, bf16[256,1024]{1,0:T(8,128)(2,1)S(1)}, u32[]{:S(2)}, u32[]{:S(2)}) collective-permute-start(bf16[256,1024]{1,0:T(8,128)(2,1)S(1)} %get-tuple-element.31), channel_id=1, source_target_pairs={{8,24},{12,28},{16,0},{20,4},{9,25},{13,29},{17,1},{21,5},{10,26},... | collective-permute-start | bytes 1572872 | tf_op jit(solution)/shard_map/ppermute | solution.py:23
  34.7 26.8 %collective-permute-start.12 = (bf16[256,1024]{1,0:T(8,128)(2,1)S(1)}, bf16[256,1024]{1,0:T(8,128)(2,1)S(1)}, u32[]{:S(2)}, u32[]{:S(2)}) collective-permute-start(bf16[256,1024]{1,0:T(8,128)(2,1)S(1)} %get-tuple-element.31), channel_id=1, source_target_pairs={{0,8},{4,12},{8,0},{12,4},{16,24},{20,28},{24,16},{28,20},{1,9},{5... | collective-permute-start | bytes 1572872 | tf_op jit(solution)/shard_map/ppermute | solution.py:23
  37.0 7.6 %collective-permute-start.4 = (bf16[128,1024]{1,0:T(8,128)(2,1)S(1)}, bf16[128,1024]{1,0:T(8,128)(2,1)S(1)}, u32[]{:S(2)}, u32[]{:S(2)}) collective-permute-start(bf16[128,1024]{1,0:T(8,128)(2,1)S(1)} %convolution_convert_fusion.7), channel_id=1, source_target_pairs={{0,1},{1,0},{2,3},{3,2},{4,5},{5,4},{6,7},{7,6},{8,9},{9,8},{10,11... | collective-permute-start | bytes 786440 | tf_op jit(solution)/shard_map/ppermute | solution.py:19
  44.6 18.4 %collective-permute-start.11 = (bf16[256,1024]{1,0:T(8,128)(2,1)S(1)}, bf16[256,1024]{1,0:T(8,128)(2,1)S(1)}, u32[]{:S(2)}, u32[]{:S(2)}) collective-permute-start(bf16[256,1024]{1,0:T(8,128)(2,1)S(1)} %get-tuple-element.31), channel_id=1, source_target_pairs={{0,4},{4,0},{8,12},{12,8},{16,20},{20,16},{24,28},{28,24},{1,5},{5... | collective-permute-start | bytes 1572872 | tf_op jit(solution)/shard_map/ppermute | solution.py:23
  45.4 14.7 %collective-permute-start.7 = (bf16[128,1024]{1,0:T(8,128)(2,1)S(1)}, bf16[128,1024]{1,0:T(8,128)(2,1)S(1)}, u32[]{:S(2)}, u32[]{:S(2)}) collective-permute-start(bf16[128,1024]{1,0:T(8,128)(2,1)S(1)} %convolution_convert_fusion.5), channel_id=1, source_target_pairs={{0,2},{1,3},{2,0},{3,1},{4,6},{5,7},{6,4},{7,5},{8,10},{9,11},{10,... | collective-permute-start | bytes 786440 | tf_op jit(solution)/shard_map/ppermute | solution.py:19
  59.5 9.2 %collective-permute-start.1 = (bf16[128,1024]{1,0:T(8,128)(2,1)S(1)}, bf16[128,1024]{1,0:T(8,128)(2,1)S(1)}, u32[]{:S(2)}, u32[]{:S(2)}) collective-permute-start(bf16[128,1024]{1,0:T(8,128)(2,1)S(1)} %convolution_convert_fusion.8), channel_id=1, source_target_pairs={{0,1},{1,0},{2,3},{3,2},{4,5},{5,4},{6,7},{7,6},{8,9},{9,8},{10,11... | collective-permute-start | bytes 786440 | tf_op jit(solution)/shard_map/ppermute | solution.py:19
  60.1 9.2 %collective-permute-start.6 = (bf16[128,1024]{1,0:T(8,128)(2,1)S(1)}, bf16[128,1024]{1,0:T(8,128)(2,1)S(1)}, u32[]{:S(2)}, u32[]{:S(2)}) collective-permute-start(bf16[128,1024]{1,0:T(8,128)(2,1)S(1)} %convolution_convert_fusion.6), channel_id=1, source_target_pairs={{0,2},{1,3},{2,0},{3,1},{4,6},{5,7},{6,4},{7,5},{8,10},{9,11},{10,... | collective-permute-start | bytes 786440 | tf_op jit(solution)/shard_map/ppermute | solution.py:19
  61.4 13.5 %copy-start.6 = (f32[128,1024]{1,0:T(8,128)S(1)}, f32[128,1024]{1,0:T(8,128)}, u32[]{:S(2)}) copy-start(f32[128,1024]{1,0:T(8,128)} %fusion.15) | copy-start | bytes 1572868
  61.5 13.5 %copy-start.7 = (f32[128,1024]{1,0:T(8,128)S(1)}, f32[128,1024]{1,0:T(8,128)}, u32[]{:S(2)}) copy-start(f32[128,1024]{1,0:T(8,128)} %fusion.17) | copy-start | bytes 1572868
  61.5 12.2 %collective-permute-start.5 = (bf16[128,1024]{1,0:T(8,128)(2,1)S(1)}, bf16[128,1024]{1,0:T(8,128)(2,1)S(1)}, u32[]{:S(2)}, u32[]{:S(2)}) collective-permute-start(bf16[128,1024]{1,0:T(8,128)(2,1)S(1)} %fusion.13), channel_id=1, source_target_pairs={{0,2},{1,3},{2,0},{3,1},{4,6},{5,7},{6,4},{7,5},{8,10},{9,11},{10,... | collective-permute-start | bytes 786440 | tf_op jit(solution)/shard_map/ppermute | solution.py:19
  63.0 11.9 %collective-permute-start.8 = (bf16[128,1024]{1,0:T(8,128)(2,1)S(1)}, bf16[128,1024]{1,0:T(8,128)(2,1)S(1)}, u32[]{:S(2)}, u32[]{:S(2)}) collective-permute-start(bf16[128,1024]{1,0:T(8,128)(2,1)S(1)} %fusion.14), channel_id=1, source_target_pairs={{0,1},{1,0},{2,3},{3,2},{4,5},{5,4},{6,7},{7,6},{8,9},{9,8},{10,11... | collective-permute-start | bytes 786440 | tf_op jit(solution)/shard_map/ppermute | solution.py:19
  64.7 11.4 %copy-start.3 = (bf16[1024,2048]{1,0:T(8,128)(2,1)S(1)}, bf16[1024,2048]{1,0:T(8,128)(2,1)}, u32[]{:S(2)}) copy-start(bf16[1024,2048]{1,0:T(8,128)(2,1)} %param.7) | copy-start | bytes 12582916
  68.7 22.8 %collective-permute-start.15 = (bf16[256,1024]{1,0:T(8,128)(2,1)S(1)}, bf16[256,1024]{1,0:T(8,128)(2,1)S(1)}, u32[]{:S(2)}, u32[]{:S(2)}) collective-permute-start(bf16[256,1024]{1,0:T(8,128)(2,1)S(1)} %collective-permute-done.12), channel_id=1, source_target_pairs={{0,4},{4,0},{8,12},{12,8},{16,20},{20,16},{24,28},{28,24},{1,5},{5... | collective-permute-start | bytes 1572872 | tf_op jit(solution)/shard_map/ppermute | solution.py:23
  69.3 22.2 %collective-permute-start.16 = (bf16[256,1024]{1,0:T(8,128)(2,1)S(1)}, bf16[256,1024]{1,0:T(8,128)(2,1)S(1)}, u32[]{:S(2)}, u32[]{:S(2)}) collective-permute-start(bf16[256,1024]{1,0:T(8,128)(2,1)S(1)} %broadcast_select_fusion.1), channel_id=1, source_target_pairs={{0,4},{4,0},{8,12},{12,8},{16,20},{20,16},{24,28},{28,24},{1,5},{5... | collective-permute-start | bytes 1572872 | tf_op jit(solution)/shard_map/ppermute | solution.py:23
  73.7 14.5 %collective-permute-start.17 = (bf16[256,1024]{1,0:T(8,128)(2,1)S(1)}, bf16[256,1024]{1,0:T(8,128)(2,1)S(1)}, u32[]{:S(2)}, u32[]{:S(2)}) collective-permute-start(bf16[256,1024]{1,0:T(8,128)(2,1)S(1)} %collective-permute-done.14), channel_id=1, source_target_pairs={{16,24},{20,28},{8,0},{12,4},{17,25},{21,29},{9,1},{13,5},{18,26},... | collective-permute-start | bytes 1572872 | tf_op jit(solution)/shard_map/ppermute | solution.py:23
  75.3 13.1 %collective-permute-start.20 = (bf16[128,1024]{1,0:T(8,128)(2,1)S(1)}, bf16[128,1024]{1,0:T(8,128)(2,1)S(1)}, u32[]{:S(2)}, u32[]{:S(2)}) collective-permute-start(bf16[128,1024]{1,0:T(8,128)(2,1)S(1)} %multiply_convert_fusion), channel_id=1, source_target_pairs={{0,2},{1,3},{2,0},{3,1},{4,6},{5,7},{6,4},{7,5},{8,10},{9,11},{10,... | collective-permute-start | bytes 786440 | tf_op jit(solution)/shard_map/ppermute | solution.py:19
  76.8 12.6 %collective-permute-start.22 = (bf16[128,1024]{1,0:T(8,128)(2,1)S(1)}, bf16[128,1024]{1,0:T(8,128)(2,1)S(1)}, u32[]{:S(2)}, u32[]{:S(2)}) collective-permute-start(bf16[128,1024]{1,0:T(8,128)(2,1)S(1)} %multiply_convert_fusion), channel_id=1, source_target_pairs={{0,1},{1,0},{2,3},{3,2},{4,5},{5,4},{6,7},{7,6},{8,9},{9,8},{10,11... | collective-permute-start | bytes 786440 | tf_op jit(solution)/shard_map/ppermute | solution.py:19
  88.3 3.4 %collective-permute-start.19 = (bf16[256,1024]{1,0:T(8,128)(2,1)S(1)}, bf16[256,1024]{1,0:T(8,128)(2,1)S(1)}, u32[]{:S(2)}, u32[]{:S(2)}) collective-permute-start(bf16[256,1024]{1,0:T(8,128)(2,1)S(1)} %broadcast_select_fusion), channel_id=1, source_target_pairs={{0,4},{4,0},{8,12},{12,8},{16,20},{20,16},{24,28},{28,24},{1,5},{5... | collective-permute-start | bytes 1572872 | tf_op jit(solution)/shard_map/ppermute | solution.py:23
  88.8 9.2 %collective-permute-start.21 = (bf16[128,1024]{1,0:T(8,128)(2,1)S(1)}, bf16[128,1024]{1,0:T(8,128)(2,1)S(1)}, u32[]{:S(2)}, u32[]{:S(2)}) collective-permute-start(bf16[128,1024]{1,0:T(8,128)(2,1)S(1)} %fusion.5), channel_id=1, source_target_pairs={{0,2},{1,3},{2,0},{3,1},{4,6},{5,7},{6,4},{7,5},{8,10},{9,11},{10,... | collective-permute-start | bytes 786440 | tf_op jit(solution)/shard_map/ppermute | solution.py:19
  89.9 9.2 %collective-permute-start.23 = (bf16[128,1024]{1,0:T(8,128)(2,1)S(1)}, bf16[128,1024]{1,0:T(8,128)(2,1)S(1)}, u32[]{:S(2)}, u32[]{:S(2)}) collective-permute-start(bf16[128,1024]{1,0:T(8,128)(2,1)S(1)} %fusion.8), channel_id=1, source_target_pairs={{0,1},{1,0},{2,3},{3,2},{4,5},{5,4},{6,7},{7,6},{8,9},{9,8},{10,11... | collective-permute-start | bytes 786440 | tf_op jit(solution)/shard_map/ppermute | solution.py:19
  92.2 11.0 %collective-permute-start.24 = (bf16[128,1024]{1,0:T(8,128)(2,1)S(1)}, bf16[128,1024]{1,0:T(8,128)(2,1)S(1)}, u32[]{:S(2)}, u32[]{:S(2)}) collective-permute-start(bf16[128,1024]{1,0:T(8,128)(2,1)S(1)} %convolution_convert_fusion.2), channel_id=1, source_target_pairs={{0,2},{1,3},{2,0},{3,1},{4,6},{5,7},{6,4},{7,5},{8,10},{9,11},{10,... | collective-permute-start | bytes 786440 | tf_op jit(solution)/shard_map/ppermute | solution.py:19
  94.6 9.3 %collective-permute-start.25 = (bf16[128,1024]{1,0:T(8,128)(2,1)S(1)}, bf16[128,1024]{1,0:T(8,128)(2,1)S(1)}, u32[]{:S(2)}, u32[]{:S(2)}) collective-permute-start(bf16[128,1024]{1,0:T(8,128)(2,1)S(1)} %convolution_convert_fusion.1), channel_id=1, source_target_pairs={{0,1},{1,0},{2,3},{3,2},{4,5},{5,4},{6,7},{7,6},{8,9},{9,8},{10,11... | collective-permute-start | bytes 786440 | tf_op jit(solution)/shard_map/ppermute | solution.py:19
  (2 other events, 5.2 us)

commit v3 on v2

--- a/solution.py
+++ b/solution.py
@@ -36,7 +36,7 @@
         chip, core = d // cores, d % cores
         slab = w_gate.shape[0]
         hidden_width, width = w_down.shape
-        half = width // 2
+        cut = width * 9 // 16
         share = hidden_width // dp
 
         def place(shift):
@@ -44,7 +44,9 @@
 
         piece = lax.dynamic_slice_in_dim(w_down, d * share, share, axis=0)
         sides = [(0, dc) for dc in range(1, cols)] + [(dr, 0) for dr in range(1, rows)]
-        held = jnp.concatenate([send(piece[:, half:] if s[0] else piece[:, :half], back(s)) for s in sides], axis=0)
+        held = jnp.concatenate([send(piece[:, cut:] if s[0] else piece[:, :cut], back(s)) for s in sides], axis=1)
+        ends = [(width - cut if s[0] else cut) for s in sides]
+        ends = {s: (sum(ends[:i]), sum(ends[: i + 1])) for i, s in enumerate(sides)}
 
         feats = {s: lax.dynamic_slice_in_dim(tokens, place(s) * slab, slab, axis=1) for s in shifts}
         got = {s: send(feats[s], s) for s in away}
@@ -59,8 +61,9 @@
             relayed = send_dp(two_a, [(2, 3), (1, 0)], 0)
             outer = (chip == 0) | (chip == chips - 1)
             two = jnp.where(outer, two_b, two_a)
-            early += [(one, chip ^ 1), (two, chip ^ 2)]
+            early += [(held, chip), (one, chip ^ 1), (two, chip ^ 2)]
         else:
+            early.append((held, chip))
             for z in range(1, chips):
                 turn = send_dp(held, [(i, (i + z) % chips) for i in range(chips)], 0)
                 late.append((turn, (chip - z) % chips))
@@ -71,7 +74,9 @@
             def shift(a, b):
                 return (b, a) if col_first else (a, b)
 
-            parts = {s: matmul(got[s], weight) for s in away}
+            parts = {}
+            for s in away:
+                parts[s] = matmul(got[s], weight)
             parts[0, 0] = matmul(got[0, 0], weight)
             sums = {b: parts[shift(0, b)] for b in range(second)}
             for b in reversed(range(second)):
@@ -91,17 +96,16 @@
         if chips == 4:
             late.append((jnp.where(outer, relayed, middle), chip ^ 3))
 
-        far = {s: jnp.zeros((hidden_width, half), jnp.bfloat16) for s in sides}
+        far = {s: jnp.zeros((hidden_width, ends[s][1] - ends[s][0]), jnp.bfloat16) for s in sides}
 
         def fill(pieces):
             for k in range(cores):
                 for block, from_chip in pieces:
                     moved = swap(block, k) if k else block
                     at = (from_chip * cores + (core - k) % cores) * share
-                    for i, s in enumerate(sides):
-                        far[s] = lax.dynamic_update_slice_in_dim(far[s], moved[i * share : (i + 1) * share], at, axis=0)
+                    for s in sides:
+                        far[s] = lax.dynamic_update_slice_in_dim(far[s], moved[:, slice(*ends[s])], at, axis=0)
 
-        fill([(held, chip)])
         tied, _ = lax.optimization_barrier(([p for p, _ in early], gate_passed + up_passed))
         fill([(p, at) for p, (_, at) in zip(tied, early)])
 
@@ -111,15 +115,15 @@
         landed = [(matmul(hidden, w_down).astype(jnp.bfloat16), place((0, 0)) * width)]
         outs = []
         for s, other in near.items():
-            weight, at = (w_down[:, :half], 0) if s[1] == 0 else (w_down[:, half:], half)
+            weight, at = (w_down[:, :cut], 0) if s[1] == 0 else (w_down[:, cut:], cut)
             own_out = matmul(other, weight).astype(jnp.bfloat16)
             outs.append((send(own_out, s), place(back(s)) * width + at))
 
         for s in sides:
-            at = half if s[0] else 0
+            at = cut if s[0] else 0
             landed.append((matmul(hidden, far[s]).astype(jnp.bfloat16), place(s) * width + at))
         for s, other in near.items():
-            at = 0 if s[1] == 0 else half
+            at = 0 if s[1] == 0 else cut
             for t in sides:
                 if (t[0] == 0) == (s[1] == 0):
                     far_out = send(matmul(other, far[t]).astype(jnp.bfloat16), s)

time: 106 us -> 109 us (1.028)
  starting transfers between devices: 30.3 us -> 33 us
  waiting for transfers between devices: 49.7 us -> 47.4 us
  matrix products: 15.4 us -> 17.1 us
  local copies, waits for them, and re-layouts: 9.06 us -> 10.3 us
    ppermute x9, waiting for transfers between devices: 23.2 us -> 1.57 us  [send_dp(): return lax.ppermute(x, 'dp', pairs)]
    ppermute x17, waiting for transfers between devices: 26.4 us -> 45.9 us  [send(): return lax.ppermute(x, ('row', 'col'), pairs)]
    ppermute x9, starting transfers between devices: 9.7 us -> 11.4 us  [send_dp(): return lax.ppermute(x, 'dp', pairs)]
    dot_general x15, matrix products: 15.4 us -> 17.1 us  [matmul(): return jnp.dot(a, b, preferred_element_type=jnp.float32)]
    slice x1 -> x2, local copies, waits for them, and re-layouts: 1.92 us -> 3.35 us  [the longest x1 1.69 us: shards(): piece[:, :cut]]
where the time goes in v3:
time: 109 us
  waiting for transfers between devices  47.4 us (43%)
  starting transfers between devices  33 us (30%)
  matrix products  17.1 us (16%)
  local copies, waits for them, and re-layouts  10.3 us (9%)
    ppermute x17, waiting for transfers between devices, send(): return lax.ppermute(x, ('row', 'col'), pairs)  45.9 us
    ppermute x17, starting transfers between devices, send(): return lax.ppermute(x, ('row', 'col'), pairs)  21.5 us
    dot_general x15, matrix products, matmul(): return jnp.dot(a, b, preferred_element_type=jnp.float32)  17.1 us
    ppermute x9, starting transfers between devices, send_dp(): return lax.ppermute(x, 'dp', pairs)  11.4 us
    dynamic_slice x1, local copies, waits for them, and re-layouts, shards(): lax.dynamic_slice_in_dim(tokens, place(s) * slab, slab, axis=1)  2.7 us
  transfers between devices with their start and end apart: 26, of which 11 were waited for; matrix products, arithmetic and copies ran while one was open for 21% of the time, Pallas kernels for 0%

profile of v3, /device:TPU:0, one launch (start us, length us, event | category | flops | bytes accessed | tf_op | source)
XLA Modules:
  0.0 108.6 jit_solution(6590667173975540772)
XLA Ops:
  0.0 2.7 %constant_dynamic-slice_fusion.2 = (bf16[128,2048]{1,0:T(8,128)(2,1)}, bf16[128,2048]{1,0:T(8,128)(2,1)}, bf16[128,2048]{1,0:T(8,128)(2,1)}) fusion(bf16[128,8192]{1,0:T(8,128)(2,1)} %param.4, s32[]{:T(128)S(6)} %select_n.167, s32[]{:T(128)S(6)} %select_n.165, s32[]{:T(128)S(6)} %select_n.168), kind=kLoop, calls=%fused_computation.51 | loop fusion | bytes 3145740 | tf_op jit(solution)/shard_map/dynamic_slice | solution.py:51
  2.7 3.9 %collective-permute-start.3 = (bf16[128,2048]{1,0:T(8,128)(2,1)}, bf16[128,2048]{1,0:T(8,128)(2,1)}, u32[]{:S(2)}, u32[]{:S(2)}) collective-permute-start(bf16[128,2048]{1,0:T(8,128)(2,1)} %get-tuple-element.15), channel_id=1, source_target_pairs={{0,3},{1,2},{2,1},{3,0},{4,7},{5,6},{6,5},{7,4},{8,11},{9,10},{10,... | collective-permute-start | bytes 1572872 | tf_op jit(solution)/shard_map/ppermute | solution.py:19
  7.2 1.7 %constant_dynamic-slice_fusion = bf16[128,1152]{1,0:T(8,128)(2,1)} fusion(bf16[1024,2048]{1,0:T(8,128)(2,1)} %param.7, s32[]{:T(128)S(6)} %select_n.169), kind=kLoop, calls=%fused_computation.45 | loop fusion | bytes 589828 | tf_op jit(solution)/shard_map/slice | solution.py:47
  8.9 1.7 %dynamic-slice.1 = bf16[128,896]{1,0:T(8,128)(2,1)} dynamic-slice(bf16[1024,2048]{1,0:T(8,128)(2,1)} %param.7, s32[]{:T(128)S(6)} %select_n.169, s32[]{:T(128)S(6)} %add.272), dynamic_slice_sizes={128,896} | dynamic-slice | bytes 458756 | tf_op jit(solution)/shard_map/slice | solution.py:47
  10.5 2.0 %collective-permute-start.10 = (bf16[128,896]{1,0:T(8,128)(2,1)}, bf16[128,896]{1,0:T(8,128)(2,1)}, u32[]{:S(2)}, u32[]{:S(2)}) collective-permute-start(bf16[128,896]{1,0:T(8,128)(2,1)} %dynamic-slice.1), channel_id=1, source_target_pairs={{0,2},{1,3},{2,0},{3,1},{4,6},{5,7},{6,4},{7,5},{8,10},{9,11},{10,... | collective-permute-start | bytes 688136 | tf_op jit(solution)/shard_map/ppermute | solution.py:19
  12.5 1.5 %collective-permute-start = (bf16[128,2048]{1,0:T(8,128)(2,1)}, bf16[128,2048]{1,0:T(8,128)(2,1)S(1)}, u32[]{:S(2)}, u32[]{:S(2)}) collective-permute-start(bf16[128,2048]{1,0:T(8,128)(2,1)} %get-tuple-element.14), channel_id=1, source_target_pairs={{0,1},{1,0},{2,3},{3,2},{4,5},{5,4},{6,7},{7,6},{8,9},{9,8},{10,11... | collective-permute-start | bytes 1572872 | tf_op jit(solution)/shard_map/ppermute | solution.py:19
  14.0 3.8 %fusion.11 = f32[128,1024]{1,0:T(8,128)} fusion(bf16[2048,1024]{1,0:T(8,128)(2,1)} %param.6, bf16[128,8192]{1,0:T(8,128)(2,1)S(1)} %copy-done.4, s32[]{:T(128)S(6)} %select_n.163), kind=kOutput, calls=%fused_computation.24 | convolution fusion | flops 536870912 | bytes 5242884 | tf_op jit(solution)/shard_map/dot_general | solution.py:32
  17.9 1.5 %fusion.13 = f32[128,1024]{1,0:T(8,128)} fusion(bf16[2048,1024]{1,0:T(8,128)(2,1)S(1)} %copy-done, bf16[128,8192]{1,0:T(8,128)(2,1)S(1)} %copy-done.4, s32[]{:T(128)S(6)} %select_n.163), kind=kOutput, calls=%fused_computation.26 | convolution fusion | flops 536870912 | bytes 5242884 | tf_op jit(solution)/shard_map/dot_general | solution.py:32
  19.4 5.8 %collective-permute-done.9 = bf16[128,1152]{1,0:T(8,128)(2,1)S(1)} collective-permute-done((bf16[128,1152]{1,0:T(8,128)(2,1)}, bf16[128,1152]{1,0:T(8,128)(2,1)S(1)}, u32[]{:S(2)}, u32[]{:S(2)}) %collective-permute-start.9) | collective-permute-done | bytes 294944 | tf_op jit(solution)/shard_map/ppermute | solution.py:19
  25.2 10.1 %collective-permute-done.10 = bf16[128,896]{1,0:T(8,128)(2,1)} collective-permute-done((bf16[128,896]{1,0:T(8,128)(2,1)}, bf16[128,896]{1,0:T(8,128)(2,1)}, u32[]{:S(2)}, u32[]{:S(2)}) %collective-permute-start.10) | collective-permute-done | bytes 229408 | tf_op jit(solution)/shard_map/ppermute | solution.py:19
  36.3 4.8 %collective-permute-start.13 = (bf16[128,2048]{1,0:T(8,128)(2,1)S(1)}, bf16[128,2048]{1,0:T(8,128)(2,1)S(1)}, u32[]{:S(2)}, u32[]{:S(2)}) collective-permute-start(bf16[128,2048]{1,0:T(8,128)(2,1)S(1)} %constant_dynamic-update-slice_fusion.4), channel_id=1, source_target_pairs={{0,16},{4,20},{24,8},{28,12},{1,17},{5,21},{25,9},{29,13},{2,18},{... | collective-permute-start | bytes 1572872 | tf_op jit(solution)/shard_map/ppermute | solution.py:23
  42.4 2.6 %collective-permute-start.11 = (bf16[128,2048]{1,0:T(8,128)(2,1)S(1)}, bf16[128,2048]{1,0:T(8,128)(2,1)S(1)}, u32[]{:S(2)}, u32[]{:S(2)}) collective-permute-start(bf16[128,2048]{1,0:T(8,128)(2,1)S(1)} %constant_dynamic-update-slice_fusion.4), channel_id=1, source_target_pairs={{0,8},{4,12},{8,0},{12,4},{16,24},{20,28},{24,16},{28,20},{1,9},{5... | collective-permute-start | bytes 1572872 | tf_op jit(solution)/shard_map/ppermute | solution.py:23
  45.0 3.1 %convolution_convert_fusion.6 = bf16[128,1024]{1,0:T(8,128)(2,1)S(1)} fusion(bf16[128,2048]{1,0:T(8,128)(2,1)} %collective-permute-done.3, bf16[2048,1024]{1,0:T(8,128)(2,1)} %param.5), kind=kOutput, calls=%fused_computation.15 | convolution fusion | flops 537001984 | bytes 4980736 | tf_op jit(solution)/shard_map/dot_general | solution.py:32
  48.1 1.9 %convolution_convert_fusion.4 = bf16[128,1024]{1,0:T(8,128)(2,1)S(1)} fusion(bf16[128,2048]{1,0:T(8,128)(2,1)} %collective-permute-done.3, bf16[2048,1024]{1,0:T(8,128)(2,1)S(1)} %copy-done.2), kind=kOutput, calls=%fused_computation.13 | convolution fusion | flops 537001984 | bytes 4980736 | tf_op jit(solution)/shard_map/dot_general | solution.py:32
  52.9 5.1 %collective-permute-done.4 = bf16[128,1024]{1,0:T(8,128)(2,1)S(1)} collective-permute-done((bf16[128,1024]{1,0:T(8,128)(2,1)S(1)}, bf16[128,1024]{1,0:T(8,128)(2,1)S(1)}, u32[]{:S(2)}, u32[]{:S(2)}) %collective-permute-start.4) | collective-permute-done | bytes 262176 | tf_op jit(solution)/shard_map/ppermute | solution.py:19
  58.0 1.5 %collective-permute-start.7 = (bf16[128,1024]{1,0:T(8,128)(2,1)S(1)}, bf16[128,1024]{1,0:T(8,128)(2,1)S(1)}, u32[]{:S(2)}, u32[]{:S(2)}) collective-permute-start(bf16[128,1024]{1,0:T(8,128)(2,1)S(1)} %convolution_convert_fusion.4), channel_id=1, source_target_pairs={{0,2},{1,3},{2,0},{3,1},{4,6},{5,7},{6,4},{7,5},{8,10},{9,11},{10,... | collective-permute-start | bytes 786440 | tf_op jit(solution)/shard_map/ppermute | solution.py:19
  60.2 4.1 %collective-permute-done.7 = bf16[128,1024]{1,0:T(8,128)(2,1)S(1)} collective-permute-done((bf16[128,1024]{1,0:T(8,128)(2,1)S(1)}, bf16[128,1024]{1,0:T(8,128)(2,1)S(1)}, u32[]{:S(2)}, u32[]{:S(2)}) %collective-permute-start.7) | collective-permute-done | bytes 262176 | tf_op jit(solution)/shard_map/ppermute | solution.py:19
  65.6 1.6 %collective-permute-start.6 = (bf16[128,1024]{1,0:T(8,128)(2,1)S(1)}, bf16[128,1024]{1,0:T(8,128)(2,1)S(1)}, u32[]{:S(2)}, u32[]{:S(2)}) collective-permute-start(bf16[128,1024]{1,0:T(8,128)(2,1)S(1)} %convolution_convert_fusion.5), channel_id=1, source_target_pairs={{0,2},{1,3},{2,0},{3,1},{4,6},{5,7},{6,4},{7,5},{8,10},{9,11},{10,... | collective-permute-start | bytes 786440 | tf_op jit(solution)/shard_map/ppermute | solution.py:19
  67.8 1.6 %collective-permute-start.8 = (bf16[128,1024]{1,0:T(8,128)(2,1)S(1)}, bf16[128,1024]{1,0:T(8,128)(2,1)S(1)}, u32[]{:S(2)}, u32[]{:S(2)}) collective-permute-start(bf16[128,1024]{1,0:T(8,128)(2,1)S(1)} %fusion.6), channel_id=1, source_target_pairs={{0,1},{1,0},{2,3},{3,2},{4,5},{5,4},{6,7},{7,6},{8,9},{9,8},{10,11... | collective-permute-start | bytes 786440 | tf_op jit(solution)/shard_map/ppermute | solution.py:19
  70.0 3.1 %collective-permute-done.1 = bf16[128,1024]{1,0:T(8,128)(2,1)S(1)} collective-permute-done((bf16[128,1024]{1,0:T(8,128)(2,1)S(1)}, bf16[128,1024]{1,0:T(8,128)(2,1)S(1)}, u32[]{:S(2)}, u32[]{:S(2)}) %collective-permute-start.1) | collective-permute-done | bytes 262176 | tf_op jit(solution)/shard_map/ppermute | solution.py:19
  73.6 2.1 %collective-permute-done.5 = bf16[128,1024]{1,0:T(8,128)(2,1)S(1)} collective-permute-done((bf16[128,1024]{1,0:T(8,128)(2,1)S(1)}, bf16[128,1024]{1,0:T(8,128)(2,1)S(1)}, u32[]{:S(2)}, u32[]{:S(2)}) %collective-permute-start.5) | collective-permute-done | bytes 262176 | tf_op jit(solution)/shard_map/ppermute | solution.py:19
  75.7 1.5 %collective-permute-start.17 = (bf16[128,2048]{1,0:T(8,128)(2,1)S(1)}, bf16[128,2048]{1,0:T(8,128)(2,1)S(1)}, u32[]{:S(2)}, u32[]{:S(2)}) collective-permute-start(bf16[128,2048]{1,0:T(8,128)(2,1)S(1)} %collective-permute-done.13), channel_id=1, source_target_pairs={{16,24},{20,28},{8,0},{12,4},{17,25},{21,29},{9,1},{13,5},{18,26},... | collective-permute-start | bytes 1572872 | tf_op jit(solution)/shard_map/ppermute | solution.py:23
  77.5 1.6 %collective-permute-start.20 = (bf16[128,1024]{1,0:T(8,128)(2,1)S(1)}, bf16[128,1024]{1,0:T(8,128)(2,1)S(1)}, u32[]{:S(2)}, u32[]{:S(2)}) collective-permute-start(bf16[128,1024]{1,0:T(8,128)(2,1)S(1)} %multiply_convert_fusion), channel_id=1, source_target_pairs={{0,2},{1,3},{2,0},{3,1},{4,6},{5,7},{6,4},{7,5},{8,10},{9,11},{10,... | collective-permute-start | bytes 786440 | tf_op jit(solution)/shard_map/ppermute | solution.py:19
  80.0 3.9 %collective-permute-done.20 = bf16[128,1024]{1,0:T(8,128)(2,1)S(1)} collective-permute-done((bf16[128,1024]{1,0:T(8,128)(2,1)S(1)}, bf16[128,1024]{1,0:T(8,128)(2,1)S(1)}, u32[]{:S(2)}, u32[]{:S(2)}) %collective-permute-start.20) | collective-permute-done | bytes 262176 | tf_op jit(solution)/shard_map/ppermute | solution.py:19
  83.9 1.5 %collective-permute-start.22 = (bf16[128,1024]{1,0:T(8,128)(2,1)S(1)}, bf16[128,1024]{1,0:T(8,128)(2,1)S(1)}, u32[]{:S(2)}, u32[]{:S(2)}) collective-permute-start(bf16[128,1024]{1,0:T(8,128)(2,1)S(1)} %multiply_convert_fusion), channel_id=1, source_target_pairs={{0,1},{1,0},{2,3},{3,2},{4,5},{5,4},{6,7},{7,6},{8,9},{9,8},{10,11... | collective-permute-start | bytes 786440 | tf_op jit(solution)/shard_map/ppermute | solution.py:19
  86.0 4.3 %collective-permute-done.22 = bf16[128,1024]{1,0:T(8,128)(2,1)S(1)} collective-permute-done((bf16[128,1024]{1,0:T(8,128)(2,1)S(1)}, bf16[128,1024]{1,0:T(8,128)(2,1)S(1)}, u32[]{:S(2)}, u32[]{:S(2)}) %collective-permute-start.22) | collective-permute-done | bytes 262176 | tf_op jit(solution)/shard_map/ppermute | solution.py:19
  90.8 1.6 %collective-permute-start.21 = (bf16[128,1152]{1,0:T(8,128)(2,1)S(1)}, bf16[128,1152]{1,0:T(8,128)(2,1)S(1)}, u32[]{:S(2)}, u32[]{:S(2)}) collective-permute-start(bf16[128,1152]{1,0:T(8,128)(2,1)S(1)} %convolution_convert_fusion.1), channel_id=1, source_target_pairs={{0,2},{1,3},{2,0},{3,1},{4,6},{5,7},{6,4},{7,5},{8,10},{9,11},{10,... | collective-permute-start | bytes 884744 | tf_op jit(solution)/shard_map/ppermute | solution.py:19
  92.3 1.5 %collective-permute-start.23 = (bf16[128,896]{1,0:T(8,128)(2,1)S(1)}, bf16[128,896]{1,0:T(8,128)(2,1)S(1)}, u32[]{:S(2)}, u32[]{:S(2)}) collective-permute-start(bf16[128,896]{1,0:T(8,128)(2,1)S(1)} %fusion.7), channel_id=1, source_target_pairs={{0,1},{1,0},{2,3},{3,2},{4,5},{5,4},{6,7},{7,6},{8,9},{9,8},{10,11... | collective-permute-start | bytes 688136 | tf_op jit(solution)/shard_map/ppermute | solution.py:19
  94.3 1.5 %collective-permute-done.19 = bf16[128,2048]{1,0:T(8,128)(2,1)S(1)} collective-permute-done((bf16[128,2048]{1,0:T(8,128)(2,1)S(1)}, bf16[128,2048]{1,0:T(8,128)(2,1)S(1)}, u32[]{:S(2)}, u32[]{:S(2)}) %collective-permute-start.19) | collective-permute-done | bytes 524320 | tf_op jit(solution)/shard_map/ppermute | solution.py:23
  99.1 1.6 %collective-permute-done.21 = bf16[128,1152]{1,0:T(8,128)(2,1)S(1)} collective-permute-done((bf16[128,1152]{1,0:T(8,128)(2,1)S(1)}, bf16[128,1152]{1,0:T(8,128)(2,1)S(1)}, u32[]{:S(2)}, u32[]{:S(2)}) %collective-permute-start.21) | collective-permute-done | bytes 294944 | tf_op jit(solution)/shard_map/ppermute | solution.py:19
  100.8 5.8 %collective-permute-done.24 = bf16[128,1152]{1,0:T(8,128)(2,1)S(1)} collective-permute-done((bf16[128,1152]{1,0:T(8,128)(2,1)S(1)}, bf16[128,1152]{1,0:T(8,128)(2,1)S(1)}, u32[]{:S(2)}, u32[]{:S(2)}) %collective-permute-start.24) | collective-permute-done | bytes 294944 | tf_op jit(solution)/shard_map/ppermute | solution.py:19
  106.6 1.3 %copy-done.5 = bf16[128,8192]{1,0:T(8,128)(2,1)} copy-done((bf16[128,8192]{1,0:T(8,128)(2,1)}, bf16[128,8192]{1,0:T(8,128)(2,1)S(1)}, u32[]{:S(2)}) %copy-start.5) | copy-done | bytes 2097176
  (82 shorter events, 16.0 us)
Async XLA Ops:
  0.0 14.0 %copy-start.4 = (bf16[128,8192]{1,0:T(8,128)(2,1)S(1)}, bf16[128,8192]{1,0:T(8,128)(2,1)}, u32[]{:S(2)}) copy-start(bf16[128,8192]{1,0:T(8,128)(2,1)} %param.4) | copy-start | bytes 6291460
  2.7 39.7 %collective-permute-start.3 = (bf16[128,2048]{1,0:T(8,128)(2,1)}, bf16[128,2048]{1,0:T(8,128)(2,1)}, u32[]{:S(2)}, u32[]{:S(2)}) collective-permute-start(bf16[128,2048]{1,0:T(8,128)(2,1)} %get-tuple-element.15), channel_id=1, source_target_pairs={{0,3},{1,2},{2,1},{3,0},{4,7},{5,6},{6,5},{7,4},{8,11},{9,10},{10,... | collective-permute-start | bytes 1572872 | tf_op jit(solution)/shard_map/ppermute | solution.py:19
  6.6 44.9 %collective-permute-start.2 = (bf16[128,2048]{1,0:T(8,128)(2,1)}, bf16[128,2048]{1,0:T(8,128)(2,1)S(1)}, u32[]{:S(2)}, u32[]{:S(2)}) collective-permute-start(bf16[128,2048]{1,0:T(8,128)(2,1)} %get-tuple-element.13), channel_id=1, source_target_pairs={{0,2},{1,3},{2,0},{3,1},{4,6},{5,7},{6,4},{7,5},{8,10},{9,11},{10,... | collective-permute-start | bytes 1572872 | tf_op jit(solution)/shard_map/ppermute | solution.py:19
  8.9 16.3 %collective-permute-start.9 = (bf16[128,1152]{1,0:T(8,128)(2,1)}, bf16[128,1152]{1,0:T(8,128)(2,1)S(1)}, u32[]{:S(2)}, u32[]{:S(2)}) collective-permute-start(bf16[128,1152]{1,0:T(8,128)(2,1)} %constant_dynamic-slice_fusion), channel_id=1, source_target_pairs={{0,1},{1,0},{2,3},{3,2},{4,5},{5,4},{6,7},{7,6},{8,9},{9,8},{10,11... | collective-permute-start | bytes 884744 | tf_op jit(solution)/shard_map/ppermute | solution.py:19
  10.5 24.8 %collective-permute-start.10 = (bf16[128,896]{1,0:T(8,128)(2,1)}, bf16[128,896]{1,0:T(8,128)(2,1)}, u32[]{:S(2)}, u32[]{:S(2)}) collective-permute-start(bf16[128,896]{1,0:T(8,128)(2,1)} %dynamic-slice.1), channel_id=1, source_target_pairs={{0,2},{1,3},{2,0},{3,1},{4,6},{5,7},{6,4},{7,5},{8,10},{9,11},{10,... | collective-permute-start | bytes 688136 | tf_op jit(solution)/shard_map/ppermute | solution.py:19
  12.5 37.6 %collective-permute-start = (bf16[128,2048]{1,0:T(8,128)(2,1)}, bf16[128,2048]{1,0:T(8,128)(2,1)S(1)}, u32[]{:S(2)}, u32[]{:S(2)}) collective-permute-start(bf16[128,2048]{1,0:T(8,128)(2,1)} %get-tuple-element.14), channel_id=1, source_target_pairs={{0,1},{1,0},{2,3},{3,2},{4,5},{5,4},{6,7},{7,6},{8,9},{9,8},{10,11... | collective-permute-start | bytes 1572872 | tf_op jit(solution)/shard_map/ppermute | solution.py:19
  14.0 3.8 %copy-start = (bf16[2048,1024]{1,0:T(8,128)(2,1)S(1)}, bf16[2048,1024]{1,0:T(8,128)(2,1)}, u32[]{:S(2)}) copy-start(bf16[2048,1024]{1,0:T(8,128)(2,1)} %param.5) | copy-start | bytes 12582916
  36.3 11.8 %copy-start.2 = (bf16[2048,1024]{1,0:T(8,128)(2,1)S(1)}, bf16[2048,1024]{1,0:T(8,128)(2,1)}, u32[]{:S(2)}) copy-start(bf16[2048,1024]{1,0:T(8,128)(2,1)} %param.6) | copy-start | bytes 12582916
  36.3 29.3 %collective-permute-start.13 = (bf16[128,2048]{1,0:T(8,128)(2,1)S(1)}, bf16[128,2048]{1,0:T(8,128)(2,1)S(1)}, u32[]{:S(2)}, u32[]{:S(2)}) collective-permute-start(bf16[128,2048]{1,0:T(8,128)(2,1)S(1)} %constant_dynamic-update-slice_fusion.4), channel_id=1, source_target_pairs={{0,16},{4,20},{24,8},{28,12},{1,17},{5,21},{25,9},{29,13},{2,18},{... | collective-permute-start | bytes 1572872 | tf_op jit(solution)/shard_map/ppermute | solution.py:23
  41.1 26.1 %collective-permute-start.12 = (bf16[128,2048]{1,0:T(8,128)(2,1)S(1)}, bf16[128,2048]{1,0:T(8,128)(2,1)S(1)}, u32[]{:S(2)}, u32[]{:S(2)}) collective-permute-start(bf16[128,2048]{1,0:T(8,128)(2,1)S(1)} %constant_dynamic-update-slice_fusion.4), channel_id=1, source_target_pairs={{8,24},{12,28},{16,0},{20,4},{9,25},{13,29},{17,1},{21,5},{10,26},... | collective-permute-start | bytes 1572872 | tf_op jit(solution)/shard_map/ppermute | solution.py:23
  42.4 25.4 %collective-permute-start.11 = (bf16[128,2048]{1,0:T(8,128)(2,1)S(1)}, bf16[128,2048]{1,0:T(8,128)(2,1)S(1)}, u32[]{:S(2)}, u32[]{:S(2)}) collective-permute-start(bf16[128,2048]{1,0:T(8,128)(2,1)S(1)} %constant_dynamic-update-slice_fusion.4), channel_id=1, source_target_pairs={{0,8},{4,12},{8,0},{12,4},{16,24},{20,28},{24,16},{28,20},{1,9},{5... | collective-permute-start | bytes 1572872 | tf_op jit(solution)/shard_map/ppermute | solution.py:23
  50.1 40.7 %collective-permute-start.18 = (bf16[128,2048]{1,0:T(8,128)(2,1)S(1)}, bf16[128,2048]{1,0:T(8,128)(2,1)S(1)}, u32[]{:S(2)}, u32[]{:S(2)}) collective-permute-start(bf16[128,2048]{1,0:T(8,128)(2,1)S(1)} %constant_dynamic-update-slice_fusion.4), channel_id=1, source_target_pairs={{8,16},{12,20},{16,8},{20,12},{9,17},{13,21},{17,9},{21,13},{10,18... | collective-permute-start | bytes 1572872 | tf_op jit(solution)/shard_map/ppermute | solution.py:23
  51.6 6.4 %collective-permute-start.4 = (bf16[128,1024]{1,0:T(8,128)(2,1)S(1)}, bf16[128,1024]{1,0:T(8,128)(2,1)S(1)}, u32[]{:S(2)}, u32[]{:S(2)}) collective-permute-start(bf16[128,1024]{1,0:T(8,128)(2,1)S(1)} %convolution_convert_fusion.6), channel_id=1, source_target_pairs={{0,1},{1,0},{2,3},{3,2},{4,5},{5,4},{6,7},{7,6},{8,9},{9,8},{10,11... | collective-permute-start | bytes 786440 | tf_op jit(solution)/shard_map/ppermute | solution.py:19
  58.0 6.4 %collective-permute-start.7 = (bf16[128,1024]{1,0:T(8,128)(2,1)S(1)}, bf16[128,1024]{1,0:T(8,128)(2,1)S(1)}, u32[]{:S(2)}, u32[]{:S(2)}) collective-permute-start(bf16[128,1024]{1,0:T(8,128)(2,1)S(1)} %convolution_convert_fusion.4), channel_id=1, source_target_pairs={{0,2},{1,3},{2,0},{3,1},{4,6},{5,7},{6,4},{7,5},{8,10},{9,11},{10,... | collective-permute-start | bytes 786440 | tf_op jit(solution)/shard_map/ppermute | solution.py:19
  64.4 8.7 %collective-permute-start.1 = (bf16[128,1024]{1,0:T(8,128)(2,1)S(1)}, bf16[128,1024]{1,0:T(8,128)(2,1)S(1)}, u32[]{:S(2)}, u32[]{:S(2)}) collective-permute-start(bf16[128,1024]{1,0:T(8,128)(2,1)S(1)} %convolution_convert_fusion.7), channel_id=1, source_target_pairs={{0,1},{1,0},{2,3},{3,2},{4,5},{5,4},{6,7},{7,6},{8,9},{9,8},{10,11... | collective-permute-start | bytes 786440 | tf_op jit(solution)/shard_map/ppermute | solution.py:19
  65.6 7.4 %collective-permute-start.6 = (bf16[128,1024]{1,0:T(8,128)(2,1)S(1)}, bf16[128,1024]{1,0:T(8,128)(2,1)S(1)}, u32[]{:S(2)}, u32[]{:S(2)}) collective-permute-start(bf16[128,1024]{1,0:T(8,128)(2,1)S(1)} %convolution_convert_fusion.5), channel_id=1, source_target_pairs={{0,2},{1,3},{2,0},{3,1},{4,6},{5,7},{6,4},{7,5},{8,10},{9,11},{10,... | collective-permute-start | bytes 786440 | tf_op jit(solution)/shard_map/ppermute | solution.py:19
  67.2 8.5 %collective-permute-start.5 = (bf16[128,1024]{1,0:T(8,128)(2,1)S(1)}, bf16[128,1024]{1,0:T(8,128)(2,1)S(1)}, u32[]{:S(2)}, u32[]{:S(2)}) collective-permute-start(bf16[128,1024]{1,0:T(8,128)(2,1)S(1)} %fusion.5), channel_id=1, source_target_pairs={{0,2},{1,3},{2,0},{3,1},{4,6},{5,7},{6,4},{7,5},{8,10},{9,11},{10,... | collective-permute-start | bytes 786440 | tf_op jit(solution)/shard_map/ppermute | solution.py:19
  67.8 9.3 %collective-permute-start.8 = (bf16[128,1024]{1,0:T(8,128)(2,1)S(1)}, bf16[128,1024]{1,0:T(8,128)(2,1)S(1)}, u32[]{:S(2)}, u32[]{:S(2)}) collective-permute-start(bf16[128,1024]{1,0:T(8,128)(2,1)S(1)} %fusion.6), channel_id=1, source_target_pairs={{0,1},{1,0},{2,3},{3,2},{4,5},{5,4},{6,7},{7,6},{8,9},{9,8},{10,11... | collective-permute-start | bytes 786440 | tf_op jit(solution)/shard_map/ppermute | solution.py:19
  69.6 7.6 %copy-start.6 = (f32[128,1024]{1,0:T(8,128)S(1)}, f32[128,1024]{1,0:T(8,128)}, u32[]{:S(2)}) copy-start(f32[128,1024]{1,0:T(8,128)} %fusion.11) | copy-start | bytes 1572868
  69.6 7.6 %copy-start.7 = (f32[128,1024]{1,0:T(8,128)S(1)}, f32[128,1024]{1,0:T(8,128)}, u32[]{:S(2)}) copy-start(f32[128,1024]{1,0:T(8,128)} %fusion.13) | copy-start | bytes 1572868
  69.9 9.3 %copy-start.3 = (bf16[1024,2048]{1,0:T(8,128)(2,1)S(1)}, bf16[1024,2048]{1,0:T(8,128)(2,1)}, u32[]{:S(2)}) copy-start(bf16[1024,2048]{1,0:T(8,128)(2,1)} %param.7) | copy-start | bytes 12582916
  73.1 20.8 %collective-permute-start.14 = (bf16[128,2048]{1,0:T(8,128)(2,1)S(1)}, bf16[128,2048]{1,0:T(8,128)(2,1)S(1)}, u32[]{:S(2)}, u32[]{:S(2)}) collective-permute-start(bf16[128,2048]{1,0:T(8,128)(2,1)S(1)} %constant_dynamic-update-slice_fusion.4), channel_id=1, source_target_pairs={{0,4},{4,0},{8,12},{12,8},{16,20},{20,16},{24,28},{28,24},{1,5},{5... | collective-permute-start | bytes 1572872 | tf_op jit(solution)/shard_map/ppermute | solution.py:23
  73.1 21.0 %collective-permute-start.15 = (bf16[128,2048]{1,0:T(8,128)(2,1)S(1)}, bf16[128,2048]{1,0:T(8,128)(2,1)S(1)}, u32[]{:S(2)}, u32[]{:S(2)}) collective-permute-start(bf16[128,2048]{1,0:T(8,128)(2,1)S(1)} %collective-permute-done.11), channel_id=1, source_target_pairs={{0,4},{4,0},{8,12},{12,8},{16,20},{20,16},{24,28},{28,24},{1,5},{5... | collective-permute-start | bytes 1572872 | tf_op jit(solution)/shard_map/ppermute | solution.py:23
  75.7 16.6 %collective-permute-start.17 = (bf16[128,2048]{1,0:T(8,128)(2,1)S(1)}, bf16[128,2048]{1,0:T(8,128)(2,1)S(1)}, u32[]{:S(2)}, u32[]{:S(2)}) collective-permute-start(bf16[128,2048]{1,0:T(8,128)(2,1)S(1)} %collective-permute-done.13), channel_id=1, source_target_pairs={{16,24},{20,28},{8,0},{12,4},{17,25},{21,29},{9,1},{13,5},{18,26},... | collective-permute-start | bytes 1572872 | tf_op jit(solution)/shard_map/ppermute | solution.py:23
  77.5 6.4 %collective-permute-start.20 = (bf16[128,1024]{1,0:T(8,128)(2,1)S(1)}, bf16[128,1024]{1,0:T(8,128)(2,1)S(1)}, u32[]{:S(2)}, u32[]{:S(2)}) collective-permute-start(bf16[128,1024]{1,0:T(8,128)(2,1)S(1)} %multiply_convert_fusion), channel_id=1, source_target_pairs={{0,2},{1,3},{2,0},{3,1},{4,6},{5,7},{6,4},{7,5},{8,10},{9,11},{10,... | collective-permute-start | bytes 786440 | tf_op jit(solution)/shard_map/ppermute | solution.py:19
  83.9 6.4 %collective-permute-start.22 = (bf16[128,1024]{1,0:T(8,128)(2,1)S(1)}, bf16[128,1024]{1,0:T(8,128)(2,1)S(1)}, u32[]{:S(2)}, u32[]{:S(2)}) collective-permute-start(bf16[128,1024]{1,0:T(8,128)(2,1)S(1)} %multiply_convert_fusion), channel_id=1, source_target_pairs={{0,1},{1,0},{2,3},{3,2},{4,5},{5,4},{6,7},{7,6},{8,9},{9,8},{10,11... | collective-permute-start | bytes 786440 | tf_op jit(solution)/shard_map/ppermute | solution.py:19
  90.3 3.9 %collective-permute-start.16 = (bf16[128,2048]{1,0:T(8,128)(2,1)S(1)}, bf16[128,2048]{1,0:T(8,128)(2,1)S(1)}, u32[]{:S(2)}, u32[]{:S(2)}) collective-permute-start(bf16[128,2048]{1,0:T(8,128)(2,1)S(1)} %broadcast_select_fusion.1), channel_id=1, source_target_pairs={{0,4},{4,0},{8,12},{12,8},{16,20},{20,16},{24,28},{28,24},{1,5},{5... | collective-permute-start | bytes 1572872 | tf_op jit(solution)/shard_map/ppermute | solution.py:23
  90.8 9.9 %collective-permute-start.21 = (bf16[128,1152]{1,0:T(8,128)(2,1)S(1)}, bf16[128,1152]{1,0:T(8,128)(2,1)S(1)}, u32[]{:S(2)}, u32[]{:S(2)}) collective-permute-start(bf16[128,1152]{1,0:T(8,128)(2,1)S(1)} %convolution_convert_fusion.1), channel_id=1, source_target_pairs={{0,2},{1,3},{2,0},{3,1},{4,6},{5,7},{6,4},{7,5},{8,10},{9,11},{10,... | collective-permute-start | bytes 884744 | tf_op jit(solution)/shard_map/ppermute | solution.py:19
  92.3 8.4 %collective-permute-start.23 = (bf16[128,896]{1,0:T(8,128)(2,1)S(1)}, bf16[128,896]{1,0:T(8,128)(2,1)S(1)}, u32[]{:S(2)}, u32[]{:S(2)}) collective-permute-start(bf16[128,896]{1,0:T(8,128)(2,1)S(1)} %fusion.7), channel_id=1, source_target_pairs={{0,1},{1,0},{2,3},{3,2},{4,5},{5,4},{6,7},{7,6},{8,9},{9,8},{10,11... | collective-permute-start | bytes 688136 | tf_op jit(solution)/shard_map/ppermute | solution.py:19
  93.9 2.0 %collective-permute-start.19 = (bf16[128,2048]{1,0:T(8,128)(2,1)S(1)}, bf16[128,2048]{1,0:T(8,128)(2,1)S(1)}, u32[]{:S(2)}, u32[]{:S(2)}) collective-permute-start(bf16[128,2048]{1,0:T(8,128)(2,1)S(1)} %broadcast_select_fusion), channel_id=1, source_target_pairs={{0,4},{4,0},{8,12},{12,8},{16,20},{20,16},{24,28},{28,24},{1,5},{5... | collective-permute-start | bytes 1572872 | tf_op jit(solution)/shard_map/ppermute | solution.py:23
  97.0 9.6 %collective-permute-start.24 = (bf16[128,1152]{1,0:T(8,128)(2,1)S(1)}, bf16[128,1152]{1,0:T(8,128)(2,1)S(1)}, u32[]{:S(2)}, u32[]{:S(2)}) collective-permute-start(bf16[128,1152]{1,0:T(8,128)(2,1)S(1)} %convolution_convert_fusion), channel_id=1, source_target_pairs={{0,2},{1,3},{2,0},{3,1},{4,6},{5,7},{6,4},{7,5},{8,10},{9,11},{10,... | collective-permute-start | bytes 884744 | tf_op jit(solution)/shard_map/ppermute | solution.py:19
  98.1 8.5 %collective-permute-start.25 = (bf16[128,896]{1,0:T(8,128)(2,1)S(1)}, bf16[128,896]{1,0:T(8,128)(2,1)S(1)}, u32[]{:S(2)}, u32[]{:S(2)}) collective-permute-start(bf16[128,896]{1,0:T(8,128)(2,1)S(1)} %convolution_convert_fusion.8), channel_id=1, source_target_pairs={{0,1},{1,0},{2,3},{3,2},{4,5},{5,4},{6,7},{7,6},{8,9},{9,8},{10,11... | collective-permute-start | bytes 688136 | tf_op jit(solution)/shard_map/ppermute | solution.py:19
  (2 other events, 4.0 us)

commit v4 on v2

--- a/solution.py
+++ b/solution.py
@@ -18,6 +18,19 @@
         ]
         return lax.ppermute(x, ("row", "col"), pairs)
 
+    turned = cores == 2 and rows == cols
+    line = turned and chips == 4
+
+    def send_turned(x, step):
+        pairs = []
+        for d in range(dp):
+            dr, dc = (step, 0) if d % cores else (0, step)
+            for r in range(rows):
+                for c in range(cols):
+                    to = (d * rows + (r + dr) % rows) * cols + (c + dc) % cols
+                    pairs.append(((d * rows + r) * cols + c, to))
+        return lax.ppermute(x, ("dp", "row", "col"), pairs)
+
     def send_dp(x, chip_pairs, core_shift):
         pairs = [(z * cores + k, to * cores + (k + core_shift) % cores) for z, to in chip_pairs for k in range(cores)]
         return lax.ppermute(x, "dp", pairs)
@@ -37,21 +50,23 @@
         slab = w_gate.shape[0]
         hidden_width, width = w_down.shape
         half = width // 2
-        share = hidden_width // dp
 
         def place(shift):
             return (r + shift[0]) % rows * cols + (c + shift[1]) % cols
 
-        piece = lax.dynamic_slice_in_dim(w_down, d * share, share, axis=0)
         sides = [(0, dc) for dc in range(1, cols)] + [(dr, 0) for dr in range(1, rows)]
-        held = jnp.concatenate([send(piece[:, half:] if s[0] else piece[:, :half], back(s)) for s in sides], axis=0)
+        if turned:
+            share = hidden_width // chips
+            piece = lax.dynamic_slice(w_down, (chip * share, core * half), (share, half))
+            parts_of = [piece[: share // 2], piece[share // 2 :]]
+            held = jnp.concatenate([send_turned(x, -i) for i in range(1, rows) for x in parts_of], axis=0)
 
         feats = {s: lax.dynamic_slice_in_dim(tokens, place(s) * slab, slab, axis=1) for s in shifts}
         got = {s: send(feats[s], s) for s in away}
         got[0, 0] = feats[0, 0]
 
         early, late = [], []
-        if chips == 4:
+        if line:
             two_a = send_dp(held, [(0, 2), (3, 1)], 0)
             two_b = send_dp(held, [(1, 3), (2, 0)], 0)
             one = send_dp(held, [(z, z ^ 1) for z in range(chips)], 0)
@@ -59,8 +74,9 @@
             relayed = send_dp(two_a, [(2, 3), (1, 0)], 0)
             outer = (chip == 0) | (chip == chips - 1)
             two = jnp.where(outer, two_b, two_a)
-            early += [(one, chip ^ 1), (two, chip ^ 2)]
-        else:
+            early += [(held, chip), (one, chip ^ 1), (two, chip ^ 2)]
+        elif turned:
+            early.append((held, chip))
             for z in range(1, chips):
                 turn = send_dp(held, [(i, (i + z) % chips) for i in range(chips)], 0)
                 late.append((turn, (chip - z) % chips))
@@ -71,7 +87,9 @@
             def shift(a, b):
                 return (b, a) if col_first else (a, b)
 
-            parts = {s: matmul(got[s], weight) for s in away}
+            parts = {}
+            for s in away:
+                parts[s] = matmul(got[s], weight)
             parts[0, 0] = matmul(got[0, 0], weight)
             sums = {b: parts[shift(0, b)] for b in range(second)}
             for b in reversed(range(second)):
@@ -88,25 +106,26 @@
         up, up_passed = crossed(w_up, False)
         hidden = (jax.nn.silu(gate) * up).astype(jnp.bfloat16)
 
-        if chips == 4:
+        if line:
             late.append((jnp.where(outer, relayed, middle), chip ^ 3))
+        if turned:
+            far = {s: jnp.zeros((hidden_width, half), jnp.bfloat16) for s in sides}
 
-        far = {s: jnp.zeros((hidden_width, half), jnp.bfloat16) for s in sides}
+            def fill(pieces):
+                for block, from_chip in pieces:
+                    other = swap(block, 1)
+                    for s in sides:
+                        moved = jnp.where(core == (1 if s[0] else 0), block, other)
+                        lower = (sum(s) - 1) * share
+                        moved = moved[lower : lower + share]
+                        far[s] = lax.dynamic_update_slice_in_dim(far[s], moved, from_chip * share, axis=0)
 
-        def fill(pieces):
-            for k in range(cores):
-                for block, from_chip in pieces:
-                    moved = swap(block, k) if k else block
-                    at = (from_chip * cores + (core - k) % cores) * share
-                    for i, s in enumerate(sides):
-                        far[s] = lax.dynamic_update_slice_in_dim(far[s], moved[i * share : (i + 1) * share], at, axis=0)
-
-        fill([(held, chip)])
-        tied, _ = lax.optimization_barrier(([p for p, _ in early], gate_passed + up_passed))
-        fill([(p, at) for p, (_, at) in zip(tied, early)])
-
-        tied, _ = lax.optimization_barrier(([p for p, _ in late], hidden))
-        fill([(p, at) for p, (_, at) in zip(tied, late)])
+            tied, _ = lax.optimization_barrier(([p for p, _ in early], gate_passed + up_passed))
+            fill([(p, at) for p, (_, at) in zip(tied, early)])
+            tied, _ = lax.optimization_barrier(([p for p, _ in late], hidden))
+            fill([(p, at) for p, (_, at) in zip(tied, late)])
+        else:
+            far = {s: send(w_down[:, half:] if s[0] else w_down[:, :half], back(s)) for s in sides}
         near = {s: send(hidden, back(s)) for s in reversed(sides)}
         landed = [(matmul(hidden, w_down).astype(jnp.bfloat16), place((0, 0)) * width)]
         outs = []

time: 106 us -> 99.4 us (0.938)
  waiting for transfers between devices: 49.7 us -> 40.7 us
  matrix products: 15.4 us -> 16.8 us
  other arithmetic: 0.4 us -> 1.76 us
  starting transfers between devices: 30.3 us -> 31.5 us
  local copies, waits for them, and re-layouts: 9.06 us -> 7.93 us
    ppermute x9, waiting for transfers between devices: 23.2 us -> 11.9 us  [send_dp(): return lax.ppermute(x, 'dp', pairs)]
    ppermute x0 -> x2, waiting for transfers between devices: none -> 7.2 us  [send_turned(): return lax.ppermute(x, ('dp', 'row', 'col'), pairs)]
    ppermute x17 -> x15, waiting for transfers between devices: 26.4 us -> 21.6 us  [send(): return lax.ppermute(x, ('row', 'col'), pairs)]
    ppermute x0 -> x2, starting transfers between devices: none -> 3.02 us  [send_turned(): return lax.ppermute(x, ('dp', 'row', 'col'), pairs)]
    ppermute x17 -> x15, starting transfers between devices: 20.6 us -> 18.4 us  [send(): return lax.ppermute(x, ('row', 'col'), pairs)]
    dot_general x15, matrix products: 15.4 us -> 16.8 us  [matmul(): return jnp.dot(a, b, preferred_element_type=jnp.float32)]
    dynamic_update_slice x0 -> x5, other arithmetic: none -> 1.35 us  [fill(): lax.dynamic_update_slice_in_dim(far[s], moved, from_chip * share, axis=0)]
    dynamic_update_slice x8 -> x0, local copies, waits for them, and re-layouts: 1.33 us -> none  [fill(): lax.dynamic_update_slice_in_dim(far[s], moved[i * share:(i + 1) * share],...]
  transfers between devices with their start and end apart: 26 -> 26, of which waited for: 11 -> 10; matrix products, arithmetic and copies ran while one was open for 21% -> 24% of each run, Pallas kernels for 0% -> 0%
where the time goes in v4:
time: 99.4 us; the launch traced here: 99.1 us
  waiting for transfers between devices  40.7 us (41%)
  starting transfers between devices  31.5 us (32%)
  matrix products  16.8 us (17%)
  local copies, waits for them, and re-layouts  7.93 us (8%)
  other arithmetic  1.76 us (2%)
    ppermute x15, waiting for transfers between devices, send(): return lax.ppermute(x, ('row', 'col'), pairs)  21.6 us
    ppermute x15, starting transfers between devices, send(): return lax.ppermute(x, ('row', 'col'), pairs)  18.4 us
    dot_general x15, matrix products, matmul(): return jnp.dot(a, b, preferred_element_type=jnp.float32)  16.8 us
    ppermute x9, waiting for transfers between devices, send_dp(): return lax.ppermute(x, 'dp', pairs)  11.9 us
    ppermute x9, starting transfers between devices, send_dp(): return lax.ppermute(x, 'dp', pairs)  10 us
    ppermute x2, waiting for transfers between devices, send_turned(): return lax.ppermute(x, ('dp', 'row', 'col'), pairs)  7.2 us
    ppermute x2, starting transfers between devices, send_turned(): return lax.ppermute(x, ('dp', 'row', 'col'), pairs)  3.02 us
    dynamic_slice x1, local copies, waits for them, and re-layouts, shards(): lax.dynamic_slice_in_dim(tokens, place(s) * slab, slab, axis=1)  2.55 us
  transfers between devices with their start and end apart: 26, of which 10 were waited for; matrix products, arithmetic and copies ran while one was open for 24% of the time, Pallas kernels for 0%

profile of v4, /device:TPU:0, one launch (start us, length us, event | category | flops | bytes accessed | tf_op | source)
XLA Modules:
  0.0 99.1 jit_solution(15961983117823582600)
XLA Ops:
  0.0 1.9 %fusion.21 = (bf16[128,1024]{1,0:T(8,128)(2,1)S(1)}, bf16[128,1024]{1,0:T(8,128)(2,1)}) fusion(bf16[1024,2048]{1,0:T(8,128)(2,1)} %param.7, s32[]{:T(128)S(6)} %add.206, s32[]{:T(128)S(6)} %select_n.174, s32[]{:T(128)S(6)} %select_n.173), kind=kLoop, calls=%fused_computation.48 | loop fusion | bytes 1048588 | tf_op jit(solution)/shard_map/slice | solution.py:61
  1.9 3.0 %collective-permute-start.9 = (bf16[128,1024]{1,0:T(8,128)(2,1)}, bf16[128,1024]{1,0:T(8,128)(2,1)}, u32[]{:S(2)}, u32[]{:S(2)}) collective-permute-start(bf16[128,1024]{1,0:T(8,128)(2,1)} %get-tuple-element.14), channel_id=1, source_target_pairs={{0,1},{1,0},{2,3},{3,2},{4,6},{5,7},{6,4},{7,5},{8,9},{9,8},{10,11... | collective-permute-start | bytes 786440 | tf_op jit(solution)/shard_map/ppermute | solution.py:32
  4.9 2.6 %constant_dynamic-slice_fusion.1 = (bf16[128,2048]{1,0:T(8,128)(2,1)}, bf16[128,2048]{1,0:T(8,128)(2,1)}, bf16[128,2048]{1,0:T(8,128)(2,1)}) fusion(bf16[128,8192]{1,0:T(8,128)(2,1)} %param.4, s32[]{:T(128)S(6)} %select_n.168, s32[]{:T(128)S(6)} %select_n.166, s32[]{:T(128)S(6)} %select_n.169), kind=kLoop, calls=%fused_computation.45 | loop fusion | bytes 3145740 | tf_op jit(solution)/shard_map/dynamic_slice | solution.py:64
  7.5 2.9 %collective-permute-start.3 = (bf16[128,2048]{1,0:T(8,128)(2,1)}, bf16[128,2048]{1,0:T(8,128)(2,1)}, u32[]{:S(2)}, u32[]{:S(2)}) collective-permute-start(bf16[128,2048]{1,0:T(8,128)(2,1)} %get-tuple-element.17), channel_id=1, source_target_pairs={{0,3},{1,2},{2,1},{3,0},{4,7},{5,6},{6,5},{7,4},{8,11},{9,10},{10,... | collective-permute-start | bytes 1572872 | tf_op jit(solution)/shard_map/ppermute | solution.py:19
  11.0 3.9 %fusion.15 = f32[128,1024]{1,0:T(8,128)} fusion(bf16[2048,1024]{1,0:T(8,128)(2,1)} %param.6, bf16[128,8192]{1,0:T(8,128)(2,1)S(1)} %copy-done.4, s32[]{:T(128)S(6)} %select_n.164), kind=kOutput, calls=%fused_computation.33 | convolution fusion | flops 536870912 | bytes 5242884 | tf_op jit(solution)/shard_map/dot_general | solution.py:45
  14.8 1.6 %fusion.17 = f32[128,1024]{1,0:T(8,128)} fusion(bf16[2048,1024]{1,0:T(8,128)(2,1)S(1)} %copy-done, bf16[128,8192]{1,0:T(8,128)(2,1)S(1)} %copy-done.4, s32[]{:T(128)S(6)} %select_n.164), kind=kOutput, calls=%fused_computation.35 | convolution fusion | flops 536870912 | bytes 5242884 | tf_op jit(solution)/shard_map/dot_general | solution.py:45
  16.4 1.0 constant_dynamic-update-slice_fusion.1
  17.4 7.2 %collective-permute-done.10 = bf16[128,1024]{1,0:T(8,128)(2,1)} collective-permute-done((bf16[128,1024]{1,0:T(8,128)(2,1)S(1)}, bf16[128,1024]{1,0:T(8,128)(2,1)}, u32[]{:S(2)}, u32[]{:S(2)}) %collective-permute-start.10) | collective-permute-done | bytes 262176 | tf_op jit(solution)/shard_map/ppermute | solution.py:32
  24.6 1.0 constant_dynamic-update-slice_fusion
  25.6 1.6 %collective-permute-start.12 = (bf16[256,1024]{1,0:T(8,128)(2,1)S(1)}, bf16[256,1024]{1,0:T(8,128)(2,1)S(1)}, u32[]{:S(2)}, u32[]{:S(2)}) collective-permute-start(bf16[256,1024]{1,0:T(8,128)(2,1)S(1)} %constant_dynamic-update-slice_fusion), channel_id=1, source_target_pairs={{8,24},{12,28},{16,0},{20,4},{9,25},{13,29},{17,1},{21,5},{10,26},... | collective-permute-start | bytes 1572872 | tf_op jit(solution)/shard_map/ppermute | solution.py:36
  27.1 5.5 %collective-permute-start.13 = (bf16[256,1024]{1,0:T(8,128)(2,1)S(1)}, bf16[256,1024]{1,0:T(8,128)(2,1)S(1)}, u32[]{:S(2)}, u32[]{:S(2)}) collective-permute-start(bf16[256,1024]{1,0:T(8,128)(2,1)S(1)} %constant_dynamic-update-slice_fusion), channel_id=1, source_target_pairs={{0,16},{4,20},{24,8},{28,12},{1,17},{5,21},{25,9},{29,13},{2,18},{... | collective-permute-start | bytes 1572872 | tf_op jit(solution)/shard_map/ppermute | solution.py:36
  33.2 3.1 %convolution_convert_fusion.7 = bf16[128,1024]{1,0:T(8,128)(2,1)S(1)} fusion(bf16[128,2048]{1,0:T(8,128)(2,1)} %collective-permute-done.3, bf16[2048,1024]{1,0:T(8,128)(2,1)} %param.5), kind=kOutput, calls=%fused_computation.20 | convolution fusion | flops 537001984 | bytes 4980736 | tf_op jit(solution)/shard_map/dot_general | solution.py:45
  36.3 1.9 %convolution_convert_fusion.5 = bf16[128,1024]{1,0:T(8,128)(2,1)S(1)} fusion(bf16[128,2048]{1,0:T(8,128)(2,1)} %collective-permute-done.3, bf16[2048,1024]{1,0:T(8,128)(2,1)S(1)} %copy-done.2), kind=kOutput, calls=%fused_computation.18 | convolution fusion | flops 537001984 | bytes 4980736 | tf_op jit(solution)/shard_map/dot_general | solution.py:45
  38.2 2.6 %collective-permute-start.4 = (bf16[128,1024]{1,0:T(8,128)(2,1)S(1)}, bf16[128,1024]{1,0:T(8,128)(2,1)S(1)}, u32[]{:S(2)}, u32[]{:S(2)}) collective-permute-start(bf16[128,1024]{1,0:T(8,128)(2,1)S(1)} %convolution_convert_fusion.7), channel_id=1, source_target_pairs={{0,1},{1,0},{2,3},{3,2},{4,5},{5,4},{6,7},{7,6},{8,9},{9,8},{10,11... | collective-permute-start | bytes 786440 | tf_op jit(solution)/shard_map/ppermute | solution.py:19
  41.6 1.6 %collective-permute-start.7 = (bf16[128,1024]{1,0:T(8,128)(2,1)S(1)}, bf16[128,1024]{1,0:T(8,128)(2,1)S(1)}, u32[]{:S(2)}, u32[]{:S(2)}) collective-permute-start(bf16[128,1024]{1,0:T(8,128)(2,1)S(1)} %convolution_convert_fusion.5), channel_id=1, source_target_pairs={{0,2},{1,3},{2,0},{3,1},{4,6},{5,7},{6,4},{7,5},{8,10},{9,11},{10,... | collective-permute-start | bytes 786440 | tf_op jit(solution)/shard_map/ppermute | solution.py:19
  43.9 3.8 %collective-permute-done.4 = bf16[128,1024]{1,0:T(8,128)(2,1)S(1)} collective-permute-done((bf16[128,1024]{1,0:T(8,128)(2,1)S(1)}, bf16[128,1024]{1,0:T(8,128)(2,1)S(1)}, u32[]{:S(2)}, u32[]{:S(2)}) %collective-permute-start.4) | collective-permute-done | bytes 262176 | tf_op jit(solution)/shard_map/ppermute | solution.py:19
  47.7 2.3 %collective-permute-start.1 = (bf16[128,1024]{1,0:T(8,128)(2,1)S(1)}, bf16[128,1024]{1,0:T(8,128)(2,1)S(1)}, u32[]{:S(2)}, u32[]{:S(2)}) collective-permute-start(bf16[128,1024]{1,0:T(8,128)(2,1)S(1)} %convolution_convert_fusion.8), channel_id=1, source_target_pairs={{0,1},{1,0},{2,3},{3,2},{4,5},{5,4},{6,7},{7,6},{8,9},{9,8},{10,11... | collective-permute-start | bytes 786440 | tf_op jit(solution)/shard_map/ppermute | solution.py:19
  50.0 0.7 fusion.13
  50.8 1.5 %collective-permute-start.6 = (bf16[128,1024]{1,0:T(8,128)(2,1)S(1)}, bf16[128,1024]{1,0:T(8,128)(2,1)S(1)}, u32[]{:S(2)}, u32[]{:S(2)}) collective-permute-start(bf16[128,1024]{1,0:T(8,128)(2,1)S(1)} %convolution_convert_fusion.6), channel_id=1, source_target_pairs={{0,2},{1,3},{2,0},{3,1},{4,6},{5,7},{6,4},{7,5},{8,10},{9,11},{10,... | collective-permute-start | bytes 786440 | tf_op jit(solution)/shard_map/ppermute | solution.py:19
  52.3 0.7 fusion.14
  54.1 0.8 collective-permute-start.18
  55.0 2.2 %collective-permute-done.6 = bf16[128,1024]{1,0:T(8,128)(2,1)S(1)} collective-permute-done((bf16[128,1024]{1,0:T(8,128)(2,1)S(1)}, bf16[128,1024]{1,0:T(8,128)(2,1)S(1)}, u32[]{:S(2)}, u32[]{:S(2)}) %collective-permute-start.6) | collective-permute-done | bytes 262176 | tf_op jit(solution)/shard_map/ppermute | solution.py:19
  57.2 2.8 %collective-permute-done.5 = bf16[128,1024]{1,0:T(8,128)(2,1)S(1)} collective-permute-done((bf16[128,1024]{1,0:T(8,128)(2,1)S(1)}, bf16[128,1024]{1,0:T(8,128)(2,1)S(1)}, u32[]{:S(2)}, u32[]{:S(2)}) %collective-permute-start.5) | collective-permute-done | bytes 262176 | tf_op jit(solution)/shard_map/ppermute | solution.py:19
  60.1 1.5 %collective-permute-start.17 = (bf16[256,1024]{1,0:T(8,128)(2,1)S(1)}, bf16[256,1024]{1,0:T(8,128)(2,1)S(1)}, u32[]{:S(2)}, u32[]{:S(2)}) collective-permute-start(bf16[256,1024]{1,0:T(8,128)(2,1)S(1)} %collective-permute-done.13), channel_id=1, source_target_pairs={{16,24},{20,28},{8,0},{12,4},{17,25},{21,29},{9,1},{13,5},{18,26},... | collective-permute-start | bytes 1572872 | tf_op jit(solution)/shard_map/ppermute | solution.py:36
  62.8 1.6 %collective-permute-start.20 = (bf16[128,1024]{1,0:T(8,128)(2,1)S(1)}, bf16[128,1024]{1,0:T(8,128)(2,1)S(1)}, u32[]{:S(2)}, u32[]{:S(2)}) collective-permute-start(bf16[128,1024]{1,0:T(8,128)(2,1)S(1)} %multiply_convert_fusion), channel_id=1, source_target_pairs={{0,2},{1,3},{2,0},{3,1},{4,6},{5,7},{6,4},{7,5},{8,10},{9,11},{10,... | collective-permute-start | bytes 786440 | tf_op jit(solution)/shard_map/ppermute | solution.py:19
  64.4 11.9 %collective-permute-done.17 = bf16[256,1024]{1,0:T(8,128)(2,1)S(1)} collective-permute-done((bf16[256,1024]{1,0:T(8,128)(2,1)S(1)}, bf16[256,1024]{1,0:T(8,128)(2,1)S(1)}, u32[]{:S(2)}, u32[]{:S(2)}) %collective-permute-start.17) | collective-permute-done | bytes 524320 | tf_op jit(solution)/shard_map/ppermute | solution.py:36
  77.2 6.9 %collective-permute-done.22 = bf16[128,1024]{1,0:T(8,128)(2,1)S(1)} collective-permute-done((bf16[128,1024]{1,0:T(8,128)(2,1)S(1)}, bf16[128,1024]{1,0:T(8,128)(2,1)S(1)}, u32[]{:S(2)}, u32[]{:S(2)}) %collective-permute-start.22) | collective-permute-done | bytes 262176 | tf_op jit(solution)/shard_map/ppermute | solution.py:19
  84.1 1.5 %collective-permute-start.21 = (bf16[128,1024]{1,0:T(8,128)(2,1)S(1)}, bf16[128,1024]{1,0:T(8,128)(2,1)S(1)}, u32[]{:S(2)}, u32[]{:S(2)}) collective-permute-start(bf16[128,1024]{1,0:T(8,128)(2,1)S(1)} %fusion.5), channel_id=1, source_target_pairs={{0,2},{1,3},{2,0},{3,1},{4,6},{5,7},{6,4},{7,5},{8,10},{9,11},{10,... | collective-permute-start | bytes 786440 | tf_op jit(solution)/shard_map/ppermute | solution.py:19
  90.3 1.8 %collective-permute-start.25 = (bf16[128,1024]{1,0:T(8,128)(2,1)S(1)}, bf16[128,1024]{1,0:T(8,128)(2,1)S(1)}, u32[]{:S(2)}, u32[]{:S(2)}) collective-permute-start(bf16[128,1024]{1,0:T(8,128)(2,1)S(1)} %convolution_convert_fusion.1), channel_id=1, source_target_pairs={{0,1},{1,0},{2,3},{3,2},{4,5},{5,4},{6,7},{7,6},{8,9},{9,8},{10,11... | collective-permute-start | bytes 786440 | tf_op jit(solution)/shard_map/ppermute | solution.py:19
  92.6 1.8 %collective-permute-done.23 = bf16[128,1024]{1,0:T(8,128)(2,1)S(1)} collective-permute-done((bf16[128,1024]{1,0:T(8,128)(2,1)S(1)}, bf16[128,1024]{1,0:T(8,128)(2,1)S(1)}, u32[]{:S(2)}, u32[]{:S(2)}) %collective-permute-start.23) | collective-permute-done | bytes 262176 | tf_op jit(solution)/shard_map/ppermute | solution.py:19
  94.4 2.2 %collective-permute-done.24 = bf16[128,1024]{1,0:T(8,128)(2,1)S(1)} collective-permute-done((bf16[128,1024]{1,0:T(8,128)(2,1)S(1)}, bf16[128,1024]{1,0:T(8,128)(2,1)S(1)}, u32[]{:S(2)}, u32[]{:S(2)}) %collective-permute-start.24) | collective-permute-done | bytes 262176 | tf_op jit(solution)/shard_map/ppermute | solution.py:19
  96.7 1.7 %collective-permute-done.25 = bf16[128,1024]{1,0:T(8,128)(2,1)S(1)} collective-permute-done((bf16[128,1024]{1,0:T(8,128)(2,1)S(1)}, bf16[128,1024]{1,0:T(8,128)(2,1)S(1)}, u32[]{:S(2)}, u32[]{:S(2)}) %collective-permute-start.25) | collective-permute-done | bytes 262176 | tf_op jit(solution)/shard_map/ppermute | solution.py:19
  (70 shorter events, 11.8 us)
Async XLA Ops:
  0.0 11.0 %copy-start.4 = (bf16[128,8192]{1,0:T(8,128)(2,1)S(1)}, bf16[128,8192]{1,0:T(8,128)(2,1)}, u32[]{:S(2)}) copy-start(bf16[128,8192]{1,0:T(8,128)(2,1)} %param.4) | copy-start | bytes 6291460
  1.9 14.5 %collective-permute-start.9 = (bf16[128,1024]{1,0:T(8,128)(2,1)}, bf16[128,1024]{1,0:T(8,128)(2,1)}, u32[]{:S(2)}, u32[]{:S(2)}) collective-permute-start(bf16[128,1024]{1,0:T(8,128)(2,1)} %get-tuple-element.14), channel_id=1, source_target_pairs={{0,1},{1,0},{2,3},{3,2},{4,6},{5,7},{6,4},{7,5},{8,9},{9,8},{10,11... | collective-permute-start | bytes 786440 | tf_op jit(solution)/shard_map/ppermute | solution.py:32
  4.9 19.7 %collective-permute-start.10 = (bf16[128,1024]{1,0:T(8,128)(2,1)S(1)}, bf16[128,1024]{1,0:T(8,128)(2,1)}, u32[]{:S(2)}, u32[]{:S(2)}) collective-permute-start(bf16[128,1024]{1,0:T(8,128)(2,1)S(1)} %get-tuple-element.13), channel_id=1, source_target_pairs={{0,1},{1,0},{2,3},{3,2},{4,6},{5,7},{6,4},{7,5},{8,9},{9,8},{10,11... | collective-permute-start | bytes 786440 | tf_op jit(solution)/shard_map/ppermute | solution.py:32
  7.5 25.2 %collective-permute-start.3 = (bf16[128,2048]{1,0:T(8,128)(2,1)}, bf16[128,2048]{1,0:T(8,128)(2,1)}, u32[]{:S(2)}, u32[]{:S(2)}) collective-permute-start(bf16[128,2048]{1,0:T(8,128)(2,1)} %get-tuple-element.17), channel_id=1, source_target_pairs={{0,3},{1,2},{2,1},{3,0},{4,7},{5,6},{6,5},{7,4},{8,11},{9,10},{10,... | collective-permute-start | bytes 1572872 | tf_op jit(solution)/shard_map/ppermute | solution.py:19
  10.4 31.2 %collective-permute-start.2 = (bf16[128,2048]{1,0:T(8,128)(2,1)}, bf16[128,2048]{1,0:T(8,128)(2,1)S(1)}, u32[]{:S(2)}, u32[]{:S(2)}) collective-permute-start(bf16[128,2048]{1,0:T(8,128)(2,1)} %get-tuple-element.15), channel_id=1, source_target_pairs={{0,2},{1,3},{2,0},{3,1},{4,6},{5,7},{6,4},{7,5},{8,10},{9,11},{10,... | collective-permute-start | bytes 1572872 | tf_op jit(solution)/shard_map/ppermute | solution.py:19
  11.0 27.3 %collective-permute-start = (bf16[128,2048]{1,0:T(8,128)(2,1)}, bf16[128,2048]{1,0:T(8,128)(2,1)S(1)}, u32[]{:S(2)}, u32[]{:S(2)}) collective-permute-start(bf16[128,2048]{1,0:T(8,128)(2,1)} %get-tuple-element.16), channel_id=1, source_target_pairs={{0,1},{1,0},{2,3},{3,2},{4,5},{5,4},{6,7},{7,6},{8,9},{9,8},{10,11... | collective-permute-start | bytes 1572872 | tf_op jit(solution)/shard_map/ppermute | solution.py:19
  25.5 10.7 %copy-start.2 = (bf16[2048,1024]{1,0:T(8,128)(2,1)S(1)}, bf16[2048,1024]{1,0:T(8,128)(2,1)}, u32[]{:S(2)}) copy-start(bf16[2048,1024]{1,0:T(8,128)(2,1)} %param.6) | copy-start | bytes 12582916
  25.6 27.5 %collective-permute-start.12 = (bf16[256,1024]{1,0:T(8,128)(2,1)S(1)}, bf16[256,1024]{1,0:T(8,128)(2,1)S(1)}, u32[]{:S(2)}, u32[]{:S(2)}) collective-permute-start(bf16[256,1024]{1,0:T(8,128)(2,1)S(1)} %constant_dynamic-update-slice_fusion), channel_id=1, source_target_pairs={{8,24},{12,28},{16,0},{20,4},{9,25},{13,29},{17,1},{21,5},{10,26},... | collective-permute-start | bytes 1572872 | tf_op jit(solution)/shard_map/ppermute | solution.py:36
  27.1 26.6 %collective-permute-start.13 = (bf16[256,1024]{1,0:T(8,128)(2,1)S(1)}, bf16[256,1024]{1,0:T(8,128)(2,1)S(1)}, u32[]{:S(2)}, u32[]{:S(2)}) collective-permute-start(bf16[256,1024]{1,0:T(8,128)(2,1)S(1)} %constant_dynamic-update-slice_fusion), channel_id=1, source_target_pairs={{0,16},{4,20},{24,8},{28,12},{1,17},{5,21},{25,9},{29,13},{2,18},{... | collective-permute-start | bytes 1572872 | tf_op jit(solution)/shard_map/ppermute | solution.py:36
  32.6 21.4 %collective-permute-start.11 = (bf16[256,1024]{1,0:T(8,128)(2,1)S(1)}, bf16[256,1024]{1,0:T(8,128)(2,1)S(1)}, u32[]{:S(2)}, u32[]{:S(2)}) collective-permute-start(bf16[256,1024]{1,0:T(8,128)(2,1)S(1)} %constant_dynamic-update-slice_fusion), channel_id=1, source_target_pairs={{0,8},{4,12},{8,0},{12,4},{16,24},{20,28},{24,16},{28,20},{1,9},{5... | collective-permute-start | bytes 1572872 | tf_op jit(solution)/shard_map/ppermute | solution.py:36
  36.2 4.6 %copy-start.1 = (bf16[2048,1024]{1,0:T(8,128)(2,1)S(1)}, bf16[2048,1024]{1,0:T(8,128)(2,1)}, u32[]{:S(2)}) copy-start(bf16[2048,1024]{1,0:T(8,128)(2,1)} %param.5) | copy-start | bytes 12582916
  38.2 9.5 %collective-permute-start.4 = (bf16[128,1024]{1,0:T(8,128)(2,1)S(1)}, bf16[128,1024]{1,0:T(8,128)(2,1)S(1)}, u32[]{:S(2)}, u32[]{:S(2)}) collective-permute-start(bf16[128,1024]{1,0:T(8,128)(2,1)S(1)} %convolution_convert_fusion.7), channel_id=1, source_target_pairs={{0,1},{1,0},{2,3},{3,2},{4,5},{5,4},{6,7},{7,6},{8,9},{9,8},{10,11... | collective-permute-start | bytes 786440 | tf_op jit(solution)/shard_map/ppermute | solution.py:19
  41.6 9.2 %collective-permute-start.7 = (bf16[128,1024]{1,0:T(8,128)(2,1)S(1)}, bf16[128,1024]{1,0:T(8,128)(2,1)S(1)}, u32[]{:S(2)}, u32[]{:S(2)}) collective-permute-start(bf16[128,1024]{1,0:T(8,128)(2,1)S(1)} %convolution_convert_fusion.5), channel_id=1, source_target_pairs={{0,2},{1,3},{2,0},{3,1},{4,6},{5,7},{6,4},{7,5},{8,10},{9,11},{10,... | collective-permute-start | bytes 786440 | tf_op jit(solution)/shard_map/ppermute | solution.py:19
  47.7 7.2 %collective-permute-start.1 = (bf16[128,1024]{1,0:T(8,128)(2,1)S(1)}, bf16[128,1024]{1,0:T(8,128)(2,1)S(1)}, u32[]{:S(2)}, u32[]{:S(2)}) collective-permute-start(bf16[128,1024]{1,0:T(8,128)(2,1)S(1)} %convolution_convert_fusion.8), channel_id=1, source_target_pairs={{0,1},{1,0},{2,3},{3,2},{4,5},{5,4},{6,7},{7,6},{8,9},{9,8},{10,11... | collective-permute-start | bytes 786440 | tf_op jit(solution)/shard_map/ppermute | solution.py:19
  50.8 10.8 %copy-start.6 = (f32[128,1024]{1,0:T(8,128)S(1)}, f32[128,1024]{1,0:T(8,128)}, u32[]{:S(2)}) copy-start(f32[128,1024]{1,0:T(8,128)} %fusion.15) | copy-start | bytes 1572868
  50.8 10.8 %copy-start.7 = (f32[128,1024]{1,0:T(8,128)S(1)}, f32[128,1024]{1,0:T(8,128)}, u32[]{:S(2)}) copy-start(f32[128,1024]{1,0:T(8,128)} %fusion.17) | copy-start | bytes 1572868
  50.8 6.4 %collective-permute-start.6 = (bf16[128,1024]{1,0:T(8,128)(2,1)S(1)}, bf16[128,1024]{1,0:T(8,128)(2,1)S(1)}, u32[]{:S(2)}, u32[]{:S(2)}) collective-permute-start(bf16[128,1024]{1,0:T(8,128)(2,1)S(1)} %convolution_convert_fusion.6), channel_id=1, source_target_pairs={{0,2},{1,3},{2,0},{3,1},{4,6},{5,7},{6,4},{7,5},{8,10},{9,11},{10,... | collective-permute-start | bytes 786440 | tf_op jit(solution)/shard_map/ppermute | solution.py:19
  53.1 6.9 %collective-permute-start.5 = (bf16[128,1024]{1,0:T(8,128)(2,1)S(1)}, bf16[128,1024]{1,0:T(8,128)(2,1)S(1)}, u32[]{:S(2)}, u32[]{:S(2)}) collective-permute-start(bf16[128,1024]{1,0:T(8,128)(2,1)S(1)} %fusion.13), channel_id=1, source_target_pairs={{0,2},{1,3},{2,0},{3,1},{4,6},{5,7},{6,4},{7,5},{8,10},{9,11},{10,... | collective-permute-start | bytes 786440 | tf_op jit(solution)/shard_map/ppermute | solution.py:19
  53.7 6.4 %collective-permute-start.8 = (bf16[128,1024]{1,0:T(8,128)(2,1)S(1)}, bf16[128,1024]{1,0:T(8,128)(2,1)S(1)}, u32[]{:S(2)}, u32[]{:S(2)}) collective-permute-start(bf16[128,1024]{1,0:T(8,128)(2,1)S(1)} %fusion.14), channel_id=1, source_target_pairs={{0,1},{1,0},{2,3},{3,2},{4,5},{5,4},{6,7},{7,6},{8,9},{9,8},{10,11... | collective-permute-start | bytes 786440 | tf_op jit(solution)/shard_map/ppermute | solution.py:19
  54.1 8.0 %copy-start.3 = (bf16[1024,2048]{1,0:T(8,128)(2,1)S(1)}, bf16[1024,2048]{1,0:T(8,128)(2,1)}, u32[]{:S(2)}) copy-start(bf16[1024,2048]{1,0:T(8,128)(2,1)} %param.7) | copy-start | bytes 12582916
  54.1 8.7 %collective-permute-start.18 = (bf16[256,1024]{1,0:T(8,128)(2,1)S(1)}, bf16[256,1024]{1,0:T(8,128)(2,1)S(1)}, u32[]{:S(2)}, u32[]{:S(2)}) collective-permute-start(bf16[256,1024]{1,0:T(8,128)(2,1)S(1)} %constant_dynamic-update-slice_fusion), channel_id=1, source_target_pairs={{8,16},{12,20},{16,8},{20,12},{9,17},{13,21},{17,9},{21,13},{10,18... | collective-permute-start | bytes 1572872 | tf_op jit(solution)/shard_map/ppermute | solution.py:36
  54.9 31.1 %collective-permute-start.14 = (bf16[256,1024]{1,0:T(8,128)(2,1)S(1)}, bf16[256,1024]{1,0:T(8,128)(2,1)S(1)}, u32[]{:S(2)}, u32[]{:S(2)}) collective-permute-start(bf16[256,1024]{1,0:T(8,128)(2,1)S(1)} %constant_dynamic-update-slice_fusion), channel_id=1, source_target_pairs={{0,4},{4,0},{8,12},{12,8},{16,20},{20,16},{24,28},{28,24},{1,5},{5... | collective-permute-start | bytes 1572872 | tf_op jit(solution)/shard_map/ppermute | solution.py:36
  57.2 30.4 %collective-permute-start.15 = (bf16[256,1024]{1,0:T(8,128)(2,1)S(1)}, bf16[256,1024]{1,0:T(8,128)(2,1)S(1)}, u32[]{:S(2)}, u32[]{:S(2)}) collective-permute-start(bf16[256,1024]{1,0:T(8,128)(2,1)S(1)} %collective-permute-done.11), channel_id=1, source_target_pairs={{0,4},{4,0},{8,12},{12,8},{16,20},{20,16},{24,28},{28,24},{1,5},{5... | collective-permute-start | bytes 1572872 | tf_op jit(solution)/shard_map/ppermute | solution.py:36
  60.0 27.9 %collective-permute-start.16 = (bf16[256,1024]{1,0:T(8,128)(2,1)S(1)}, bf16[256,1024]{1,0:T(8,128)(2,1)S(1)}, u32[]{:S(2)}, u32[]{:S(2)}) collective-permute-start(bf16[256,1024]{1,0:T(8,128)(2,1)S(1)} %broadcast_select_fusion.1), channel_id=1, source_target_pairs={{0,4},{4,0},{8,12},{12,8},{16,20},{20,16},{24,28},{28,24},{1,5},{5... | collective-permute-start | bytes 1572872 | tf_op jit(solution)/shard_map/ppermute | solution.py:36
  60.1 16.2 %collective-permute-start.17 = (bf16[256,1024]{1,0:T(8,128)(2,1)S(1)}, bf16[256,1024]{1,0:T(8,128)(2,1)S(1)}, u32[]{:S(2)}, u32[]{:S(2)}) collective-permute-start(bf16[256,1024]{1,0:T(8,128)(2,1)S(1)} %collective-permute-done.13), channel_id=1, source_target_pairs={{16,24},{20,28},{8,0},{12,4},{17,25},{21,29},{9,1},{13,5},{18,26},... | collective-permute-start | bytes 1572872 | tf_op jit(solution)/shard_map/ppermute | solution.py:36
  62.8 13.8 %collective-permute-start.20 = (bf16[128,1024]{1,0:T(8,128)(2,1)S(1)}, bf16[128,1024]{1,0:T(8,128)(2,1)S(1)}, u32[]{:S(2)}, u32[]{:S(2)}) collective-permute-start(bf16[128,1024]{1,0:T(8,128)(2,1)S(1)} %multiply_convert_fusion), channel_id=1, source_target_pairs={{0,2},{1,3},{2,0},{3,1},{4,6},{5,7},{6,4},{7,5},{8,10},{9,11},{10,... | collective-permute-start | bytes 786440 | tf_op jit(solution)/shard_map/ppermute | solution.py:19
  76.3 7.8 %collective-permute-start.22 = (bf16[128,1024]{1,0:T(8,128)(2,1)S(1)}, bf16[128,1024]{1,0:T(8,128)(2,1)S(1)}, u32[]{:S(2)}, u32[]{:S(2)}) collective-permute-start(bf16[128,1024]{1,0:T(8,128)(2,1)S(1)} %multiply_convert_fusion), channel_id=1, source_target_pairs={{0,1},{1,0},{2,3},{3,2},{4,5},{5,4},{6,7},{7,6},{8,9},{9,8},{10,11... | collective-permute-start | bytes 786440 | tf_op jit(solution)/shard_map/ppermute | solution.py:19
  76.6 11.6 %collective-permute-start.19 = (bf16[256,1024]{1,0:T(8,128)(2,1)S(1)}, bf16[256,1024]{1,0:T(8,128)(2,1)S(1)}, u32[]{:S(2)}, u32[]{:S(2)}) collective-permute-start(bf16[256,1024]{1,0:T(8,128)(2,1)S(1)} %broadcast_select_fusion), channel_id=1, source_target_pairs={{0,4},{4,0},{8,12},{12,8},{16,20},{20,16},{24,28},{28,24},{1,5},{5... | collective-permute-start | bytes 1572872 | tf_op jit(solution)/shard_map/ppermute | solution.py:36
  84.1 8.5 %collective-permute-start.21 = (bf16[128,1024]{1,0:T(8,128)(2,1)S(1)}, bf16[128,1024]{1,0:T(8,128)(2,1)S(1)}, u32[]{:S(2)}, u32[]{:S(2)}) collective-permute-start(bf16[128,1024]{1,0:T(8,128)(2,1)S(1)} %fusion.5), channel_id=1, source_target_pairs={{0,2},{1,3},{2,0},{3,1},{4,6},{5,7},{6,4},{7,5},{8,10},{9,11},{10,... | collective-permute-start | bytes 786440 | tf_op jit(solution)/shard_map/ppermute | solution.py:19
  86.0 8.4 %collective-permute-start.23 = (bf16[128,1024]{1,0:T(8,128)(2,1)S(1)}, bf16[128,1024]{1,0:T(8,128)(2,1)S(1)}, u32[]{:S(2)}, u32[]{:S(2)}) collective-permute-start(bf16[128,1024]{1,0:T(8,128)(2,1)S(1)} %fusion.8), channel_id=1, source_target_pairs={{0,1},{1,0},{2,3},{3,2},{4,5},{5,4},{6,7},{7,6},{8,9},{9,8},{10,11... | collective-permute-start | bytes 786440 | tf_op jit(solution)/shard_map/ppermute | solution.py:19
  89.0 7.6 %collective-permute-start.24 = (bf16[128,1024]{1,0:T(8,128)(2,1)S(1)}, bf16[128,1024]{1,0:T(8,128)(2,1)S(1)}, u32[]{:S(2)}, u32[]{:S(2)}) collective-permute-start(bf16[128,1024]{1,0:T(8,128)(2,1)S(1)} %convolution_convert_fusion.2), channel_id=1, source_target_pairs={{0,2},{1,3},{2,0},{3,1},{4,6},{5,7},{6,4},{7,5},{8,10},{9,11},{10,... | collective-permute-start | bytes 786440 | tf_op jit(solution)/shard_map/ppermute | solution.py:19
  90.3 8.0 %collective-permute-start.25 = (bf16[128,1024]{1,0:T(8,128)(2,1)S(1)}, bf16[128,1024]{1,0:T(8,128)(2,1)S(1)}, u32[]{:S(2)}, u32[]{:S(2)}) collective-permute-start(bf16[128,1024]{1,0:T(8,128)(2,1)S(1)} %convolution_convert_fusion.1), channel_id=1, source_target_pairs={{0,1},{1,0},{2,3},{3,2},{4,5},{5,4},{6,7},{7,6},{8,9},{9,8},{10,11... | collective-permute-start | bytes 786440 | tf_op jit(solution)/shard_map/ppermute | solution.py:19
  (2 other events, 5.6 us)

commit v5 on v2

--- a/solution.py
+++ b/solution.py
@@ -17,6 +17,18 @@
             (r * cols + c, (r + dr) % rows * cols + (c + dc) % cols) for r in range(rows) for c in range(cols)
         ]
         return lax.ppermute(x, ("row", "col"), pairs)
+
+    turned = cores == 2 and rows == cols
+
+    def send_turned(x, step, along_row):
+        pairs = []
+        for d in range(dp):
+            dr, dc = (step, 0) if along_row != bool(d % cores) else (0, step)
+            for r in range(rows):
+                for c in range(cols):
+                    to = (d * rows + (r + dr) % rows) * cols + (c + dc) % cols
+                    pairs.append(((d * rows + r) * cols + c, to))
+        return lax.ppermute(x, ("dp", "row", "col"), pairs)
 
     def send_dp(x, chip_pairs, core_shift):
         pairs = [(z * cores + k, to * cores + (k + core_shift) % cores) for z, to in chip_pairs for k in range(cores)]
@@ -44,7 +56,17 @@
 
         piece = lax.dynamic_slice_in_dim(w_down, d * share, share, axis=0)
         sides = [(0, dc) for dc in range(1, cols)] + [(dr, 0) for dr in range(1, rows)]
-        held = jnp.concatenate([send(piece[:, half:] if s[0] else piece[:, :half], back(s)) for s in sides], axis=0)
+        if turned:
+            held = jnp.zeros((len(sides) * share, half), jnp.bfloat16)
+            for turn in range(2):
+                kind = turn + core * (1 - 2 * turn)
+                block = lax.dynamic_slice_in_dim(piece, kind * half, half, axis=1)
+                for i in range(1, rows):
+                    got_block = send_turned(block, -i, bool(turn))
+                    at = (kind * (rows - 1) + i - 1) * share
+                    held = lax.dynamic_update_slice_in_dim(held, got_block, at, axis=0)
+        else:
+            held = jnp.concatenate([send(piece[:, half:] if s[0] else piece[:, :half], back(s)) for s in sides], axis=0)
 
         feats = {s: lax.dynamic_slice_in_dim(tokens, place(s) * slab, slab, axis=1) for s in shifts}
         got = {s: send(feats[s], s) for s in away}
@@ -59,8 +81,9 @@
             relayed = send_dp(two_a, [(2, 3), (1, 0)], 0)
             outer = (chip == 0) | (chip == chips - 1)
             two = jnp.where(outer, two_b, two_a)
-            early += [(one, chip ^ 1), (two, chip ^ 2)]
+            early += [(held, chip), (one, chip ^ 1), (two, chip ^ 2)]
         else:
+            early.append((held, chip))
             for z in range(1, chips):
                 turn = send_dp(held, [(i, (i + z) % chips) for i in range(chips)], 0)
                 late.append((turn, (chip - z) % chips))
@@ -71,7 +94,9 @@
             def shift(a, b):
                 return (b, a) if col_first else (a, b)
 
-            parts = {s: matmul(got[s], weight) for s in away}
+            parts = {}
+            for s in away:
+                parts[s] = matmul(got[s], weight)
             parts[0, 0] = matmul(got[0, 0], weight)
             sums = {b: parts[shift(0, b)] for b in range(second)}
             for b in reversed(range(second)):
@@ -101,13 +126,12 @@
                     for i, s in enumerate(sides):
                         far[s] = lax.dynamic_update_slice_in_dim(far[s], moved[i * share : (i + 1) * share], at, axis=0)
 
-        fill([(held, chip)])
         tied, _ = lax.optimization_barrier(([p for p, _ in early], gate_passed + up_passed))
         fill([(p, at) for p, (_, at) in zip(tied, early)])
 
         tied, _ = lax.optimization_barrier(([p for p, _ in late], hidden))
         fill([(p, at) for p, (_, at) in zip(tied, late)])
-        near = {s: send(hidden, back(s)) for s in reversed(sides)}
+        near = {s: send(hidden, back(s)) for s in sides}
         landed = [(matmul(hidden, w_down).astype(jnp.bfloat16), place((0, 0)) * width)]
         outs = []
         for s, other in near.items():

time: 106 us -> 107 us (level)
  waiting for transfers between devices: 49.7 us -> 48.1 us
  matrix products: 15.4 us -> 16.8 us
    ppermute x0 -> x2, waiting for transfers between devices: none -> 4.93 us  [send_turned(): return lax.ppermute(x, ('dp', 'row', 'col'), pairs)]
    ppermute x0 -> x2, starting transfers between devices: none -> 4.49 us  [send_turned(): return lax.ppermute(x, ('dp', 'row', 'col'), pairs)]
    ppermute x17 -> x15, starting transfers between devices: 20.6 us -> 16.5 us  [send(): return lax.ppermute(x, ('row', 'col'), pairs)]
    ppermute x17 -> x15, waiting for transfers between devices: 26.4 us -> 22.8 us  [send(): return lax.ppermute(x, ('row', 'col'), pairs)]
    ppermute x9, waiting for transfers between devices: 23.2 us -> 20.4 us  [send_dp(): return lax.ppermute(x, 'dp', pairs)]
    dynamic_slice x0 -> x1, local copies, waits for them, and re-layouts: none -> 2.16 us  [shards(): block = lax.dynamic_slice_in_dim(piece, kind * half, half, axis=1)]
    dynamic_update_slice x0 -> x2, local copies, waits for them, and re-layouts: none -> 1.95 us  [shards(): held = lax.dynamic_update_slice_in_dim(held, got_block, at, axis=0)]
    slice x1 -> x0, local copies, waits for them, and re-layouts: 1.92 us -> none  [shards(): piece[:, half:]]
  transfers between devices with their start and end apart: 26 -> 26, of which waited for: 11 -> 13; matrix products, arithmetic and copies ran while one was open for 21% -> 22% of each run, Pallas kernels for 0% -> 0%
where the time goes in v5:
time: 107 us
  waiting for transfers between devices  48.1 us (45%)
  starting transfers between devices  31.3 us (29%)
  matrix products  16.8 us (16%)
  local copies, waits for them, and re-layouts  9.48 us (9%)
    ppermute x15, waiting for transfers between devices, send(): return lax.ppermute(x, ('row', 'col'), pairs)  22.8 us
    ppermute x9, waiting for transfers between devices, send_dp(): return lax.ppermute(x, 'dp', pairs)  20.4 us
    dot_general x15, matrix products, matmul(): return jnp.dot(a, b, preferred_element_type=jnp.float32)  16.8 us
    ppermute x15, starting transfers between devices, send(): return lax.ppermute(x, ('row', 'col'), pairs)  16.5 us
    ppermute x9, starting transfers between devices, send_dp(): return lax.ppermute(x, 'dp', pairs)  10.3 us
    ppermute x2, waiting for transfers between devices, send_turned(): return lax.ppermute(x, ('dp', 'row', 'col'), pairs)  4.93 us
    ppermute x2, starting transfers between devices, send_turned(): return lax.ppermute(x, ('dp', 'row', 'col'), pairs)  4.49 us
    dynamic_slice x1, local copies, waits for them, and re-layouts, shards(): lax.dynamic_slice_in_dim(tokens, place(s) * slab, slab, axis=1)  2.59 us
  transfers between devices with their start and end apart: 26, of which 13 were waited for; matrix products, arithmetic and copies ran while one was open for 22% of the time, Pallas kernels for 0%

profile of v5, /device:TPU:0, one launch (start us, length us, event | category | flops | bytes accessed | tf_op | source)
XLA Modules:
  0.0 106.6 jit_solution(16010414475411480651)
XLA Ops:
  0.0 2.2 %fusion.21 = (bf16[128,1024]{1,0:T(8,128)(2,1)S(1)}, bf16[128,1024]{1,0:T(8,128)(2,1)}) fusion(bf16[1024,2048]{1,0:T(8,128)(2,1)} %param.7, s32[]{:T(128)S(6)} %select_n.188, s32[]{:T(128)S(6)} %select_n.194, s32[]{:T(128)S(6)} %select_n.191), kind=kLoop, calls=%fused_computation.56 | loop fusion | bytes 1048588 | tf_op jit(solution)/shard_map/dynamic_slice | solution.py:63
  2.2 3.0 %collective-permute-start.9 = (bf16[128,1024]{1,0:T(8,128)(2,1)}, bf16[128,1024]{1,0:T(8,128)(2,1)}, u32[]{:S(2)}, u32[]{:S(2)}) collective-permute-start(bf16[128,1024]{1,0:T(8,128)(2,1)} %get-tuple-element.14), channel_id=1, source_target_pairs={{0,1},{1,0},{2,3},{3,2},{4,6},{5,7},{6,4},{7,5},{8,9},{9,8},{10,11... | collective-permute-start | bytes 786440 | tf_op jit(solution)/shard_map/ppermute | solution.py:31
  5.2 1.5 %collective-permute-start.10 = (bf16[128,1024]{1,0:T(8,128)(2,1)S(1)}, bf16[128,1024]{1,0:T(8,128)(2,1)}, u32[]{:S(2)}, u32[]{:S(2)}) collective-permute-start(bf16[128,1024]{1,0:T(8,128)(2,1)S(1)} %get-tuple-element.13), channel_id=1, source_target_pairs={{0,2},{1,3},{2,0},{3,1},{4,5},{5,4},{6,7},{7,6},{8,10},{9,11},{10,... | collective-permute-start | bytes 786440 | tf_op jit(solution)/shard_map/ppermute | solution.py:31
  6.7 2.6 %constant_dynamic-slice_fusion.1 = (bf16[128,2048]{1,0:T(8,128)(2,1)}, bf16[128,2048]{1,0:T(8,128)(2,1)}, bf16[128,2048]{1,0:T(8,128)(2,1)}) fusion(bf16[128,8192]{1,0:T(8,128)(2,1)} %param.4, s32[]{:T(128)S(6)} %select_n.185, s32[]{:T(128)S(6)} %select_n.183, s32[]{:T(128)S(6)} %select_n.186), kind=kLoop, calls=%fused_computation.53 | loop fusion | bytes 3145740 | tf_op jit(solution)/shard_map/dynamic_slice | solution.py:71
  9.2 2.0 %collective-permute-start.2 = (bf16[128,2048]{1,0:T(8,128)(2,1)}, bf16[128,2048]{1,0:T(8,128)(2,1)S(1)}, u32[]{:S(2)}, u32[]{:S(2)}) collective-permute-start(bf16[128,2048]{1,0:T(8,128)(2,1)} %get-tuple-element.15), channel_id=1, source_target_pairs={{0,2},{1,3},{2,0},{3,1},{4,6},{5,7},{6,4},{7,5},{8,10},{9,11},{10,... | collective-permute-start | bytes 1572872 | tf_op jit(solution)/shard_map/ppermute | solution.py:19
  11.2 1.5 %collective-permute-start = (bf16[128,2048]{1,0:T(8,128)(2,1)}, bf16[128,2048]{1,0:T(8,128)(2,1)S(1)}, u32[]{:S(2)}, u32[]{:S(2)}) collective-permute-start(bf16[128,2048]{1,0:T(8,128)(2,1)} %get-tuple-element.16), channel_id=1, source_target_pairs={{0,1},{1,0},{2,3},{3,2},{4,5},{5,4},{6,7},{7,6},{8,9},{9,8},{10,11... | collective-permute-start | bytes 1572872 | tf_op jit(solution)/shard_map/ppermute | solution.py:19
  12.7 3.9 %fusion.15 = f32[128,1024]{1,0:T(8,128)} fusion(bf16[2048,1024]{1,0:T(8,128)(2,1)} %param.6, bf16[128,8192]{1,0:T(8,128)(2,1)S(1)} %copy-done.4, s32[]{:T(128)S(6)} %select_n.181), kind=kOutput, calls=%fused_computation.25 | convolution fusion | flops 536870912 | bytes 5242884 | tf_op jit(solution)/shard_map/dot_general | solution.py:44
  16.6 1.6 %fusion.17 = f32[128,1024]{1,0:T(8,128)} fusion(bf16[2048,1024]{1,0:T(8,128)(2,1)S(1)} %copy-done, bf16[128,8192]{1,0:T(8,128)(2,1)S(1)} %copy-done.4, s32[]{:T(128)S(6)} %select_n.181), kind=kOutput, calls=%fused_computation.27 | convolution fusion | flops 536870912 | bytes 5242884 | tf_op jit(solution)/shard_map/dot_general | solution.py:44
  18.1 4.9 %collective-permute-done.9 = bf16[128,1024]{1,0:T(8,128)(2,1)} collective-permute-done((bf16[128,1024]{1,0:T(8,128)(2,1)}, bf16[128,1024]{1,0:T(8,128)(2,1)}, u32[]{:S(2)}, u32[]{:S(2)}) %collective-permute-start.9) | collective-permute-done | bytes 262176 | tf_op jit(solution)/shard_map/ppermute | solution.py:31
  23.1 1.0 constant_dynamic-update-slice_fusion.5
  24.1 1.0 constant_dynamic-update-slice_fusion.4
  25.1 1.6 %collective-permute-start.12 = (bf16[256,1024]{1,0:T(8,128)(2,1)S(1)}, bf16[256,1024]{1,0:T(8,128)(2,1)S(1)}, u32[]{:S(2)}, u32[]{:S(2)}) collective-permute-start(bf16[256,1024]{1,0:T(8,128)(2,1)S(1)} %constant_dynamic-update-slice_fusion.4), channel_id=1, source_target_pairs={{8,24},{12,28},{16,0},{20,4},{9,25},{13,29},{17,1},{21,5},{10,26},... | collective-permute-start | bytes 1572872 | tf_op jit(solution)/shard_map/ppermute | solution.py:35
  26.7 5.5 %collective-permute-start.13 = (bf16[256,1024]{1,0:T(8,128)(2,1)S(1)}, bf16[256,1024]{1,0:T(8,128)(2,1)S(1)}, u32[]{:S(2)}, u32[]{:S(2)}) collective-permute-start(bf16[256,1024]{1,0:T(8,128)(2,1)S(1)} %constant_dynamic-update-slice_fusion.4), channel_id=1, source_target_pairs={{0,16},{4,20},{24,8},{28,12},{1,17},{5,21},{25,9},{29,13},{2,18},{... | collective-permute-start | bytes 1572872 | tf_op jit(solution)/shard_map/ppermute | solution.py:35
  32.2 1.0 collective-permute-start.11
  33.2 3.1 %convolution_convert_fusion.7 = bf16[128,1024]{1,0:T(8,128)(2,1)S(1)} fusion(bf16[128,2048]{1,0:T(8,128)(2,1)} %collective-permute-done.3, bf16[2048,1024]{1,0:T(8,128)(2,1)} %param.5), kind=kOutput, calls=%fused_computation.20 | convolution fusion | flops 537001984 | bytes 4980736 | tf_op jit(solution)/shard_map/dot_general | solution.py:44
  36.3 1.9 %convolution_convert_fusion.5 = bf16[128,1024]{1,0:T(8,128)(2,1)S(1)} fusion(bf16[128,2048]{1,0:T(8,128)(2,1)} %collective-permute-done.3, bf16[2048,1024]{1,0:T(8,128)(2,1)S(1)} %copy-done.2), kind=kOutput, calls=%fused_computation.18 | convolution fusion | flops 537001984 | bytes 4980736 | tf_op jit(solution)/shard_map/dot_general | solution.py:44
  39.0 0.7 convolution_convert_fusion.8
  39.8 2.5 %collective-permute-start.4 = (bf16[128,1024]{1,0:T(8,128)(2,1)S(1)}, bf16[128,1024]{1,0:T(8,128)(2,1)S(1)}, u32[]{:S(2)}, u32[]{:S(2)}) collective-permute-start(bf16[128,1024]{1,0:T(8,128)(2,1)S(1)} %convolution_convert_fusion.7), channel_id=1, source_target_pairs={{0,1},{1,0},{2,3},{3,2},{4,5},{5,4},{6,7},{7,6},{8,9},{9,8},{10,11... | collective-permute-start | bytes 786440 | tf_op jit(solution)/shard_map/ppermute | solution.py:19
  43.0 3.7 %collective-permute-done.4 = bf16[128,1024]{1,0:T(8,128)(2,1)S(1)} collective-permute-done((bf16[128,1024]{1,0:T(8,128)(2,1)S(1)}, bf16[128,1024]{1,0:T(8,128)(2,1)S(1)}, u32[]{:S(2)}, u32[]{:S(2)}) %collective-permute-start.4) | collective-permute-done | bytes 262176 | tf_op jit(solution)/shard_map/ppermute | solution.py:19
  48.1 6.1 %collective-permute-done.12 = bf16[256,1024]{1,0:T(8,128)(2,1)S(1)} collective-permute-done((bf16[256,1024]{1,0:T(8,128)(2,1)S(1)}, bf16[256,1024]{1,0:T(8,128)(2,1)S(1)}, u32[]{:S(2)}, u32[]{:S(2)}) %collective-permute-start.12) | collective-permute-done | bytes 524320 | tf_op jit(solution)/shard_map/ppermute | solution.py:35
  54.2 2.8 %collective-permute-start.1 = (bf16[128,1024]{1,0:T(8,128)(2,1)S(1)}, bf16[128,1024]{1,0:T(8,128)(2,1)S(1)}, u32[]{:S(2)}, u32[]{:S(2)}) collective-permute-start(bf16[128,1024]{1,0:T(8,128)(2,1)S(1)} %convolution_convert_fusion.8), channel_id=1, source_target_pairs={{0,1},{1,0},{2,3},{3,2},{4,5},{5,4},{6,7},{7,6},{8,9},{9,8},{10,11... | collective-permute-start | bytes 786440 | tf_op jit(solution)/shard_map/ppermute | solution.py:19
  57.1 2.1 %collective-permute-start.5 = (bf16[128,1024]{1,0:T(8,128)(2,1)S(1)}, bf16[128,1024]{1,0:T(8,128)(2,1)S(1)}, u32[]{:S(2)}, u32[]{:S(2)}) collective-permute-start(bf16[128,1024]{1,0:T(8,128)(2,1)S(1)} %fusion.13), channel_id=1, source_target_pairs={{0,2},{1,3},{2,0},{3,1},{4,6},{5,7},{6,4},{7,5},{8,10},{9,11},{10,... | collective-permute-start | bytes 786440 | tf_op jit(solution)/shard_map/ppermute | solution.py:19
  60.8 2.0 %collective-permute-done.1 = bf16[128,1024]{1,0:T(8,128)(2,1)S(1)} collective-permute-done((bf16[128,1024]{1,0:T(8,128)(2,1)S(1)}, bf16[128,1024]{1,0:T(8,128)(2,1)S(1)}, u32[]{:S(2)}, u32[]{:S(2)}) %collective-permute-start.1) | collective-permute-done | bytes 262176 | tf_op jit(solution)/shard_map/ppermute | solution.py:19
  63.4 2.8 %collective-permute-done.5 = bf16[128,1024]{1,0:T(8,128)(2,1)S(1)} collective-permute-done((bf16[128,1024]{1,0:T(8,128)(2,1)S(1)}, bf16[128,1024]{1,0:T(8,128)(2,1)S(1)}, u32[]{:S(2)}, u32[]{:S(2)}) %collective-permute-start.5) | collective-permute-done | bytes 262176 | tf_op jit(solution)/shard_map/ppermute | solution.py:19
  66.4 1.5 %collective-permute-start.17 = (bf16[256,1024]{1,0:T(8,128)(2,1)S(1)}, bf16[256,1024]{1,0:T(8,128)(2,1)S(1)}, u32[]{:S(2)}, u32[]{:S(2)}) collective-permute-start(bf16[256,1024]{1,0:T(8,128)(2,1)S(1)} %collective-permute-done.13), channel_id=1, source_target_pairs={{16,24},{20,28},{8,0},{12,4},{17,25},{21,29},{9,1},{13,5},{18,26},... | collective-permute-start | bytes 1572872 | tf_op jit(solution)/shard_map/ppermute | solution.py:35
  69.2 14.2 %collective-permute-done.17 = bf16[256,1024]{1,0:T(8,128)(2,1)S(1)} collective-permute-done((bf16[256,1024]{1,0:T(8,128)(2,1)S(1)}, bf16[256,1024]{1,0:T(8,128)(2,1)S(1)}, u32[]{:S(2)}, u32[]{:S(2)}) %collective-permute-start.17) | collective-permute-done | bytes 524320 | tf_op jit(solution)/shard_map/ppermute | solution.py:35
  84.6 7.0 %collective-permute-done.22 = bf16[128,1024]{1,0:T(8,128)(2,1)S(1)} collective-permute-done((bf16[128,1024]{1,0:T(8,128)(2,1)S(1)}, bf16[128,1024]{1,0:T(8,128)(2,1)S(1)}, u32[]{:S(2)}, u32[]{:S(2)}) %collective-permute-start.22) | collective-permute-done | bytes 262176 | tf_op jit(solution)/shard_map/ppermute | solution.py:19
  93.3 2.1 %collective-permute-start.24 = (bf16[128,1024]{1,0:T(8,128)(2,1)S(1)}, bf16[128,1024]{1,0:T(8,128)(2,1)S(1)}, u32[]{:S(2)}, u32[]{:S(2)}) collective-permute-start(bf16[128,1024]{1,0:T(8,128)(2,1)S(1)} %convolution_convert_fusion.2), channel_id=1, source_target_pairs={{0,1},{1,0},{2,3},{3,2},{4,5},{5,4},{6,7},{7,6},{8,9},{9,8},{10,11... | collective-permute-start | bytes 786440 | tf_op jit(solution)/shard_map/ppermute | solution.py:19
  96.3 1.7 %collective-permute-start.25 = (bf16[128,1024]{1,0:T(8,128)(2,1)S(1)}, bf16[128,1024]{1,0:T(8,128)(2,1)S(1)}, u32[]{:S(2)}, u32[]{:S(2)}) collective-permute-start(bf16[128,1024]{1,0:T(8,128)(2,1)S(1)} %convolution_convert_fusion.1), channel_id=1, source_target_pairs={{0,2},{1,3},{2,0},{3,1},{4,6},{5,7},{6,4},{7,5},{8,10},{9,11},{10,... | collective-permute-start | bytes 786440 | tf_op jit(solution)/shard_map/ppermute | solution.py:19
  98.4 2.3 %collective-permute-done.21 = bf16[128,1024]{1,0:T(8,128)(2,1)S(1)} collective-permute-done((bf16[128,1024]{1,0:T(8,128)(2,1)S(1)}, bf16[128,1024]{1,0:T(8,128)(2,1)S(1)}, u32[]{:S(2)}, u32[]{:S(2)}) %collective-permute-start.21) | collective-permute-done | bytes 262176 | tf_op jit(solution)/shard_map/ppermute | solution.py:19
  101.3 3.2 %collective-permute-done.24 = bf16[128,1024]{1,0:T(8,128)(2,1)S(1)} collective-permute-done((bf16[128,1024]{1,0:T(8,128)(2,1)S(1)}, bf16[128,1024]{1,0:T(8,128)(2,1)S(1)}, u32[]{:S(2)}, u32[]{:S(2)}) %collective-permute-start.24) | collective-permute-done | bytes 262176 | tf_op jit(solution)/shard_map/ppermute | solution.py:19
  105.0 0.8 copy-done.5
  (75 shorter events, 12.4 us)
Async XLA Ops:
  0.0 12.7 %copy-start.4 = (bf16[128,8192]{1,0:T(8,128)(2,1)S(1)}, bf16[128,8192]{1,0:T(8,128)(2,1)}, u32[]{:S(2)}) copy-start(bf16[128,8192]{1,0:T(8,128)(2,1)} %param.4) | copy-start | bytes 6291460
  2.2 20.9 %collective-permute-start.9 = (bf16[128,1024]{1,0:T(8,128)(2,1)}, bf16[128,1024]{1,0:T(8,128)(2,1)}, u32[]{:S(2)}, u32[]{:S(2)}) collective-permute-start(bf16[128,1024]{1,0:T(8,128)(2,1)} %get-tuple-element.14), channel_id=1, source_target_pairs={{0,1},{1,0},{2,3},{3,2},{4,6},{5,7},{6,4},{7,5},{8,9},{9,8},{10,11... | collective-permute-start | bytes 786440 | tf_op jit(solution)/shard_map/ppermute | solution.py:31
  5.2 19.0 %collective-permute-start.10 = (bf16[128,1024]{1,0:T(8,128)(2,1)S(1)}, bf16[128,1024]{1,0:T(8,128)(2,1)}, u32[]{:S(2)}, u32[]{:S(2)}) collective-permute-start(bf16[128,1024]{1,0:T(8,128)(2,1)S(1)} %get-tuple-element.13), channel_id=1, source_target_pairs={{0,2},{1,3},{2,0},{3,1},{4,5},{5,4},{6,7},{7,6},{8,10},{9,11},{10,... | collective-permute-start | bytes 786440 | tf_op jit(solution)/shard_map/ppermute | solution.py:31
  9.2 23.0 %collective-permute-start.3 = (bf16[128,2048]{1,0:T(8,128)(2,1)}, bf16[128,2048]{1,0:T(8,128)(2,1)}, u32[]{:S(2)}, u32[]{:S(2)}) collective-permute-start(bf16[128,2048]{1,0:T(8,128)(2,1)} %get-tuple-element.17), channel_id=1, source_target_pairs={{0,3},{1,2},{2,1},{3,0},{4,7},{5,6},{6,5},{7,4},{8,11},{9,10},{10,... | collective-permute-start | bytes 1572872 | tf_op jit(solution)/shard_map/ppermute | solution.py:19
  9.2 30.5 %collective-permute-start.2 = (bf16[128,2048]{1,0:T(8,128)(2,1)}, bf16[128,2048]{1,0:T(8,128)(2,1)S(1)}, u32[]{:S(2)}, u32[]{:S(2)}) collective-permute-start(bf16[128,2048]{1,0:T(8,128)(2,1)} %get-tuple-element.15), channel_id=1, source_target_pairs={{0,2},{1,3},{2,0},{3,1},{4,6},{5,7},{6,4},{7,5},{8,10},{9,11},{10,... | collective-permute-start | bytes 1572872 | tf_op jit(solution)/shard_map/ppermute | solution.py:19
  11.2 27.1 %collective-permute-start = (bf16[128,2048]{1,0:T(8,128)(2,1)}, bf16[128,2048]{1,0:T(8,128)(2,1)S(1)}, u32[]{:S(2)}, u32[]{:S(2)}) collective-permute-start(bf16[128,2048]{1,0:T(8,128)(2,1)} %get-tuple-element.16), channel_id=1, source_target_pairs={{0,1},{1,0},{2,3},{3,2},{4,5},{5,4},{6,7},{7,6},{8,9},{9,8},{10,11... | collective-permute-start | bytes 1572872 | tf_op jit(solution)/shard_map/ppermute | solution.py:19
  12.7 3.9 %copy-start = (bf16[2048,1024]{1,0:T(8,128)(2,1)S(1)}, bf16[2048,1024]{1,0:T(8,128)(2,1)}, u32[]{:S(2)}) copy-start(bf16[2048,1024]{1,0:T(8,128)(2,1)} %param.5) | copy-start | bytes 12582916
  25.1 11.2 %copy-start.2 = (bf16[2048,1024]{1,0:T(8,128)(2,1)S(1)}, bf16[2048,1024]{1,0:T(8,128)(2,1)}, u32[]{:S(2)}) copy-start(bf16[2048,1024]{1,0:T(8,128)(2,1)} %param.6) | copy-start | bytes 12582916
  25.1 29.1 %collective-permute-start.12 = (bf16[256,1024]{1,0:T(8,128)(2,1)S(1)}, bf16[256,1024]{1,0:T(8,128)(2,1)S(1)}, u32[]{:S(2)}, u32[]{:S(2)}) collective-permute-start(bf16[256,1024]{1,0:T(8,128)(2,1)S(1)} %constant_dynamic-update-slice_fusion.4), channel_id=1, source_target_pairs={{8,24},{12,28},{16,0},{20,4},{9,25},{13,29},{17,1},{21,5},{10,26},... | collective-permute-start | bytes 1572872 | tf_op jit(solution)/shard_map/ppermute | solution.py:35
  26.7 30.4 %collective-permute-start.13 = (bf16[256,1024]{1,0:T(8,128)(2,1)S(1)}, bf16[256,1024]{1,0:T(8,128)(2,1)S(1)}, u32[]{:S(2)}, u32[]{:S(2)}) collective-permute-start(bf16[256,1024]{1,0:T(8,128)(2,1)S(1)} %constant_dynamic-update-slice_fusion.4), channel_id=1, source_target_pairs={{0,16},{4,20},{24,8},{28,12},{1,17},{5,21},{25,9},{29,13},{2,18},{... | collective-permute-start | bytes 1572872 | tf_op jit(solution)/shard_map/ppermute | solution.py:35
  32.2 27.8 %collective-permute-start.11 = (bf16[256,1024]{1,0:T(8,128)(2,1)S(1)}, bf16[256,1024]{1,0:T(8,128)(2,1)S(1)}, u32[]{:S(2)}, u32[]{:S(2)}) collective-permute-start(bf16[256,1024]{1,0:T(8,128)(2,1)S(1)} %constant_dynamic-update-slice_fusion.4), channel_id=1, source_target_pairs={{0,8},{4,12},{8,0},{12,4},{16,24},{20,28},{24,16},{28,20},{1,9},{5... | collective-permute-start | bytes 1572872 | tf_op jit(solution)/shard_map/ppermute | solution.py:35
  38.3 30.9 %collective-permute-start.18 = (bf16[256,1024]{1,0:T(8,128)(2,1)S(1)}, bf16[256,1024]{1,0:T(8,128)(2,1)S(1)}, u32[]{:S(2)}, u32[]{:S(2)}) collective-permute-start(bf16[256,1024]{1,0:T(8,128)(2,1)S(1)} %constant_dynamic-update-slice_fusion.4), channel_id=1, source_target_pairs={{8,16},{12,20},{16,8},{20,12},{9,17},{13,21},{17,9},{21,13},{10,18... | collective-permute-start | bytes 1572872 | tf_op jit(solution)/shard_map/ppermute | solution.py:35
  39.8 7.0 %collective-permute-start.4 = (bf16[128,1024]{1,0:T(8,128)(2,1)S(1)}, bf16[128,1024]{1,0:T(8,128)(2,1)S(1)}, u32[]{:S(2)}, u32[]{:S(2)}) collective-permute-start(bf16[128,1024]{1,0:T(8,128)(2,1)S(1)} %convolution_convert_fusion.7), channel_id=1, source_target_pairs={{0,1},{1,0},{2,3},{3,2},{4,5},{5,4},{6,7},{7,6},{8,9},{9,8},{10,11... | collective-permute-start | bytes 786440 | tf_op jit(solution)/shard_map/ppermute | solution.py:19
  46.8 10.4 %collective-permute-start.7 = (bf16[128,1024]{1,0:T(8,128)(2,1)S(1)}, bf16[128,1024]{1,0:T(8,128)(2,1)S(1)}, u32[]{:S(2)}, u32[]{:S(2)}) collective-permute-start(bf16[128,1024]{1,0:T(8,128)(2,1)S(1)} %convolution_convert_fusion.5), channel_id=1, source_target_pairs={{0,2},{1,3},{2,0},{3,1},{4,6},{5,7},{6,4},{7,5},{8,10},{9,11},{10,... | collective-permute-start | bytes 786440 | tf_op jit(solution)/shard_map/ppermute | solution.py:19
  54.2 8.6 %collective-permute-start.1 = (bf16[128,1024]{1,0:T(8,128)(2,1)S(1)}, bf16[128,1024]{1,0:T(8,128)(2,1)S(1)}, u32[]{:S(2)}, u32[]{:S(2)}) collective-permute-start(bf16[128,1024]{1,0:T(8,128)(2,1)S(1)} %convolution_convert_fusion.8), channel_id=1, source_target_pairs={{0,1},{1,0},{2,3},{3,2},{4,5},{5,4},{6,7},{7,6},{8,9},{9,8},{10,11... | collective-permute-start | bytes 786440 | tf_op jit(solution)/shard_map/ppermute | solution.py:19
  57.0 6.4 %collective-permute-start.6 = (bf16[128,1024]{1,0:T(8,128)(2,1)S(1)}, bf16[128,1024]{1,0:T(8,128)(2,1)S(1)}, u32[]{:S(2)}, u32[]{:S(2)}) collective-permute-start(bf16[128,1024]{1,0:T(8,128)(2,1)S(1)} %convolution_convert_fusion.6), channel_id=1, source_target_pairs={{0,2},{1,3},{2,0},{3,1},{4,6},{5,7},{6,4},{7,5},{8,10},{9,11},{10,... | collective-permute-start | bytes 786440 | tf_op jit(solution)/shard_map/ppermute | solution.py:19
  57.1 9.1 %collective-permute-start.5 = (bf16[128,1024]{1,0:T(8,128)(2,1)S(1)}, bf16[128,1024]{1,0:T(8,128)(2,1)S(1)}, u32[]{:S(2)}, u32[]{:S(2)}) collective-permute-start(bf16[128,1024]{1,0:T(8,128)(2,1)S(1)} %fusion.13), channel_id=1, source_target_pairs={{0,2},{1,3},{2,0},{3,1},{4,6},{5,7},{6,4},{7,5},{8,10},{9,11},{10,... | collective-permute-start | bytes 786440 | tf_op jit(solution)/shard_map/ppermute | solution.py:19
  60.0 6.4 %collective-permute-start.8 = (bf16[128,1024]{1,0:T(8,128)(2,1)S(1)}, bf16[128,1024]{1,0:T(8,128)(2,1)S(1)}, u32[]{:S(2)}, u32[]{:S(2)}) collective-permute-start(bf16[128,1024]{1,0:T(8,128)(2,1)S(1)} %fusion.14), channel_id=1, source_target_pairs={{0,1},{1,0},{2,3},{3,2},{4,5},{5,4},{6,7},{7,6},{8,9},{9,8},{10,11... | collective-permute-start | bytes 786440 | tf_op jit(solution)/shard_map/ppermute | solution.py:19
  60.3 7.5 %copy-start.6 = (f32[128,1024]{1,0:T(8,128)S(1)}, f32[128,1024]{1,0:T(8,128)}, u32[]{:S(2)}) copy-start(f32[128,1024]{1,0:T(8,128)} %fusion.15) | copy-start | bytes 1572868
  60.4 7.5 %copy-start.7 = (f32[128,1024]{1,0:T(8,128)S(1)}, f32[128,1024]{1,0:T(8,128)}, u32[]{:S(2)}) copy-start(f32[128,1024]{1,0:T(8,128)} %fusion.17) | copy-start | bytes 1572868
  60.8 7.6 %copy-start.3 = (bf16[1024,2048]{1,0:T(8,128)(2,1)S(1)}, bf16[1024,2048]{1,0:T(8,128)(2,1)}, u32[]{:S(2)}) copy-start(bf16[1024,2048]{1,0:T(8,128)(2,1)} %param.7) | copy-start | bytes 12582916
  62.8 29.3 %collective-permute-start.14 = (bf16[256,1024]{1,0:T(8,128)(2,1)S(1)}, bf16[256,1024]{1,0:T(8,128)(2,1)S(1)}, u32[]{:S(2)}, u32[]{:S(2)}) collective-permute-start(bf16[256,1024]{1,0:T(8,128)(2,1)S(1)} %constant_dynamic-update-slice_fusion.4), channel_id=1, source_target_pairs={{0,4},{4,0},{8,12},{12,8},{16,20},{20,16},{24,28},{28,24},{1,5},{5... | collective-permute-start | bytes 1572872 | tf_op jit(solution)/shard_map/ppermute | solution.py:35
  63.4 29.1 %collective-permute-start.15 = (bf16[256,1024]{1,0:T(8,128)(2,1)S(1)}, bf16[256,1024]{1,0:T(8,128)(2,1)S(1)}, u32[]{:S(2)}, u32[]{:S(2)}) collective-permute-start(bf16[256,1024]{1,0:T(8,128)(2,1)S(1)} %collective-permute-done.11), channel_id=1, source_target_pairs={{0,4},{4,0},{8,12},{12,8},{16,20},{20,16},{24,28},{28,24},{1,5},{5... | collective-permute-start | bytes 1572872 | tf_op jit(solution)/shard_map/ppermute | solution.py:35
  66.2 26.4 %collective-permute-start.16 = (bf16[256,1024]{1,0:T(8,128)(2,1)S(1)}, bf16[256,1024]{1,0:T(8,128)(2,1)S(1)}, u32[]{:S(2)}, u32[]{:S(2)}) collective-permute-start(bf16[256,1024]{1,0:T(8,128)(2,1)S(1)} %broadcast_select_fusion.1), channel_id=1, source_target_pairs={{0,4},{4,0},{8,12},{12,8},{16,20},{20,16},{24,28},{28,24},{1,5},{5... | collective-permute-start | bytes 1572872 | tf_op jit(solution)/shard_map/ppermute | solution.py:35
  66.4 17.0 %collective-permute-start.17 = (bf16[256,1024]{1,0:T(8,128)(2,1)S(1)}, bf16[256,1024]{1,0:T(8,128)(2,1)S(1)}, u32[]{:S(2)}, u32[]{:S(2)}) collective-permute-start(bf16[256,1024]{1,0:T(8,128)(2,1)S(1)} %collective-permute-done.13), channel_id=1, source_target_pairs={{16,24},{20,28},{8,0},{12,4},{17,25},{21,29},{9,1},{13,5},{18,26},... | collective-permute-start | bytes 1572872 | tf_op jit(solution)/shard_map/ppermute | solution.py:35
  69.2 14.9 %collective-permute-start.20 = (bf16[128,1024]{1,0:T(8,128)(2,1)S(1)}, bf16[128,1024]{1,0:T(8,128)(2,1)S(1)}, u32[]{:S(2)}, u32[]{:S(2)}) collective-permute-start(bf16[128,1024]{1,0:T(8,128)(2,1)S(1)} %multiply_convert_fusion), channel_id=1, source_target_pairs={{0,1},{1,0},{2,3},{3,2},{4,5},{5,4},{6,7},{7,6},{8,9},{9,8},{10,11... | collective-permute-start | bytes 786440 | tf_op jit(solution)/shard_map/ppermute | solution.py:19
  83.5 8.1 %collective-permute-start.22 = (bf16[128,1024]{1,0:T(8,128)(2,1)S(1)}, bf16[128,1024]{1,0:T(8,128)(2,1)S(1)}, u32[]{:S(2)}, u32[]{:S(2)}) collective-permute-start(bf16[128,1024]{1,0:T(8,128)(2,1)S(1)} %multiply_convert_fusion), channel_id=1, source_target_pairs={{0,2},{1,3},{2,0},{3,1},{4,6},{5,7},{6,4},{7,5},{8,10},{9,11},{10,... | collective-permute-start | bytes 786440 | tf_op jit(solution)/shard_map/ppermute | solution.py:19
  84.1 8.6 %collective-permute-start.19 = (bf16[256,1024]{1,0:T(8,128)(2,1)S(1)}, bf16[256,1024]{1,0:T(8,128)(2,1)S(1)}, u32[]{:S(2)}, u32[]{:S(2)}) collective-permute-start(bf16[256,1024]{1,0:T(8,128)(2,1)S(1)} %broadcast_select_fusion), channel_id=1, source_target_pairs={{0,4},{4,0},{8,12},{12,8},{16,20},{20,16},{24,28},{28,24},{1,5},{5... | collective-permute-start | bytes 1572872 | tf_op jit(solution)/shard_map/ppermute | solution.py:35
  91.6 9.2 %collective-permute-start.21 = (bf16[128,1024]{1,0:T(8,128)(2,1)S(1)}, bf16[128,1024]{1,0:T(8,128)(2,1)S(1)}, u32[]{:S(2)}, u32[]{:S(2)}) collective-permute-start(bf16[128,1024]{1,0:T(8,128)(2,1)S(1)} %fusion.5), channel_id=1, source_target_pairs={{0,1},{1,0},{2,3},{3,2},{4,5},{5,4},{6,7},{7,6},{8,9},{9,8},{10,11... | collective-permute-start | bytes 786440 | tf_op jit(solution)/shard_map/ppermute | solution.py:19
  92.1 9.2 %collective-permute-start.23 = (bf16[128,1024]{1,0:T(8,128)(2,1)S(1)}, bf16[128,1024]{1,0:T(8,128)(2,1)S(1)}, u32[]{:S(2)}, u32[]{:S(2)}) collective-permute-start(bf16[128,1024]{1,0:T(8,128)(2,1)S(1)} %fusion.8), channel_id=1, source_target_pairs={{0,2},{1,3},{2,0},{3,1},{4,6},{5,7},{6,4},{7,5},{8,10},{9,11},{10,... | collective-permute-start | bytes 786440 | tf_op jit(solution)/shard_map/ppermute | solution.py:19
  93.3 11.2 %collective-permute-start.24 = (bf16[128,1024]{1,0:T(8,128)(2,1)S(1)}, bf16[128,1024]{1,0:T(8,128)(2,1)S(1)}, u32[]{:S(2)}, u32[]{:S(2)}) collective-permute-start(bf16[128,1024]{1,0:T(8,128)(2,1)S(1)} %convolution_convert_fusion.2), channel_id=1, source_target_pairs={{0,1},{1,0},{2,3},{3,2},{4,5},{5,4},{6,7},{7,6},{8,9},{9,8},{10,11... | collective-permute-start | bytes 786440 | tf_op jit(solution)/shard_map/ppermute | solution.py:19
  96.3 8.8 %collective-permute-start.25 = (bf16[128,1024]{1,0:T(8,128)(2,1)S(1)}, bf16[128,1024]{1,0:T(8,128)(2,1)S(1)}, u32[]{:S(2)}, u32[]{:S(2)}) collective-permute-start(bf16[128,1024]{1,0:T(8,128)(2,1)S(1)} %convolution_convert_fusion.1), channel_id=1, source_target_pairs={{0,2},{1,3},{2,0},{3,1},{4,6},{5,7},{6,4},{7,5},{8,10},{9,11},{10,... | collective-permute-start | bytes 786440 | tf_op jit(solution)/shard_map/ppermute | solution.py:19
  (2 other events, 4.0 us)

commit v6 on v5

--- a/solution.py
+++ b/solution.py
@@ -68,7 +68,12 @@
         else:
             held = jnp.concatenate([send(piece[:, half:] if s[0] else piece[:, :half], back(s)) for s in sides], axis=0)
 
-        feats = {s: lax.dynamic_slice_in_dim(tokens, place(s) * slab, slab, axis=1) for s in shifts}
+        def features(x, s):
+            return lax.dynamic_slice_in_dim(x, place(s) * slab, slab, axis=1)
+
+        feats = {s: features(tokens, s) for s in shifts if not (s[0] and s[1])}
+        again, _ = lax.optimization_barrier((tokens, [feats[s] for s in feats if s != (0, 0)]))
+        feats |= {s: features(again, s) for s in shifts if s[0] and s[1]}
         got = {s: send(feats[s], s) for s in away}
         got[0, 0] = feats[0, 0]
 

time: 107 us -> 108 us (level)
  waiting for transfers between devices: 48.1 us -> 49.9 us
    ppermute x15, waiting for transfers between devices: 22.8 us -> 36.5 us  [send(): return lax.ppermute(x, ('row', 'col'), pairs)]
    ppermute x9, waiting for transfers between devices: 20.4 us -> 13.3 us  [send_dp(): return lax.ppermute(x, 'dp', pairs)]
    ppermute x2, waiting for transfers between devices: 4.93 us -> 0.01 us  [send_turned(): return lax.ppermute(x, ('dp', 'row', 'col'), pairs)]
    dynamic_slice x1 -> x2, local copies, waits for them, and re-layouts: 2.59 us -> 3.1 us  [features(): return lax.dynamic_slice_in_dim(x, place(s) * slab, slab, axis=1)]
  transfers between devices with their start and end apart: 26 -> 26, of which waited for: 13 -> 12; matrix products, arithmetic and copies ran while one was open for 22% -> 22% of each run, Pallas kernels for 0% -> 0%
where the time goes in v6:
time: 108 us
  waiting for transfers between devices  49.9 us (46%)
  starting transfers between devices  31.2 us (29%)
  matrix products  16.9 us (16%)
  local copies, waits for them, and re-layouts  9.18 us (8%)
    ppermute x15, waiting for transfers between devices, send(): return lax.ppermute(x, ('row', 'col'), pairs)  36.5 us
    dot_general x15, matrix products, matmul(): return jnp.dot(a, b, preferred_element_type=jnp.float32)  16.9 us
    ppermute x15, starting transfers between devices, send(): return lax.ppermute(x, ('row', 'col'), pairs)  15.7 us
    ppermute x9, waiting for transfers between devices, send_dp(): return lax.ppermute(x, 'dp', pairs)  13.3 us
    ppermute x9, starting transfers between devices, send_dp(): return lax.ppermute(x, 'dp', pairs)  11 us
    ppermute x2, starting transfers between devices, send_turned(): return lax.ppermute(x, ('dp', 'row', 'col'), pairs)  4.49 us
    dynamic_slice x2, local copies, waits for them, and re-layouts, features(): return lax.dynamic_slice_in_dim(x, place(s) * slab, slab, axis=1)  3.1 us
    dynamic_slice x1, local copies, waits for them, and re-layouts, shards(): block = lax.dynamic_slice_in_dim(piece, kind * half, half, axis=1)  2.16 us
  transfers between devices with their start and end apart: 26, of which 12 were waited for; matrix products, arithmetic and copies ran while one was open for 22% of the time, Pallas kernels for 0%

profile of v6, /device:TPU:0, one launch (start us, length us, event | category | flops | bytes accessed | tf_op | source)
XLA Modules:
  0.0 108.0 jit_solution(11003257691924064375)
XLA Ops:
  0.0 2.2 %fusion.21 = (bf16[128,1024]{1,0:T(8,128)(2,1)S(1)}, bf16[128,1024]{1,0:T(8,128)(2,1)}) fusion(bf16[1024,2048]{1,0:T(8,128)(2,1)} %param.7, s32[]{:T(128)S(6)} %select_n.188, s32[]{:T(128)S(6)} %select_n.194, s32[]{:T(128)S(6)} %select_n.191), kind=kLoop, calls=%fused_computation.56 | loop fusion | bytes 1048588 | tf_op jit(solution)/shard_map/dynamic_slice | solution.py:63
  2.2 3.0 %collective-permute-start.9 = (bf16[128,1024]{1,0:T(8,128)(2,1)}, bf16[128,1024]{1,0:T(8,128)(2,1)}, u32[]{:S(2)}, u32[]{:S(2)}) collective-permute-start(bf16[128,1024]{1,0:T(8,128)(2,1)} %get-tuple-element.16), channel_id=1, source_target_pairs={{0,1},{1,0},{2,3},{3,2},{4,6},{5,7},{6,4},{7,5},{8,9},{9,8},{10,11... | collective-permute-start | bytes 786440 | tf_op jit(solution)/shard_map/ppermute | solution.py:31
  5.2 1.5 %collective-permute-start.10 = (bf16[128,1024]{1,0:T(8,128)(2,1)S(1)}, bf16[128,1024]{1,0:T(8,128)(2,1)}, u32[]{:S(2)}, u32[]{:S(2)}) collective-permute-start(bf16[128,1024]{1,0:T(8,128)(2,1)S(1)} %get-tuple-element.15), channel_id=1, source_target_pairs={{0,2},{1,3},{2,0},{3,1},{4,5},{5,4},{6,7},{7,6},{8,10},{9,11},{10,... | collective-permute-start | bytes 786440 | tf_op jit(solution)/shard_map/ppermute | solution.py:31
  6.7 2.3 %constant_dynamic-slice_fusion.1 = (bf16[128,2048]{1,0:T(8,128)(2,1)}, bf16[128,2048]{1,0:T(8,128)(2,1)}) fusion(bf16[128,8192]{1,0:T(8,128)(2,1)} %param.4, s32[]{:T(128)S(6)} %select_n.185, s32[]{:T(128)S(6)} %select_n.183), kind=kLoop, calls=%fused_computation.53 | loop fusion | bytes 2097160 | tf_op jit(solution)/shard_map/dynamic_slice | solution.py:72
  10.3 3.0 %collective-permute-start.3 = (bf16[128,2048]{1,0:T(8,128)(2,1)}, bf16[128,2048]{1,0:T(8,128)(2,1)}, u32[]{:S(2)}, u32[]{:S(2)}) collective-permute-start(bf16[128,2048]{1,0:T(8,128)(2,1)} %constant_dynamic-slice_fusion), channel_id=1, source_target_pairs={{0,3},{1,2},{2,1},{3,0},{4,7},{5,6},{6,5},{7,4},{8,11},{9,10},{10,... | collective-permute-start | bytes 1572872 | tf_op jit(solution)/shard_map/ppermute | solution.py:19
  13.3 3.9 %fusion.15 = f32[128,1024]{1,0:T(8,128)} fusion(bf16[2048,1024]{1,0:T(8,128)(2,1)} %param.6, bf16[128,8192]{1,0:T(8,128)(2,1)S(1)} %copy-done.4, s32[]{:T(128)S(6)} %select_n.181), kind=kOutput, calls=%fused_computation.25 | convolution fusion | flops 536870912 | bytes 5242884 | tf_op jit(solution)/shard_map/dot_general | solution.py:44
  17.1 1.5 %fusion.17 = f32[128,1024]{1,0:T(8,128)} fusion(bf16[2048,1024]{1,0:T(8,128)(2,1)S(1)} %copy-done, bf16[128,8192]{1,0:T(8,128)(2,1)S(1)} %copy-done.4, s32[]{:T(128)S(6)} %select_n.181), kind=kOutput, calls=%fused_computation.27 | convolution fusion | flops 536870912 | bytes 5242884 | tf_op jit(solution)/shard_map/dot_general | solution.py:44
  18.8 1.0 constant_dynamic-update-slice_fusion.5
  19.7 1.0 constant_dynamic-update-slice_fusion.4
  20.7 1.6 %collective-permute-start.12 = (bf16[256,1024]{1,0:T(8,128)(2,1)S(1)}, bf16[256,1024]{1,0:T(8,128)(2,1)S(1)}, u32[]{:S(2)}, u32[]{:S(2)}) collective-permute-start(bf16[256,1024]{1,0:T(8,128)(2,1)S(1)} %constant_dynamic-update-slice_fusion.4), channel_id=1, source_target_pairs={{8,24},{12,28},{16,0},{20,4},{9,25},{13,29},{17,1},{21,5},{10,26},... | collective-permute-start | bytes 1572872 | tf_op jit(solution)/shard_map/ppermute | solution.py:35
  22.3 5.5 %collective-permute-start.13 = (bf16[256,1024]{1,0:T(8,128)(2,1)S(1)}, bf16[256,1024]{1,0:T(8,128)(2,1)S(1)}, u32[]{:S(2)}, u32[]{:S(2)}) collective-permute-start(bf16[256,1024]{1,0:T(8,128)(2,1)S(1)} %constant_dynamic-update-slice_fusion.4), channel_id=1, source_target_pairs={{0,16},{4,20},{24,8},{28,12},{1,17},{5,21},{25,9},{29,13},{2,18},{... | collective-permute-start | bytes 1572872 | tf_op jit(solution)/shard_map/ppermute | solution.py:35
  27.8 7.6 %collective-permute-done.3 = bf16[128,2048]{1,0:T(8,128)(2,1)} collective-permute-done((bf16[128,2048]{1,0:T(8,128)(2,1)}, bf16[128,2048]{1,0:T(8,128)(2,1)}, u32[]{:S(2)}, u32[]{:S(2)}) %collective-permute-start.3) | collective-permute-done | bytes 524320 | tf_op jit(solution)/shard_map/ppermute | solution.py:19
  35.4 1.6 %collective-permute-start.11 = (bf16[256,1024]{1,0:T(8,128)(2,1)S(1)}, bf16[256,1024]{1,0:T(8,128)(2,1)S(1)}, u32[]{:S(2)}, u32[]{:S(2)}) collective-permute-start(bf16[256,1024]{1,0:T(8,128)(2,1)S(1)} %constant_dynamic-update-slice_fusion.4), channel_id=1, source_target_pairs={{0,8},{4,12},{8,0},{12,4},{16,24},{20,28},{24,16},{28,20},{1,9},{5... | collective-permute-start | bytes 1572872 | tf_op jit(solution)/shard_map/ppermute | solution.py:35
  37.1 3.1 %convolution_convert_fusion.7 = bf16[128,1024]{1,0:T(8,128)(2,1)S(1)} fusion(bf16[128,2048]{1,0:T(8,128)(2,1)} %collective-permute-done.3, bf16[2048,1024]{1,0:T(8,128)(2,1)} %param.5), kind=kOutput, calls=%fused_computation.20 | convolution fusion | flops 537001984 | bytes 4980736 | tf_op jit(solution)/shard_map/dot_general | solution.py:44
  40.2 1.9 %convolution_convert_fusion.5 = bf16[128,1024]{1,0:T(8,128)(2,1)S(1)} fusion(bf16[128,2048]{1,0:T(8,128)(2,1)} %collective-permute-done.3, bf16[2048,1024]{1,0:T(8,128)(2,1)S(1)} %copy-done.2), kind=kOutput, calls=%fused_computation.18 | convolution fusion | flops 537001984 | bytes 4980736 | tf_op jit(solution)/shard_map/dot_general | solution.py:44
  45.0 5.2 %collective-permute-done.4 = bf16[128,1024]{1,0:T(8,128)(2,1)S(1)} collective-permute-done((bf16[128,1024]{1,0:T(8,128)(2,1)S(1)}, bf16[128,1024]{1,0:T(8,128)(2,1)S(1)}, u32[]{:S(2)}, u32[]{:S(2)}) %collective-permute-start.4) | collective-permute-done | bytes 262176 | tf_op jit(solution)/shard_map/ppermute | solution.py:19
  50.2 1.5 %collective-permute-start.7 = (bf16[128,1024]{1,0:T(8,128)(2,1)S(1)}, bf16[128,1024]{1,0:T(8,128)(2,1)S(1)}, u32[]{:S(2)}, u32[]{:S(2)}) collective-permute-start(bf16[128,1024]{1,0:T(8,128)(2,1)S(1)} %convolution_convert_fusion.5), channel_id=1, source_target_pairs={{0,2},{1,3},{2,0},{3,1},{4,6},{5,7},{6,4},{7,5},{8,10},{9,11},{10,... | collective-permute-start | bytes 786440 | tf_op jit(solution)/shard_map/ppermute | solution.py:19
  52.9 1.2 %collective-permute-start.6 = (bf16[128,1024]{1,0:T(8,128)(2,1)S(1)}, bf16[128,1024]{1,0:T(8,128)(2,1)S(1)}, u32[]{:S(2)}, u32[]{:S(2)}) collective-permute-start(bf16[128,1024]{1,0:T(8,128)(2,1)S(1)} %convolution_convert_fusion.6), channel_id=1, source_target_pairs={{0,2},{1,3},{2,0},{3,1},{4,6},{5,7},{6,4},{7,5},{8,10},{9,11},{10,... | collective-permute-start | bytes 786440 | tf_op jit(solution)/shard_map/ppermute | solution.py:19
  54.2 5.2 %collective-permute-done.7 = bf16[128,1024]{1,0:T(8,128)(2,1)S(1)} collective-permute-done((bf16[128,1024]{1,0:T(8,128)(2,1)S(1)}, bf16[128,1024]{1,0:T(8,128)(2,1)S(1)}, u32[]{:S(2)}, u32[]{:S(2)}) %collective-permute-start.7) | collective-permute-done | bytes 262176 | tf_op jit(solution)/shard_map/ppermute | solution.py:19
  59.4 1.5 %collective-permute-start.5 = (bf16[128,1024]{1,0:T(8,128)(2,1)S(1)}, bf16[128,1024]{1,0:T(8,128)(2,1)S(1)}, u32[]{:S(2)}, u32[]{:S(2)}) collective-permute-start(bf16[128,1024]{1,0:T(8,128)(2,1)S(1)} %fusion.13), channel_id=1, source_target_pairs={{0,2},{1,3},{2,0},{3,1},{4,6},{5,7},{6,4},{7,5},{8,10},{9,11},{10,... | collective-permute-start | bytes 786440 | tf_op jit(solution)/shard_map/ppermute | solution.py:19
  62.9 1.4 %collective-permute-done.6 = bf16[128,1024]{1,0:T(8,128)(2,1)S(1)} collective-permute-done((bf16[128,1024]{1,0:T(8,128)(2,1)S(1)}, bf16[128,1024]{1,0:T(8,128)(2,1)S(1)}, u32[]{:S(2)}, u32[]{:S(2)}) %collective-permute-start.6) | collective-permute-done | bytes 262176 | tf_op jit(solution)/shard_map/ppermute | solution.py:19
  64.4 2.8 %collective-permute-done.5 = bf16[128,1024]{1,0:T(8,128)(2,1)S(1)} collective-permute-done((bf16[128,1024]{1,0:T(8,128)(2,1)S(1)}, bf16[128,1024]{1,0:T(8,128)(2,1)S(1)}, u32[]{:S(2)}, u32[]{:S(2)}) %collective-permute-start.5) | collective-permute-done | bytes 262176 | tf_op jit(solution)/shard_map/ppermute | solution.py:19
  68.1 1.5 %collective-permute-start.17 = (bf16[256,1024]{1,0:T(8,128)(2,1)S(1)}, bf16[256,1024]{1,0:T(8,128)(2,1)S(1)}, u32[]{:S(2)}, u32[]{:S(2)}) collective-permute-start(bf16[256,1024]{1,0:T(8,128)(2,1)S(1)} %collective-permute-done.13), channel_id=1, source_target_pairs={{16,24},{20,28},{8,0},{12,4},{17,25},{21,29},{9,1},{13,5},{18,26},... | collective-permute-start | bytes 1572872 | tf_op jit(solution)/shard_map/ppermute | solution.py:35
  71.6 13.3 %collective-permute-done.17 = bf16[256,1024]{1,0:T(8,128)(2,1)S(1)} collective-permute-done((bf16[256,1024]{1,0:T(8,128)(2,1)S(1)}, bf16[256,1024]{1,0:T(8,128)(2,1)S(1)}, u32[]{:S(2)}, u32[]{:S(2)}) %collective-permute-start.17) | collective-permute-done | bytes 524320 | tf_op jit(solution)/shard_map/ppermute | solution.py:35
  84.9 1.5 %collective-permute-start.22 = (bf16[128,1024]{1,0:T(8,128)(2,1)S(1)}, bf16[128,1024]{1,0:T(8,128)(2,1)S(1)}, u32[]{:S(2)}, u32[]{:S(2)}) collective-permute-start(bf16[128,1024]{1,0:T(8,128)(2,1)S(1)} %multiply_convert_fusion), channel_id=1, source_target_pairs={{0,2},{1,3},{2,0},{3,1},{4,6},{5,7},{6,4},{7,5},{8,10},{9,11},{10,... | collective-permute-start | bytes 786440 | tf_op jit(solution)/shard_map/ppermute | solution.py:19
  87.0 5.5 %collective-permute-done.22 = bf16[128,1024]{1,0:T(8,128)(2,1)S(1)} collective-permute-done((bf16[128,1024]{1,0:T(8,128)(2,1)S(1)}, bf16[128,1024]{1,0:T(8,128)(2,1)S(1)}, u32[]{:S(2)}, u32[]{:S(2)}) %collective-permute-start.22) | collective-permute-done | bytes 262176 | tf_op jit(solution)/shard_map/ppermute | solution.py:19
  92.5 1.8 %collective-permute-start.21 = (bf16[128,1024]{1,0:T(8,128)(2,1)S(1)}, bf16[128,1024]{1,0:T(8,128)(2,1)S(1)}, u32[]{:S(2)}, u32[]{:S(2)}) collective-permute-start(bf16[128,1024]{1,0:T(8,128)(2,1)S(1)} %fusion.5), channel_id=1, source_target_pairs={{0,1},{1,0},{2,3},{3,2},{4,5},{5,4},{6,7},{7,6},{8,9},{9,8},{10,11... | collective-permute-start | bytes 786440 | tf_op jit(solution)/shard_map/ppermute | solution.py:19
  95.9 1.8 %collective-permute-start.24 = (bf16[128,1024]{1,0:T(8,128)(2,1)S(1)}, bf16[128,1024]{1,0:T(8,128)(2,1)S(1)}, u32[]{:S(2)}, u32[]{:S(2)}) collective-permute-start(bf16[128,1024]{1,0:T(8,128)(2,1)S(1)} %convolution_convert_fusion.2), channel_id=1, source_target_pairs={{0,1},{1,0},{2,3},{3,2},{4,5},{5,4},{6,7},{7,6},{8,9},{9,8},{10,11... | collective-permute-start | bytes 786440 | tf_op jit(solution)/shard_map/ppermute | solution.py:19
  99.4 2.3 %collective-permute-done.21 = bf16[128,1024]{1,0:T(8,128)(2,1)S(1)} collective-permute-done((bf16[128,1024]{1,0:T(8,128)(2,1)S(1)}, bf16[128,1024]{1,0:T(8,128)(2,1)S(1)}, u32[]{:S(2)}, u32[]{:S(2)}) %collective-permute-start.21) | collective-permute-done | bytes 262176 | tf_op jit(solution)/shard_map/ppermute | solution.py:19
  101.8 2.3 %collective-permute-done.23 = bf16[128,1024]{1,0:T(8,128)(2,1)S(1)} collective-permute-done((bf16[128,1024]{1,0:T(8,128)(2,1)S(1)}, bf16[128,1024]{1,0:T(8,128)(2,1)S(1)}, u32[]{:S(2)}, u32[]{:S(2)}) %collective-permute-start.23) | collective-permute-done | bytes 262176 | tf_op jit(solution)/shard_map/ppermute | solution.py:19
  104.0 1.2 %collective-permute-done.24 = bf16[128,1024]{1,0:T(8,128)(2,1)S(1)} collective-permute-done((bf16[128,1024]{1,0:T(8,128)(2,1)S(1)}, bf16[128,1024]{1,0:T(8,128)(2,1)S(1)}, u32[]{:S(2)}, u32[]{:S(2)}) %collective-permute-start.24) | collective-permute-done | bytes 262176 | tf_op jit(solution)/shard_map/ppermute | solution.py:19
  105.3 2.0 %collective-permute-done.25 = bf16[128,1024]{1,0:T(8,128)(2,1)S(1)} collective-permute-done((bf16[128,1024]{1,0:T(8,128)(2,1)S(1)}, bf16[128,1024]{1,0:T(8,128)(2,1)S(1)}, u32[]{:S(2)}, u32[]{:S(2)}) %collective-permute-start.25) | collective-permute-done | bytes 262176 | tf_op jit(solution)/shard_map/ppermute | solution.py:19
  (76 shorter events, 14.9 us)
Async XLA Ops:
  0.0 9.5 %copy-start.4 = (bf16[128,8192]{1,0:T(8,128)(2,1)S(1)}, bf16[128,8192]{1,0:T(8,128)(2,1)}, u32[]{:S(2)}) copy-start(bf16[128,8192]{1,0:T(8,128)(2,1)} %param.4) | copy-start | bytes 6291460
  2.2 16.5 %collective-permute-start.9 = (bf16[128,1024]{1,0:T(8,128)(2,1)}, bf16[128,1024]{1,0:T(8,128)(2,1)}, u32[]{:S(2)}, u32[]{:S(2)}) collective-permute-start(bf16[128,1024]{1,0:T(8,128)(2,1)} %get-tuple-element.16), channel_id=1, source_target_pairs={{0,1},{1,0},{2,3},{3,2},{4,6},{5,7},{6,4},{7,5},{8,9},{9,8},{10,11... | collective-permute-start | bytes 786440 | tf_op jit(solution)/shard_map/ppermute | solution.py:31
  5.2 14.6 %collective-permute-start.10 = (bf16[128,1024]{1,0:T(8,128)(2,1)S(1)}, bf16[128,1024]{1,0:T(8,128)(2,1)}, u32[]{:S(2)}, u32[]{:S(2)}) collective-permute-start(bf16[128,1024]{1,0:T(8,128)(2,1)S(1)} %get-tuple-element.15), channel_id=1, source_target_pairs={{0,2},{1,3},{2,0},{3,1},{4,5},{5,4},{6,7},{7,6},{8,10},{9,11},{10,... | collective-permute-start | bytes 786440 | tf_op jit(solution)/shard_map/ppermute | solution.py:31
  8.9 34.7 %collective-permute-start.2 = (bf16[128,2048]{1,0:T(8,128)(2,1)}, bf16[128,2048]{1,0:T(8,128)(2,1)S(1)}, u32[]{:S(2)}, u32[]{:S(2)}) collective-permute-start(bf16[128,2048]{1,0:T(8,128)(2,1)} %get-tuple-element.17), channel_id=1, source_target_pairs={{0,2},{1,3},{2,0},{3,1},{4,6},{5,7},{6,4},{7,5},{8,10},{9,11},{10,... | collective-permute-start | bytes 1572872 | tf_op jit(solution)/shard_map/ppermute | solution.py:19
  9.5 32.7 %collective-permute-start = (bf16[128,2048]{1,0:T(8,128)(2,1)}, bf16[128,2048]{1,0:T(8,128)(2,1)S(1)}, u32[]{:S(2)}, u32[]{:S(2)}) collective-permute-start(bf16[128,2048]{1,0:T(8,128)(2,1)} %get-tuple-element.18), channel_id=1, source_target_pairs={{0,1},{1,0},{2,3},{3,2},{4,5},{5,4},{6,7},{7,6},{8,9},{9,8},{10,11... | collective-permute-start | bytes 1572872 | tf_op jit(solution)/shard_map/ppermute | solution.py:19
  10.3 25.1 %collective-permute-start.3 = (bf16[128,2048]{1,0:T(8,128)(2,1)}, bf16[128,2048]{1,0:T(8,128)(2,1)}, u32[]{:S(2)}, u32[]{:S(2)}) collective-permute-start(bf16[128,2048]{1,0:T(8,128)(2,1)} %constant_dynamic-slice_fusion), channel_id=1, source_target_pairs={{0,3},{1,2},{2,1},{3,0},{4,7},{5,6},{6,5},{7,4},{8,11},{9,10},{10,... | collective-permute-start | bytes 1572872 | tf_op jit(solution)/shard_map/ppermute | solution.py:19
  13.3 3.9 %copy-start = (bf16[2048,1024]{1,0:T(8,128)(2,1)S(1)}, bf16[2048,1024]{1,0:T(8,128)(2,1)}, u32[]{:S(2)}) copy-start(bf16[2048,1024]{1,0:T(8,128)(2,1)} %param.5) | copy-start | bytes 12582916
  20.7 19.4 %copy-start.2 = (bf16[2048,1024]{1,0:T(8,128)(2,1)S(1)}, bf16[2048,1024]{1,0:T(8,128)(2,1)}, u32[]{:S(2)}) copy-start(bf16[2048,1024]{1,0:T(8,128)(2,1)} %param.6) | copy-start | bytes 12582916
  20.7 31.7 %collective-permute-start.12 = (bf16[256,1024]{1,0:T(8,128)(2,1)S(1)}, bf16[256,1024]{1,0:T(8,128)(2,1)S(1)}, u32[]{:S(2)}, u32[]{:S(2)}) collective-permute-start(bf16[256,1024]{1,0:T(8,128)(2,1)S(1)} %constant_dynamic-update-slice_fusion.4), channel_id=1, source_target_pairs={{8,24},{12,28},{16,0},{20,4},{9,25},{13,29},{17,1},{21,5},{10,26},... | collective-permute-start | bytes 1572872 | tf_op jit(solution)/shard_map/ppermute | solution.py:35
  22.3 30.6 %collective-permute-start.13 = (bf16[256,1024]{1,0:T(8,128)(2,1)S(1)}, bf16[256,1024]{1,0:T(8,128)(2,1)S(1)}, u32[]{:S(2)}, u32[]{:S(2)}) collective-permute-start(bf16[256,1024]{1,0:T(8,128)(2,1)S(1)} %constant_dynamic-update-slice_fusion.4), channel_id=1, source_target_pairs={{0,16},{4,20},{24,8},{28,12},{1,17},{5,21},{25,9},{29,13},{2,18},{... | collective-permute-start | bytes 1572872 | tf_op jit(solution)/shard_map/ppermute | solution.py:35
  35.4 26.2 %collective-permute-start.11 = (bf16[256,1024]{1,0:T(8,128)(2,1)S(1)}, bf16[256,1024]{1,0:T(8,128)(2,1)S(1)}, u32[]{:S(2)}, u32[]{:S(2)}) collective-permute-start(bf16[256,1024]{1,0:T(8,128)(2,1)S(1)} %constant_dynamic-update-slice_fusion.4), channel_id=1, source_target_pairs={{0,8},{4,12},{8,0},{12,4},{16,24},{20,28},{24,16},{28,20},{1,9},{5... | collective-permute-start | bytes 1572872 | tf_op jit(solution)/shard_map/ppermute | solution.py:35
  42.1 28.7 %collective-permute-start.18 = (bf16[256,1024]{1,0:T(8,128)(2,1)S(1)}, bf16[256,1024]{1,0:T(8,128)(2,1)S(1)}, u32[]{:S(2)}, u32[]{:S(2)}) collective-permute-start(bf16[256,1024]{1,0:T(8,128)(2,1)S(1)} %constant_dynamic-update-slice_fusion.4), channel_id=1, source_target_pairs={{8,16},{12,20},{16,8},{20,12},{9,17},{13,21},{17,9},{21,13},{10,18... | collective-permute-start | bytes 1572872 | tf_op jit(solution)/shard_map/ppermute | solution.py:35
  43.6 6.6 %collective-permute-start.4 = (bf16[128,1024]{1,0:T(8,128)(2,1)S(1)}, bf16[128,1024]{1,0:T(8,128)(2,1)S(1)}, u32[]{:S(2)}, u32[]{:S(2)}) collective-permute-start(bf16[128,1024]{1,0:T(8,128)(2,1)S(1)} %convolution_convert_fusion.7), channel_id=1, source_target_pairs={{0,1},{1,0},{2,3},{3,2},{4,5},{5,4},{6,7},{7,6},{8,9},{9,8},{10,11... | collective-permute-start | bytes 786440 | tf_op jit(solution)/shard_map/ppermute | solution.py:19
  50.2 9.2 %collective-permute-start.7 = (bf16[128,1024]{1,0:T(8,128)(2,1)S(1)}, bf16[128,1024]{1,0:T(8,128)(2,1)S(1)}, u32[]{:S(2)}, u32[]{:S(2)}) collective-permute-start(bf16[128,1024]{1,0:T(8,128)(2,1)S(1)} %convolution_convert_fusion.5), channel_id=1, source_target_pairs={{0,2},{1,3},{2,0},{3,1},{4,6},{5,7},{6,4},{7,5},{8,10},{9,11},{10,... | collective-permute-start | bytes 786440 | tf_op jit(solution)/shard_map/ppermute | solution.py:19
  52.5 10.4 %collective-permute-start.1 = (bf16[128,1024]{1,0:T(8,128)(2,1)S(1)}, bf16[128,1024]{1,0:T(8,128)(2,1)S(1)}, u32[]{:S(2)}, u32[]{:S(2)}) collective-permute-start(bf16[128,1024]{1,0:T(8,128)(2,1)S(1)} %convolution_convert_fusion.8), channel_id=1, source_target_pairs={{0,1},{1,0},{2,3},{3,2},{4,5},{5,4},{6,7},{7,6},{8,9},{9,8},{10,11... | collective-permute-start | bytes 786440 | tf_op jit(solution)/shard_map/ppermute | solution.py:19
  52.9 11.4 %collective-permute-start.6 = (bf16[128,1024]{1,0:T(8,128)(2,1)S(1)}, bf16[128,1024]{1,0:T(8,128)(2,1)S(1)}, u32[]{:S(2)}, u32[]{:S(2)}) collective-permute-start(bf16[128,1024]{1,0:T(8,128)(2,1)S(1)} %convolution_convert_fusion.6), channel_id=1, source_target_pairs={{0,2},{1,3},{2,0},{3,1},{4,6},{5,7},{6,4},{7,5},{8,10},{9,11},{10,... | collective-permute-start | bytes 786440 | tf_op jit(solution)/shard_map/ppermute | solution.py:19
  59.4 7.8 %collective-permute-start.5 = (bf16[128,1024]{1,0:T(8,128)(2,1)S(1)}, bf16[128,1024]{1,0:T(8,128)(2,1)S(1)}, u32[]{:S(2)}, u32[]{:S(2)}) collective-permute-start(bf16[128,1024]{1,0:T(8,128)(2,1)S(1)} %fusion.13), channel_id=1, source_target_pairs={{0,2},{1,3},{2,0},{3,1},{4,6},{5,7},{6,4},{7,5},{8,10},{9,11},{10,... | collective-permute-start | bytes 786440 | tf_op jit(solution)/shard_map/ppermute | solution.py:19
  61.7 6.4 %collective-permute-start.8 = (bf16[128,1024]{1,0:T(8,128)(2,1)S(1)}, bf16[128,1024]{1,0:T(8,128)(2,1)S(1)}, u32[]{:S(2)}, u32[]{:S(2)}) collective-permute-start(bf16[128,1024]{1,0:T(8,128)(2,1)S(1)} %fusion.14), channel_id=1, source_target_pairs={{0,1},{1,0},{2,3},{3,2},{4,5},{5,4},{6,7},{7,6},{8,9},{9,8},{10,11... | collective-permute-start | bytes 786440 | tf_op jit(solution)/shard_map/ppermute | solution.py:19
  62.4 7.2 %copy-start.6 = (f32[128,1024]{1,0:T(8,128)S(1)}, f32[128,1024]{1,0:T(8,128)}, u32[]{:S(2)}) copy-start(f32[128,1024]{1,0:T(8,128)} %fusion.15) | copy-start | bytes 1572868
  62.4 7.2 %copy-start.7 = (f32[128,1024]{1,0:T(8,128)S(1)}, f32[128,1024]{1,0:T(8,128)}, u32[]{:S(2)}) copy-start(f32[128,1024]{1,0:T(8,128)} %fusion.17) | copy-start | bytes 1572868
  62.8 7.3 %copy-start.3 = (bf16[1024,2048]{1,0:T(8,128)(2,1)S(1)}, bf16[1024,2048]{1,0:T(8,128)(2,1)}, u32[]{:S(2)}) copy-start(bf16[1024,2048]{1,0:T(8,128)(2,1)} %param.7) | copy-start | bytes 12582916
  62.8 32.0 %collective-permute-start.14 = (bf16[256,1024]{1,0:T(8,128)(2,1)S(1)}, bf16[256,1024]{1,0:T(8,128)(2,1)S(1)}, u32[]{:S(2)}, u32[]{:S(2)}) collective-permute-start(bf16[256,1024]{1,0:T(8,128)(2,1)S(1)} %constant_dynamic-update-slice_fusion.4), channel_id=1, source_target_pairs={{0,4},{4,0},{8,12},{12,8},{16,20},{20,16},{24,28},{28,24},{1,5},{5... | collective-permute-start | bytes 1572872 | tf_op jit(solution)/shard_map/ppermute | solution.py:35
  64.4 30.8 %collective-permute-start.15 = (bf16[256,1024]{1,0:T(8,128)(2,1)S(1)}, bf16[256,1024]{1,0:T(8,128)(2,1)S(1)}, u32[]{:S(2)}, u32[]{:S(2)}) collective-permute-start(bf16[256,1024]{1,0:T(8,128)(2,1)S(1)} %collective-permute-done.11), channel_id=1, source_target_pairs={{0,4},{4,0},{8,12},{12,8},{16,20},{20,16},{24,28},{28,24},{1,5},{5... | collective-permute-start | bytes 1572872 | tf_op jit(solution)/shard_map/ppermute | solution.py:35
  67.2 28.1 %collective-permute-start.16 = (bf16[256,1024]{1,0:T(8,128)(2,1)S(1)}, bf16[256,1024]{1,0:T(8,128)(2,1)S(1)}, u32[]{:S(2)}, u32[]{:S(2)}) collective-permute-start(bf16[256,1024]{1,0:T(8,128)(2,1)S(1)} %broadcast_select_fusion.1), channel_id=1, source_target_pairs={{0,4},{4,0},{8,12},{12,8},{16,20},{20,16},{24,28},{28,24},{1,5},{5... | collective-permute-start | bytes 1572872 | tf_op jit(solution)/shard_map/ppermute | solution.py:35
  68.1 16.8 %collective-permute-start.17 = (bf16[256,1024]{1,0:T(8,128)(2,1)S(1)}, bf16[256,1024]{1,0:T(8,128)(2,1)S(1)}, u32[]{:S(2)}, u32[]{:S(2)}) collective-permute-start(bf16[256,1024]{1,0:T(8,128)(2,1)S(1)} %collective-permute-done.13), channel_id=1, source_target_pairs={{16,24},{20,28},{8,0},{12,4},{17,25},{21,29},{9,1},{13,5},{18,26},... | collective-permute-start | bytes 1572872 | tf_op jit(solution)/shard_map/ppermute | solution.py:35
  70.8 15.6 %collective-permute-start.20 = (bf16[128,1024]{1,0:T(8,128)(2,1)S(1)}, bf16[128,1024]{1,0:T(8,128)(2,1)S(1)}, u32[]{:S(2)}, u32[]{:S(2)}) collective-permute-start(bf16[128,1024]{1,0:T(8,128)(2,1)S(1)} %multiply_convert_fusion), channel_id=1, source_target_pairs={{0,1},{1,0},{2,3},{3,2},{4,5},{5,4},{6,7},{7,6},{8,9},{9,8},{10,11... | collective-permute-start | bytes 786440 | tf_op jit(solution)/shard_map/ppermute | solution.py:19
  84.9 7.6 %collective-permute-start.22 = (bf16[128,1024]{1,0:T(8,128)(2,1)S(1)}, bf16[128,1024]{1,0:T(8,128)(2,1)S(1)}, u32[]{:S(2)}, u32[]{:S(2)}) collective-permute-start(bf16[128,1024]{1,0:T(8,128)(2,1)S(1)} %multiply_convert_fusion), channel_id=1, source_target_pairs={{0,2},{1,3},{2,0},{3,1},{4,6},{5,7},{6,4},{7,5},{8,10},{9,11},{10,... | collective-permute-start | bytes 786440 | tf_op jit(solution)/shard_map/ppermute | solution.py:19
  86.5 8.9 %collective-permute-start.19 = (bf16[256,1024]{1,0:T(8,128)(2,1)S(1)}, bf16[256,1024]{1,0:T(8,128)(2,1)S(1)}, u32[]{:S(2)}, u32[]{:S(2)}) collective-permute-start(bf16[256,1024]{1,0:T(8,128)(2,1)S(1)} %broadcast_select_fusion), channel_id=1, source_target_pairs={{0,4},{4,0},{8,12},{12,8},{16,20},{20,16},{24,28},{28,24},{1,5},{5... | collective-permute-start | bytes 1572872 | tf_op jit(solution)/shard_map/ppermute | solution.py:35
  92.5 9.2 %collective-permute-start.21 = (bf16[128,1024]{1,0:T(8,128)(2,1)S(1)}, bf16[128,1024]{1,0:T(8,128)(2,1)S(1)}, u32[]{:S(2)}, u32[]{:S(2)}) collective-permute-start(bf16[128,1024]{1,0:T(8,128)(2,1)S(1)} %fusion.5), channel_id=1, source_target_pairs={{0,1},{1,0},{2,3},{3,2},{4,5},{5,4},{6,7},{7,6},{8,9},{9,8},{10,11... | collective-permute-start | bytes 786440 | tf_op jit(solution)/shard_map/ppermute | solution.py:19
  94.8 9.2 %collective-permute-start.23 = (bf16[128,1024]{1,0:T(8,128)(2,1)S(1)}, bf16[128,1024]{1,0:T(8,128)(2,1)S(1)}, u32[]{:S(2)}, u32[]{:S(2)}) collective-permute-start(bf16[128,1024]{1,0:T(8,128)(2,1)S(1)} %fusion.8), channel_id=1, source_target_pairs={{0,2},{1,3},{2,0},{3,1},{4,6},{5,7},{6,4},{7,5},{8,10},{9,11},{10,... | collective-permute-start | bytes 786440 | tf_op jit(solution)/shard_map/ppermute | solution.py:19
  95.9 9.3 %collective-permute-start.24 = (bf16[128,1024]{1,0:T(8,128)(2,1)S(1)}, bf16[128,1024]{1,0:T(8,128)(2,1)S(1)}, u32[]{:S(2)}, u32[]{:S(2)}) collective-permute-start(bf16[128,1024]{1,0:T(8,128)(2,1)S(1)} %convolution_convert_fusion.2), channel_id=1, source_target_pairs={{0,1},{1,0},{2,3},{3,2},{4,5},{5,4},{6,7},{7,6},{8,9},{9,8},{10,11... | collective-permute-start | bytes 786440 | tf_op jit(solution)/shard_map/ppermute | solution.py:19
  98.6 8.7 %collective-permute-start.25 = (bf16[128,1024]{1,0:T(8,128)(2,1)S(1)}, bf16[128,1024]{1,0:T(8,128)(2,1)S(1)}, u32[]{:S(2)}, u32[]{:S(2)}) collective-permute-start(bf16[128,1024]{1,0:T(8,128)(2,1)S(1)} %convolution_convert_fusion.1), channel_id=1, source_target_pairs={{0,2},{1,3},{2,0},{3,1},{4,6},{5,7},{6,4},{7,5},{8,10},{9,11},{10,... | collective-permute-start | bytes 786440 | tf_op jit(solution)/shard_map/ppermute | solution.py:19
  (2 other events, 4.6 us)

commit v7 on v2

--- a/solution.py
+++ b/solution.py
@@ -59,8 +59,9 @@
             relayed = send_dp(two_a, [(2, 3), (1, 0)], 0)
             outer = (chip == 0) | (chip == chips - 1)
             two = jnp.where(outer, two_b, two_a)
-            early += [(one, chip ^ 1), (two, chip ^ 2)]
+            early += [(held, chip), (one, chip ^ 1), (two, chip ^ 2)]
         else:
+            early.append((held, chip))
             for z in range(1, chips):
                 turn = send_dp(held, [(i, (i + z) % chips) for i in range(chips)], 0)
                 late.append((turn, (chip - z) % chips))
@@ -71,7 +72,9 @@
             def shift(a, b):
                 return (b, a) if col_first else (a, b)
 
-            parts = {s: matmul(got[s], weight) for s in away}
+            parts = {}
+            for s in away:
+                parts[s] = matmul(got[s], weight)
             parts[0, 0] = matmul(got[0, 0], weight)
             sums = {b: parts[shift(0, b)] for b in range(second)}
             for b in reversed(range(second)):
@@ -101,7 +104,6 @@
                     for i, s in enumerate(sides):
                         far[s] = lax.dynamic_update_slice_in_dim(far[s], moved[i * share : (i + 1) * share], at, axis=0)
 
-        fill([(held, chip)])
         tied, _ = lax.optimization_barrier(([p for p, _ in early], gate_passed + up_passed))
         fill([(p, at) for p, (_, at) in zip(tied, early)])
 

time: 106 us -> 118 us (1.11)
  waiting for transfers between devices: 49.7 us -> 61.6 us
  matrix products: 15.4 us -> 16.8 us
    ppermute x17, waiting for transfers between devices: 26.4 us -> 45.9 us  [send(): return lax.ppermute(x, ('row', 'col'), pairs)]
    ppermute x9, waiting for transfers between devices: 23.2 us -> 15.6 us  [send_dp(): return lax.ppermute(x, 'dp', pairs)]
    dot_general x15, matrix products: 15.4 us -> 16.8 us  [matmul(): return jnp.dot(a, b, preferred_element_type=jnp.float32)]
    ppermute x9, starting transfers between devices: 9.7 us -> 11 us  [send_dp(): return lax.ppermute(x, 'dp', pairs)]
  transfers between devices with their start and end apart: 26 -> 26, of which waited for: 11 -> 12; matrix products, arithmetic and copies ran while one was open for 21% -> 19% of each run, Pallas kernels for 0% -> 0%
where the time goes in v7:
time: 118 us
  waiting for transfers between devices  61.6 us (52%)
  starting transfers between devices  30.6 us (26%)
  matrix products  16.8 us (14%)
  local copies, waits for them, and re-layouts  8.34 us (7%)
    ppermute x17, waiting for transfers between devices, send(): return lax.ppermute(x, ('row', 'col'), pairs)  45.9 us
    ppermute x17, starting transfers between devices, send(): return lax.ppermute(x, ('row', 'col'), pairs)  19.6 us
    dot_general x15, matrix products, matmul(): return jnp.dot(a, b, preferred_element_type=jnp.float32)  16.8 us
    ppermute x9, waiting for transfers between devices, send_dp(): return lax.ppermute(x, 'dp', pairs)  15.6 us
    ppermute x9, starting transfers between devices, send_dp(): return lax.ppermute(x, 'dp', pairs)  11 us
    dynamic_slice x1, local copies, waits for them, and re-layouts, shards(): lax.dynamic_slice_in_dim(tokens, place(s) * slab, slab, axis=1)  2.74 us
  transfers between devices with their start and end apart: 26, of which 12 were waited for; matrix products, arithmetic and copies ran while one was open for 19% of the time, Pallas kernels for 0%

profile of v7, /device:TPU:0, one launch (start us, length us, event | category | flops | bytes accessed | tf_op | source)
XLA Modules:
  0.0 118.2 jit_solution(14645565681707080099)
XLA Ops:
  0.0 2.7 %constant_dynamic-slice_fusion.2 = (bf16[128,2048]{1,0:T(8,128)(2,1)}, bf16[128,2048]{1,0:T(8,128)(2,1)}, bf16[128,2048]{1,0:T(8,128)(2,1)}) fusion(bf16[128,8192]{1,0:T(8,128)(2,1)} %param.4, s32[]{:T(128)S(6)} %select_n.167, s32[]{:T(128)S(6)} %select_n.165, s32[]{:T(128)S(6)} %select_n.168), kind=kLoop, calls=%fused_computation.52 | loop fusion | bytes 3145740 | tf_op jit(solution)/shard_map/dynamic_slice | solution.py:49
  2.7 3.9 %collective-permute-start.3 = (bf16[128,2048]{1,0:T(8,128)(2,1)}, bf16[128,2048]{1,0:T(8,128)(2,1)}, u32[]{:S(2)}, u32[]{:S(2)}) collective-permute-start(bf16[128,2048]{1,0:T(8,128)(2,1)} %get-tuple-element.17), channel_id=1, source_target_pairs={{0,3},{1,2},{2,1},{3,0},{4,7},{5,6},{6,5},{7,4},{8,11},{9,10},{10,... | collective-permute-start | bytes 1572872 | tf_op jit(solution)/shard_map/ppermute | solution.py:19
  7.2 1.8 %fusion.21 = (bf16[128,1024]{1,0:T(8,128)(2,1)S(1)}, bf16[128,1024]{1,0:T(8,128)(2,1)}) fusion(bf16[1024,2048]{1,0:T(8,128)(2,1)} %param.7, s32[]{:T(128)S(6)} %select_n.169, s32[]{:T(128)S(6)} %add.272), kind=kLoop, calls=%fused_computation.57 | loop fusion | bytes 1048584 | tf_op jit(solution)/shard_map/slice | solution.py:47
  9.0 2.0 %collective-permute-start.10 = (bf16[128,1024]{1,0:T(8,128)(2,1)S(1)}, bf16[128,1024]{1,0:T(8,128)(2,1)}, u32[]{:S(2)}, u32[]{:S(2)}) collective-permute-start(bf16[128,1024]{1,0:T(8,128)(2,1)S(1)} %get-tuple-element.13), channel_id=1, source_target_pairs={{0,2},{1,3},{2,0},{3,1},{4,6},{5,7},{6,4},{7,5},{8,10},{9,11},{10,... | collective-permute-start | bytes 786440 | tf_op jit(solution)/shard_map/ppermute | solution.py:19
  11.0 1.5 %collective-permute-start = (bf16[128,2048]{1,0:T(8,128)(2,1)}, bf16[128,2048]{1,0:T(8,128)(2,1)S(1)}, u32[]{:S(2)}, u32[]{:S(2)}) collective-permute-start(bf16[128,2048]{1,0:T(8,128)(2,1)} %get-tuple-element.16), channel_id=1, source_target_pairs={{0,1},{1,0},{2,3},{3,2},{4,5},{5,4},{6,7},{7,6},{8,9},{9,8},{10,11... | collective-permute-start | bytes 1572872 | tf_op jit(solution)/shard_map/ppermute | solution.py:19
  12.5 3.9 %fusion.15 = f32[128,1024]{1,0:T(8,128)} fusion(bf16[2048,1024]{1,0:T(8,128)(2,1)} %param.6, bf16[128,8192]{1,0:T(8,128)(2,1)S(1)} %copy-done.4, s32[]{:T(128)S(6)} %select_n.163), kind=kOutput, calls=%fused_computation.25 | convolution fusion | flops 536870912 | bytes 5242884 | tf_op jit(solution)/shard_map/dot_general | solution.py:32
  16.3 1.6 %fusion.17 = f32[128,1024]{1,0:T(8,128)} fusion(bf16[2048,1024]{1,0:T(8,128)(2,1)S(1)} %copy-done, bf16[128,8192]{1,0:T(8,128)(2,1)S(1)} %copy-done.4, s32[]{:T(128)S(6)} %select_n.163), kind=kOutput, calls=%fused_computation.27 | convolution fusion | flops 536870912 | bytes 5242884 | tf_op jit(solution)/shard_map/dot_general | solution.py:32
  17.9 6.7 %collective-permute-done.9 = bf16[128,1024]{1,0:T(8,128)(2,1)} collective-permute-done((bf16[128,1024]{1,0:T(8,128)(2,1)}, bf16[128,1024]{1,0:T(8,128)(2,1)}, u32[]{:S(2)}, u32[]{:S(2)}) %collective-permute-start.9) | collective-permute-done | bytes 262176 | tf_op jit(solution)/shard_map/ppermute | solution.py:19
  24.6 1.0 constant_dynamic-update-slice_fusion.5
  25.6 10.5 %collective-permute-done.10 = bf16[128,1024]{1,0:T(8,128)(2,1)} collective-permute-done((bf16[128,1024]{1,0:T(8,128)(2,1)S(1)}, bf16[128,1024]{1,0:T(8,128)(2,1)}, u32[]{:S(2)}, u32[]{:S(2)}) %collective-permute-start.10) | collective-permute-done | bytes 262176 | tf_op jit(solution)/shard_map/ppermute | solution.py:19
  36.0 1.0 constant_dynamic-update-slice_fusion.4
  37.0 4.8 %collective-permute-start.13 = (bf16[256,1024]{1,0:T(8,128)(2,1)S(1)}, bf16[256,1024]{1,0:T(8,128)(2,1)S(1)}, u32[]{:S(2)}, u32[]{:S(2)}) collective-permute-start(bf16[256,1024]{1,0:T(8,128)(2,1)S(1)} %constant_dynamic-update-slice_fusion.4), channel_id=1, source_target_pairs={{0,16},{4,20},{24,8},{28,12},{1,17},{5,21},{25,9},{29,13},{2,18},{... | collective-permute-start | bytes 1572872 | tf_op jit(solution)/shard_map/ppermute | solution.py:23
  41.8 1.3 %collective-permute-start.12 = (bf16[256,1024]{1,0:T(8,128)(2,1)S(1)}, bf16[256,1024]{1,0:T(8,128)(2,1)S(1)}, u32[]{:S(2)}, u32[]{:S(2)}) collective-permute-start(bf16[256,1024]{1,0:T(8,128)(2,1)S(1)} %constant_dynamic-update-slice_fusion.4), channel_id=1, source_target_pairs={{8,24},{12,28},{16,0},{20,4},{9,25},{13,29},{17,1},{21,5},{10,26},... | collective-permute-start | bytes 1572872 | tf_op jit(solution)/shard_map/ppermute | solution.py:23
  43.1 2.6 %collective-permute-start.11 = (bf16[256,1024]{1,0:T(8,128)(2,1)S(1)}, bf16[256,1024]{1,0:T(8,128)(2,1)S(1)}, u32[]{:S(2)}, u32[]{:S(2)}) collective-permute-start(bf16[256,1024]{1,0:T(8,128)(2,1)S(1)} %constant_dynamic-update-slice_fusion.4), channel_id=1, source_target_pairs={{0,8},{4,12},{8,0},{12,4},{16,24},{20,28},{24,16},{28,20},{1,9},{5... | collective-permute-start | bytes 1572872 | tf_op jit(solution)/shard_map/ppermute | solution.py:23
  45.8 3.1 %convolution_convert_fusion.7 = bf16[128,1024]{1,0:T(8,128)(2,1)S(1)} fusion(bf16[128,2048]{1,0:T(8,128)(2,1)} %collective-permute-done.3, bf16[2048,1024]{1,0:T(8,128)(2,1)} %param.5), kind=kOutput, calls=%fused_computation.20 | convolution fusion | flops 537001984 | bytes 4980736 | tf_op jit(solution)/shard_map/dot_general | solution.py:32
  48.9 1.9 %convolution_convert_fusion.5 = bf16[128,1024]{1,0:T(8,128)(2,1)S(1)} fusion(bf16[128,2048]{1,0:T(8,128)(2,1)} %collective-permute-done.3, bf16[2048,1024]{1,0:T(8,128)(2,1)S(1)} %copy-done.2), kind=kOutput, calls=%fused_computation.18 | convolution fusion | flops 537001984 | bytes 4980736 | tf_op jit(solution)/shard_map/dot_general | solution.py:32
  53.6 5.1 %collective-permute-done.4 = bf16[128,1024]{1,0:T(8,128)(2,1)S(1)} collective-permute-done((bf16[128,1024]{1,0:T(8,128)(2,1)S(1)}, bf16[128,1024]{1,0:T(8,128)(2,1)S(1)}, u32[]{:S(2)}, u32[]{:S(2)}) %collective-permute-start.4) | collective-permute-done | bytes 262176 | tf_op jit(solution)/shard_map/ppermute | solution.py:19
  58.7 1.5 %collective-permute-start.7 = (bf16[128,1024]{1,0:T(8,128)(2,1)S(1)}, bf16[128,1024]{1,0:T(8,128)(2,1)S(1)}, u32[]{:S(2)}, u32[]{:S(2)}) collective-permute-start(bf16[128,1024]{1,0:T(8,128)(2,1)S(1)} %convolution_convert_fusion.5), channel_id=1, source_target_pairs={{0,2},{1,3},{2,0},{3,1},{4,6},{5,7},{6,4},{7,5},{8,10},{9,11},{10,... | collective-permute-start | bytes 786440 | tf_op jit(solution)/shard_map/ppermute | solution.py:19
  61.6 3.7 %collective-permute-done.12 = bf16[256,1024]{1,0:T(8,128)(2,1)S(1)} collective-permute-done((bf16[256,1024]{1,0:T(8,128)(2,1)S(1)}, bf16[256,1024]{1,0:T(8,128)(2,1)S(1)}, u32[]{:S(2)}, u32[]{:S(2)}) %collective-permute-start.12) | collective-permute-done | bytes 524320 | tf_op jit(solution)/shard_map/ppermute | solution.py:23
  65.3 1.5 %collective-permute-start.6 = (bf16[128,1024]{1,0:T(8,128)(2,1)S(1)}, bf16[128,1024]{1,0:T(8,128)(2,1)S(1)}, u32[]{:S(2)}, u32[]{:S(2)}) collective-permute-start(bf16[128,1024]{1,0:T(8,128)(2,1)S(1)} %convolution_convert_fusion.6), channel_id=1, source_target_pairs={{0,2},{1,3},{2,0},{3,1},{4,6},{5,7},{6,4},{7,5},{8,10},{9,11},{10,... | collective-permute-start | bytes 786440 | tf_op jit(solution)/shard_map/ppermute | solution.py:19
  69.6 4.9 %collective-permute-done.6 = bf16[128,1024]{1,0:T(8,128)(2,1)S(1)} collective-permute-done((bf16[128,1024]{1,0:T(8,128)(2,1)S(1)}, bf16[128,1024]{1,0:T(8,128)(2,1)S(1)}, u32[]{:S(2)}, u32[]{:S(2)}) %collective-permute-start.6) | collective-permute-done | bytes 262176 | tf_op jit(solution)/shard_map/ppermute | solution.py:19
  74.5 4.6 %collective-permute-done.5 = bf16[128,1024]{1,0:T(8,128)(2,1)S(1)} collective-permute-done((bf16[128,1024]{1,0:T(8,128)(2,1)S(1)}, bf16[128,1024]{1,0:T(8,128)(2,1)S(1)}, u32[]{:S(2)}, u32[]{:S(2)}) %collective-permute-start.5) | collective-permute-done | bytes 262176 | tf_op jit(solution)/shard_map/ppermute | solution.py:19
  79.0 1.5 %collective-permute-start.17 = (bf16[256,1024]{1,0:T(8,128)(2,1)S(1)}, bf16[256,1024]{1,0:T(8,128)(2,1)S(1)}, u32[]{:S(2)}, u32[]{:S(2)}) collective-permute-start(bf16[256,1024]{1,0:T(8,128)(2,1)S(1)} %collective-permute-done.13), channel_id=1, source_target_pairs={{16,24},{20,28},{8,0},{12,4},{17,25},{21,29},{9,1},{13,5},{18,26},... | collective-permute-start | bytes 1572872 | tf_op jit(solution)/shard_map/ppermute | solution.py:23
  81.8 1.6 %collective-permute-start.20 = (bf16[128,1024]{1,0:T(8,128)(2,1)S(1)}, bf16[128,1024]{1,0:T(8,128)(2,1)S(1)}, u32[]{:S(2)}, u32[]{:S(2)}) collective-permute-start(bf16[128,1024]{1,0:T(8,128)(2,1)S(1)} %multiply_convert_fusion), channel_id=1, source_target_pairs={{0,2},{1,3},{2,0},{3,1},{4,6},{5,7},{6,4},{7,5},{8,10},{9,11},{10,... | collective-permute-start | bytes 786440 | tf_op jit(solution)/shard_map/ppermute | solution.py:19
  83.3 11.9 %collective-permute-done.17 = bf16[256,1024]{1,0:T(8,128)(2,1)S(1)} collective-permute-done((bf16[256,1024]{1,0:T(8,128)(2,1)S(1)}, bf16[256,1024]{1,0:T(8,128)(2,1)S(1)}, u32[]{:S(2)}, u32[]{:S(2)}) %collective-permute-start.17) | collective-permute-done | bytes 524320 | tf_op jit(solution)/shard_map/ppermute | solution.py:23
  96.4 6.7 %collective-permute-done.22 = bf16[128,1024]{1,0:T(8,128)(2,1)S(1)} collective-permute-done((bf16[128,1024]{1,0:T(8,128)(2,1)S(1)}, bf16[128,1024]{1,0:T(8,128)(2,1)S(1)}, u32[]{:S(2)}, u32[]{:S(2)}) %collective-permute-start.22) | collective-permute-done | bytes 262176 | tf_op jit(solution)/shard_map/ppermute | solution.py:19
  103.1 1.5 %collective-permute-start.21 = (bf16[128,1024]{1,0:T(8,128)(2,1)S(1)}, bf16[128,1024]{1,0:T(8,128)(2,1)S(1)}, u32[]{:S(2)}, u32[]{:S(2)}) collective-permute-start(bf16[128,1024]{1,0:T(8,128)(2,1)S(1)} %fusion.5), channel_id=1, source_target_pairs={{0,2},{1,3},{2,0},{3,1},{4,6},{5,7},{6,4},{7,5},{8,10},{9,11},{10,... | collective-permute-start | bytes 786440 | tf_op jit(solution)/shard_map/ppermute | solution.py:19
  107.9 1.6 %collective-permute-start.25 = (bf16[128,1024]{1,0:T(8,128)(2,1)S(1)}, bf16[128,1024]{1,0:T(8,128)(2,1)S(1)}, u32[]{:S(2)}, u32[]{:S(2)}) collective-permute-start(bf16[128,1024]{1,0:T(8,128)(2,1)S(1)} %convolution_convert_fusion.1), channel_id=1, source_target_pairs={{0,1},{1,0},{2,3},{3,2},{4,5},{5,4},{6,7},{7,6},{8,9},{9,8},{10,11... | collective-permute-start | bytes 786440 | tf_op jit(solution)/shard_map/ppermute | solution.py:19
  110.0 2.3 %collective-permute-done.21 = bf16[128,1024]{1,0:T(8,128)(2,1)S(1)} collective-permute-done((bf16[128,1024]{1,0:T(8,128)(2,1)S(1)}, bf16[128,1024]{1,0:T(8,128)(2,1)S(1)}, u32[]{:S(2)}, u32[]{:S(2)}) %collective-permute-start.21) | collective-permute-done | bytes 262176 | tf_op jit(solution)/shard_map/ppermute | solution.py:19
  112.3 2.0 %collective-permute-done.23 = bf16[128,1024]{1,0:T(8,128)(2,1)S(1)} collective-permute-done((bf16[128,1024]{1,0:T(8,128)(2,1)S(1)}, bf16[128,1024]{1,0:T(8,128)(2,1)S(1)}, u32[]{:S(2)}, u32[]{:S(2)}) %collective-permute-start.23) | collective-permute-done | bytes 262176 | tf_op jit(solution)/shard_map/ppermute | solution.py:19
  114.3 1.4 %collective-permute-done.24 = bf16[128,1024]{1,0:T(8,128)(2,1)S(1)} collective-permute-done((bf16[128,1024]{1,0:T(8,128)(2,1)S(1)}, bf16[128,1024]{1,0:T(8,128)(2,1)S(1)}, u32[]{:S(2)}, u32[]{:S(2)}) %collective-permute-start.24) | collective-permute-done | bytes 262176 | tf_op jit(solution)/shard_map/ppermute | solution.py:19
  115.8 1.7 %collective-permute-done.25 = bf16[128,1024]{1,0:T(8,128)(2,1)S(1)} collective-permute-done((bf16[128,1024]{1,0:T(8,128)(2,1)S(1)}, bf16[128,1024]{1,0:T(8,128)(2,1)S(1)}, u32[]{:S(2)}, u32[]{:S(2)}) %collective-permute-start.25) | collective-permute-done | bytes 262176 | tf_op jit(solution)/shard_map/ppermute | solution.py:19
  (74 shorter events, 14.2 us)
Async XLA Ops:
  0.0 12.5 %copy-start.4 = (bf16[128,8192]{1,0:T(8,128)(2,1)S(1)}, bf16[128,8192]{1,0:T(8,128)(2,1)}, u32[]{:S(2)}) copy-start(bf16[128,8192]{1,0:T(8,128)(2,1)} %param.4) | copy-start | bytes 6291460
  2.7 40.4 %collective-permute-start.3 = (bf16[128,2048]{1,0:T(8,128)(2,1)}, bf16[128,2048]{1,0:T(8,128)(2,1)}, u32[]{:S(2)}, u32[]{:S(2)}) collective-permute-start(bf16[128,2048]{1,0:T(8,128)(2,1)} %get-tuple-element.17), channel_id=1, source_target_pairs={{0,3},{1,2},{2,1},{3,0},{4,7},{5,6},{6,5},{7,4},{8,11},{9,10},{10,... | collective-permute-start | bytes 1572872 | tf_op jit(solution)/shard_map/ppermute | solution.py:19
  6.7 45.6 %collective-permute-start.2 = (bf16[128,2048]{1,0:T(8,128)(2,1)}, bf16[128,2048]{1,0:T(8,128)(2,1)S(1)}, u32[]{:S(2)}, u32[]{:S(2)}) collective-permute-start(bf16[128,2048]{1,0:T(8,128)(2,1)} %get-tuple-element.15), channel_id=1, source_target_pairs={{0,2},{1,3},{2,0},{3,1},{4,6},{5,7},{6,4},{7,5},{8,10},{9,11},{10,... | collective-permute-start | bytes 1572872 | tf_op jit(solution)/shard_map/ppermute | solution.py:19
  9.0 15.7 %collective-permute-start.9 = (bf16[128,1024]{1,0:T(8,128)(2,1)}, bf16[128,1024]{1,0:T(8,128)(2,1)}, u32[]{:S(2)}, u32[]{:S(2)}) collective-permute-start(bf16[128,1024]{1,0:T(8,128)(2,1)} %get-tuple-element.14), channel_id=1, source_target_pairs={{0,1},{1,0},{2,3},{3,2},{4,5},{5,4},{6,7},{7,6},{8,9},{9,8},{10,11... | collective-permute-start | bytes 786440 | tf_op jit(solution)/shard_map/ppermute | solution.py:19
  9.0 27.1 %collective-permute-start.10 = (bf16[128,1024]{1,0:T(8,128)(2,1)S(1)}, bf16[128,1024]{1,0:T(8,128)(2,1)}, u32[]{:S(2)}, u32[]{:S(2)}) collective-permute-start(bf16[128,1024]{1,0:T(8,128)(2,1)S(1)} %get-tuple-element.13), channel_id=1, source_target_pairs={{0,2},{1,3},{2,0},{3,1},{4,6},{5,7},{6,4},{7,5},{8,10},{9,11},{10,... | collective-permute-start | bytes 786440 | tf_op jit(solution)/shard_map/ppermute | solution.py:19
  11.0 39.9 %collective-permute-start = (bf16[128,2048]{1,0:T(8,128)(2,1)}, bf16[128,2048]{1,0:T(8,128)(2,1)S(1)}, u32[]{:S(2)}, u32[]{:S(2)}) collective-permute-start(bf16[128,2048]{1,0:T(8,128)(2,1)} %get-tuple-element.16), channel_id=1, source_target_pairs={{0,1},{1,0},{2,3},{3,2},{4,5},{5,4},{6,7},{7,6},{8,9},{9,8},{10,11... | collective-permute-start | bytes 1572872 | tf_op jit(solution)/shard_map/ppermute | solution.py:19
  12.5 3.9 %copy-start = (bf16[2048,1024]{1,0:T(8,128)(2,1)S(1)}, bf16[2048,1024]{1,0:T(8,128)(2,1)}, u32[]{:S(2)}) copy-start(bf16[2048,1024]{1,0:T(8,128)(2,1)} %param.5) | copy-start | bytes 12582916
  37.0 11.8 %copy-start.2 = (bf16[2048,1024]{1,0:T(8,128)(2,1)S(1)}, bf16[2048,1024]{1,0:T(8,128)(2,1)}, u32[]{:S(2)}) copy-start(bf16[2048,1024]{1,0:T(8,128)(2,1)} %param.6) | copy-start | bytes 12582916
  37.0 24.0 %collective-permute-start.13 = (bf16[256,1024]{1,0:T(8,128)(2,1)S(1)}, bf16[256,1024]{1,0:T(8,128)(2,1)S(1)}, u32[]{:S(2)}, u32[]{:S(2)}) collective-permute-start(bf16[256,1024]{1,0:T(8,128)(2,1)S(1)} %constant_dynamic-update-slice_fusion.4), channel_id=1, source_target_pairs={{0,16},{4,20},{24,8},{28,12},{1,17},{5,21},{25,9},{29,13},{2,18},{... | collective-permute-start | bytes 1572872 | tf_op jit(solution)/shard_map/ppermute | solution.py:23
  41.8 23.5 %collective-permute-start.12 = (bf16[256,1024]{1,0:T(8,128)(2,1)S(1)}, bf16[256,1024]{1,0:T(8,128)(2,1)S(1)}, u32[]{:S(2)}, u32[]{:S(2)}) collective-permute-start(bf16[256,1024]{1,0:T(8,128)(2,1)S(1)} %constant_dynamic-update-slice_fusion.4), channel_id=1, source_target_pairs={{8,24},{12,28},{16,0},{20,4},{9,25},{13,29},{17,1},{21,5},{10,26},... | collective-permute-start | bytes 1572872 | tf_op jit(solution)/shard_map/ppermute | solution.py:23
  43.1 25.1 %collective-permute-start.11 = (bf16[256,1024]{1,0:T(8,128)(2,1)S(1)}, bf16[256,1024]{1,0:T(8,128)(2,1)S(1)}, u32[]{:S(2)}, u32[]{:S(2)}) collective-permute-start(bf16[256,1024]{1,0:T(8,128)(2,1)S(1)} %constant_dynamic-update-slice_fusion.4), channel_id=1, source_target_pairs={{0,8},{4,12},{8,0},{12,4},{16,24},{20,28},{24,16},{28,20},{1,9},{5... | collective-permute-start | bytes 1572872 | tf_op jit(solution)/shard_map/ppermute | solution.py:23
  50.8 31.0 %collective-permute-start.18 = (bf16[256,1024]{1,0:T(8,128)(2,1)S(1)}, bf16[256,1024]{1,0:T(8,128)(2,1)S(1)}, u32[]{:S(2)}, u32[]{:S(2)}) collective-permute-start(bf16[256,1024]{1,0:T(8,128)(2,1)S(1)} %constant_dynamic-update-slice_fusion.4), channel_id=1, source_target_pairs={{8,16},{12,20},{16,8},{20,12},{9,17},{13,21},{17,9},{21,13},{10,18... | collective-permute-start | bytes 1572872 | tf_op jit(solution)/shard_map/ppermute | solution.py:23
  52.3 6.4 %collective-permute-start.4 = (bf16[128,1024]{1,0:T(8,128)(2,1)S(1)}, bf16[128,1024]{1,0:T(8,128)(2,1)S(1)}, u32[]{:S(2)}, u32[]{:S(2)}) collective-permute-start(bf16[128,1024]{1,0:T(8,128)(2,1)S(1)} %convolution_convert_fusion.7), channel_id=1, source_target_pairs={{0,1},{1,0},{2,3},{3,2},{4,5},{5,4},{6,7},{7,6},{8,9},{9,8},{10,11... | collective-permute-start | bytes 786440 | tf_op jit(solution)/shard_map/ppermute | solution.py:19
  58.7 8.1 %collective-permute-start.7 = (bf16[128,1024]{1,0:T(8,128)(2,1)S(1)}, bf16[128,1024]{1,0:T(8,128)(2,1)S(1)}, u32[]{:S(2)}, u32[]{:S(2)}) collective-permute-start(bf16[128,1024]{1,0:T(8,128)(2,1)S(1)} %convolution_convert_fusion.5), channel_id=1, source_target_pairs={{0,2},{1,3},{2,0},{3,1},{4,6},{5,7},{6,4},{7,5},{8,10},{9,11},{10,... | collective-permute-start | bytes 786440 | tf_op jit(solution)/shard_map/ppermute | solution.py:19
  61.0 8.5 %collective-permute-start.1 = (bf16[128,1024]{1,0:T(8,128)(2,1)S(1)}, bf16[128,1024]{1,0:T(8,128)(2,1)S(1)}, u32[]{:S(2)}, u32[]{:S(2)}) collective-permute-start(bf16[128,1024]{1,0:T(8,128)(2,1)S(1)} %convolution_convert_fusion.8), channel_id=1, source_target_pairs={{0,1},{1,0},{2,3},{3,2},{4,5},{5,4},{6,7},{7,6},{8,9},{9,8},{10,11... | collective-permute-start | bytes 786440 | tf_op jit(solution)/shard_map/ppermute | solution.py:19
  65.3 9.2 %collective-permute-start.6 = (bf16[128,1024]{1,0:T(8,128)(2,1)S(1)}, bf16[128,1024]{1,0:T(8,128)(2,1)S(1)}, u32[]{:S(2)}, u32[]{:S(2)}) collective-permute-start(bf16[128,1024]{1,0:T(8,128)(2,1)S(1)} %convolution_convert_fusion.6), channel_id=1, source_target_pairs={{0,2},{1,3},{2,0},{3,1},{4,6},{5,7},{6,4},{7,5},{8,10},{9,11},{10,... | collective-permute-start | bytes 786440 | tf_op jit(solution)/shard_map/ppermute | solution.py:19
  66.8 12.2 %collective-permute-start.5 = (bf16[128,1024]{1,0:T(8,128)(2,1)S(1)}, bf16[128,1024]{1,0:T(8,128)(2,1)S(1)}, u32[]{:S(2)}, u32[]{:S(2)}) collective-permute-start(bf16[128,1024]{1,0:T(8,128)(2,1)S(1)} %fusion.13), channel_id=1, source_target_pairs={{0,2},{1,3},{2,0},{3,1},{4,6},{5,7},{6,4},{7,5},{8,10},{9,11},{10,... | collective-permute-start | bytes 786440 | tf_op jit(solution)/shard_map/ppermute | solution.py:19
  68.2 10.8 %collective-permute-start.8 = (bf16[128,1024]{1,0:T(8,128)(2,1)S(1)}, bf16[128,1024]{1,0:T(8,128)(2,1)S(1)}, u32[]{:S(2)}, u32[]{:S(2)}) collective-permute-start(bf16[128,1024]{1,0:T(8,128)(2,1)S(1)} %fusion.14), channel_id=1, source_target_pairs={{0,1},{1,0},{2,3},{3,2},{4,5},{5,4},{6,7},{7,6},{8,9},{9,8},{10,11... | collective-permute-start | bytes 786440 | tf_op jit(solution)/shard_map/ppermute | solution.py:19
  69.1 11.4 %copy-start.6 = (f32[128,1024]{1,0:T(8,128)S(1)}, f32[128,1024]{1,0:T(8,128)}, u32[]{:S(2)}) copy-start(f32[128,1024]{1,0:T(8,128)} %fusion.15) | copy-start | bytes 1572868
  69.1 11.4 %copy-start.7 = (f32[128,1024]{1,0:T(8,128)S(1)}, f32[128,1024]{1,0:T(8,128)}, u32[]{:S(2)}) copy-start(f32[128,1024]{1,0:T(8,128)} %fusion.17) | copy-start | bytes 1572868
  69.5 11.5 %copy-start.3 = (bf16[1024,2048]{1,0:T(8,128)(2,1)S(1)}, bf16[1024,2048]{1,0:T(8,128)(2,1)}, u32[]{:S(2)}) copy-start(bf16[1024,2048]{1,0:T(8,128)(2,1)} %param.7) | copy-start | bytes 12582916
  69.5 35.6 %collective-permute-start.14 = (bf16[256,1024]{1,0:T(8,128)(2,1)S(1)}, bf16[256,1024]{1,0:T(8,128)(2,1)S(1)}, u32[]{:S(2)}, u32[]{:S(2)}) collective-permute-start(bf16[256,1024]{1,0:T(8,128)(2,1)S(1)} %constant_dynamic-update-slice_fusion.4), channel_id=1, source_target_pairs={{0,4},{4,0},{8,12},{12,8},{16,20},{20,16},{24,28},{28,24},{1,5},{5... | collective-permute-start | bytes 1572872 | tf_op jit(solution)/shard_map/ppermute | solution.py:23
  74.5 31.2 %collective-permute-start.15 = (bf16[256,1024]{1,0:T(8,128)(2,1)S(1)}, bf16[256,1024]{1,0:T(8,128)(2,1)S(1)}, u32[]{:S(2)}, u32[]{:S(2)}) collective-permute-start(bf16[256,1024]{1,0:T(8,128)(2,1)S(1)} %collective-permute-done.11), channel_id=1, source_target_pairs={{0,4},{4,0},{8,12},{12,8},{16,20},{20,16},{24,28},{28,24},{1,5},{5... | collective-permute-start | bytes 1572872 | tf_op jit(solution)/shard_map/ppermute | solution.py:23
  79.0 26.7 %collective-permute-start.16 = (bf16[256,1024]{1,0:T(8,128)(2,1)S(1)}, bf16[256,1024]{1,0:T(8,128)(2,1)S(1)}, u32[]{:S(2)}, u32[]{:S(2)}) collective-permute-start(bf16[256,1024]{1,0:T(8,128)(2,1)S(1)} %broadcast_select_fusion.1), channel_id=1, source_target_pairs={{0,4},{4,0},{8,12},{12,8},{16,20},{20,16},{24,28},{28,24},{1,5},{5... | collective-permute-start | bytes 1572872 | tf_op jit(solution)/shard_map/ppermute | solution.py:23
  79.0 16.2 %collective-permute-start.17 = (bf16[256,1024]{1,0:T(8,128)(2,1)S(1)}, bf16[256,1024]{1,0:T(8,128)(2,1)S(1)}, u32[]{:S(2)}, u32[]{:S(2)}) collective-permute-start(bf16[256,1024]{1,0:T(8,128)(2,1)S(1)} %collective-permute-done.13), channel_id=1, source_target_pairs={{16,24},{20,28},{8,0},{12,4},{17,25},{21,29},{9,1},{13,5},{18,26},... | collective-permute-start | bytes 1572872 | tf_op jit(solution)/shard_map/ppermute | solution.py:23
  81.8 14.0 %collective-permute-start.20 = (bf16[128,1024]{1,0:T(8,128)(2,1)S(1)}, bf16[128,1024]{1,0:T(8,128)(2,1)S(1)}, u32[]{:S(2)}, u32[]{:S(2)}) collective-permute-start(bf16[128,1024]{1,0:T(8,128)(2,1)S(1)} %multiply_convert_fusion), channel_id=1, source_target_pairs={{0,2},{1,3},{2,0},{3,1},{4,6},{5,7},{6,4},{7,5},{8,10},{9,11},{10,... | collective-permute-start | bytes 786440 | tf_op jit(solution)/shard_map/ppermute | solution.py:19
  95.3 7.9 %collective-permute-start.22 = (bf16[128,1024]{1,0:T(8,128)(2,1)S(1)}, bf16[128,1024]{1,0:T(8,128)(2,1)S(1)}, u32[]{:S(2)}, u32[]{:S(2)}) collective-permute-start(bf16[128,1024]{1,0:T(8,128)(2,1)S(1)} %multiply_convert_fusion), channel_id=1, source_target_pairs={{0,1},{1,0},{2,3},{3,2},{4,5},{5,4},{6,7},{7,6},{8,9},{9,8},{10,11... | collective-permute-start | bytes 786440 | tf_op jit(solution)/shard_map/ppermute | solution.py:19
  95.8 10.1 %collective-permute-start.19 = (bf16[256,1024]{1,0:T(8,128)(2,1)S(1)}, bf16[256,1024]{1,0:T(8,128)(2,1)S(1)}, u32[]{:S(2)}, u32[]{:S(2)}) collective-permute-start(bf16[256,1024]{1,0:T(8,128)(2,1)S(1)} %broadcast_select_fusion), channel_id=1, source_target_pairs={{0,4},{4,0},{8,12},{12,8},{16,20},{20,16},{24,28},{28,24},{1,5},{5... | collective-permute-start | bytes 1572872 | tf_op jit(solution)/shard_map/ppermute | solution.py:23
  103.1 9.2 %collective-permute-start.21 = (bf16[128,1024]{1,0:T(8,128)(2,1)S(1)}, bf16[128,1024]{1,0:T(8,128)(2,1)S(1)}, u32[]{:S(2)}, u32[]{:S(2)}) collective-permute-start(bf16[128,1024]{1,0:T(8,128)(2,1)S(1)} %fusion.5), channel_id=1, source_target_pairs={{0,2},{1,3},{2,0},{3,1},{4,6},{5,7},{6,4},{7,5},{8,10},{9,11},{10,... | collective-permute-start | bytes 786440 | tf_op jit(solution)/shard_map/ppermute | solution.py:19
  105.1 9.2 %collective-permute-start.23 = (bf16[128,1024]{1,0:T(8,128)(2,1)S(1)}, bf16[128,1024]{1,0:T(8,128)(2,1)S(1)}, u32[]{:S(2)}, u32[]{:S(2)}) collective-permute-start(bf16[128,1024]{1,0:T(8,128)(2,1)S(1)} %fusion.8), channel_id=1, source_target_pairs={{0,1},{1,0},{2,3},{3,2},{4,5},{5,4},{6,7},{7,6},{8,9},{9,8},{10,11... | collective-permute-start | bytes 786440 | tf_op jit(solution)/shard_map/ppermute | solution.py:19
  106.4 9.3 %collective-permute-start.24 = (bf16[128,1024]{1,0:T(8,128)(2,1)S(1)}, bf16[128,1024]{1,0:T(8,128)(2,1)S(1)}, u32[]{:S(2)}, u32[]{:S(2)}) collective-permute-start(bf16[128,1024]{1,0:T(8,128)(2,1)S(1)} %convolution_convert_fusion.2), channel_id=1, source_target_pairs={{0,2},{1,3},{2,0},{3,1},{4,6},{5,7},{6,4},{7,5},{8,10},{9,11},{10,... | collective-permute-start | bytes 786440 | tf_op jit(solution)/shard_map/ppermute | solution.py:19
  107.9 9.6 %collective-permute-start.25 = (bf16[128,1024]{1,0:T(8,128)(2,1)S(1)}, bf16[128,1024]{1,0:T(8,128)(2,1)S(1)}, u32[]{:S(2)}, u32[]{:S(2)}) collective-permute-start(bf16[128,1024]{1,0:T(8,128)(2,1)S(1)} %convolution_convert_fusion.1), channel_id=1, source_target_pairs={{0,1},{1,0},{2,3},{3,2},{4,5},{5,4},{6,7},{7,6},{8,9},{9,8},{10,11... | collective-permute-start | bytes 786440 | tf_op jit(solution)/shard_map/ppermute | solution.py:19
  (2 other events, 4.4 us)
